TPU v7x, 256 devices: a whole 4x4x8 slice. The times are simulated.
256 devices in a mesh: shuf: 64 (over y, z, core), rep: 4 (over x).
Axes of the slice: x: 4, y: 4, z: 8, core: 2. Of those that a mesh axis runs over, the one named last changes fastest.
Arguments:
- values: bfloat16 [524288, 1024], P('shuf', 'rep')
- subgroup: int32 [4096], P('shuf'), may hold values from 0 to 31
- owners: int32 [4096, 1], P('shuf'), may hold values from 0 to 63; in each aligned block of 64 rows (0 to 63, 64 to 127, ...) at most 2 rows name the same one
- col_gain: float32 [1024], P('rep'), may hold values from 0.5 to 1.5
- col_bias: float32 [1024], P('rep'), may hold values from -3 to 3
- out_weight: bfloat16 [1024, 1024], P('rep'), may hold values from -0.1875 to 0.1875
Outputs:
- projected: bfloat16 [524288, 1024], P(('shuf', 'rep'))
Inputs may be any that keep to these rules, and one draw needn't show every extreme that they name: `owners`: among the tiles of one index of shuf no owner is named more than 2 times, a bound that some block reaches.
All inputs are finite; a program needn't handle non-finite values.
Results may differ from a plain program's by a relative error of at most 0.015.
Values may be sent and summed in bfloat16 or wider, within the bound.
No kernel may reach another device: no remote copies, remote signals or barrier semaphores. Data moves between devices by JAX's collectives and lax.ppermute only.
A program may use at most 64 MiB of HBM per device.

v0:
```python
import math

import jax
import jax.numpy as jnp
from jax import lax
from jax.sharding import PartitionSpec as P

GRP_DEV = 32
PRIOR = 256


def from_everyone(value, axis):
    peers = lax.axis_size(axis)
    return lax.all_to_all(
        jnp.broadcast_to(value[None], (peers, *value.shape)), axis, 0, 0, tiled=True
    )


def over_copies(value, axis):
    everything = from_everyone(value, axis)
    return jnp.sum(everything, axis=0)


def in_one(arrays, axis):
    flat, at, done = (jnp.concatenate([a.reshape(-1) for a in arrays]), 0, [])
    so_far = over_copies(flat, axis)
    for a in arrays:
        done.append(so_far[at : at + a.size].reshape(a.shape))
        at += a.size
    return tuple(done)


def side_by_side(arrays, axis, split_dim, concat_dim, along):
    widths = [math.prod(a.shape[along:]) for a in arrays]
    both = jnp.concatenate(
        [a.reshape(*a.shape[:along], w) for a, w in zip(arrays, widths)], axis=along
    )
    result = lax.all_to_all(both, axis, split_axis=split_dim, concat_axis=concat_dim, tiled=True)
    pieces = jnp.split(result, [sum(widths[:k]) for k in range(1, len(widths))], axis=along)
    return tuple(
        (b.reshape(*result.shape[:along], *a.shape[along:]) for a, b in zip(arrays, pieces))
    )


def in_one_piece(arrays, axis, split_dim, concat_dim, along):
    ends, at = ([], 0)
    for a in arrays[:-1]:
        at += a.shape[along]
        ends.append(at)
    both = jnp.concatenate(arrays, axis=along)
    return tuple(
        jnp.split(
            lax.all_to_all(both, axis, split_axis=split_dim, concat_axis=concat_dim, tiled=True),
            ends,
            axis=along,
        )
    )


def joined_along(pieces, dim):
    lengths = list(pieces.shape[1:])
    lengths[dim] *= pieces.shape[0]
    return jnp.moveaxis(pieces, 0, dim).reshape(lengths)


def gathered_copies(value, axis, dim):
    return joined_along(from_everyone(value, axis), dim)


def moments(group_sum, group_sq, count, mean_all, square_all):
    weight = (count + float(PRIOR))[:, None]
    center = (group_sum + float(PRIOR) * mean_all) / weight
    second = (group_sq + float(PRIOR) * square_all) / weight
    return (center, lax.rsqrt(second - center * center + 1e-05))


def slot_places(target, capacity, peer_count):
    one_hot = (target[:, None] == jnp.arange(peer_count, dtype=jnp.int32)[None, :]).astype(
        jnp.int32
    )
    position = jnp.sum((jnp.cumsum(one_hot, axis=0) - one_hot) * one_hot, axis=1)
    return target * capacity + position


def on_device(values, subgroup, owners, col_gain, col_bias, out_weight):
    local_rows, local_cols = values.shape
    tile_count = subgroup.shape[0]
    tile_rows = local_rows // tile_count
    peer_count = lax.axis_size("shuf")
    shaped = values.reshape(tile_count, tile_rows, local_cols)
    widened = shaped.astype(jnp.float32)
    tile_sum = jnp.sum(widened, axis=1)
    tile_sq = jnp.sum(widened * widened, axis=1)
    col_sum, col_square = in_one((jnp.sum(tile_sum, axis=0), jnp.sum(tile_sq, axis=0)), "shuf")
    row_count = float(local_rows * peer_count)
    mean_all = col_sum / row_count
    square_all = col_square / row_count
    target = owners[:, 0]
    capacity = max(2, 2 * tile_count // peer_count)
    slot_index = slot_places(target, capacity, peer_count)
    packed = jnp.concatenate([tile_sum, tile_sq], axis=1)
    outgoing = (
        jnp.zeros((peer_count * capacity, 2 * local_cols), jnp.float32).at[slot_index].set(packed)
    )
    labels = (
        jnp.full((peer_count * capacity,), -1.0, jnp.float32)
        .at[slot_index]
        .set(subgroup.astype(jnp.float32))
    )
    arrived, arrived_labels = tuple(
        (
            part.astype(jnp.float32)
            for part in side_by_side(
                (outgoing.astype(jnp.bfloat16), labels.astype(jnp.bfloat16)), "shuf", 0, 0, 1
            )
        )
    )
    group_ids = arrived_labels.astype(jnp.int32)
    members = (group_ids[:, None] == jnp.arange(GRP_DEV, dtype=jnp.int32)[None, :]).astype(
        jnp.float32
    )
    group_sum = jnp.dot(members.T, arrived[:, :local_cols])
    group_sq = jnp.dot(members.T, arrived[:, local_cols:])
    count = float(tile_rows) * jnp.sum(members, axis=0)
    center, inverse = moments(group_sum, group_sq, count, mean_all, square_all)
    slot_center = jnp.dot(members, center)
    slot_inverse = jnp.dot(members, inverse)
    back_center, back_inverse = tuple(
        (
            part.astype(jnp.float32)
            for part in in_one_piece(
                (slot_center.astype(jnp.bfloat16), slot_inverse.astype(jnp.bfloat16)),
                "shuf",
                0,
                0,
                1,
            )
        )
    )
    tile_center = back_center[slot_index]
    tile_scale = back_inverse[slot_index] * col_gain
    scored = ((widened - tile_center[:, None, :]) * tile_scale[:, None, :] + col_bias).astype(
        jnp.bfloat16
    )
    standard = scored.reshape(local_rows, local_cols)
    full_rows = lax.all_to_all(standard, "rep", split_axis=0, concat_axis=1, tiled=True)
    full_weight = gathered_copies(out_weight, "rep", 0)
    summed = jnp.zeros((full_rows.shape[0], full_weight.shape[1]), jnp.float32)
    for block in range(lax.axis_size("rep")):
        partial_value = jnp.dot(
            full_rows[:, block * local_cols : (block + 1) * local_cols],
            full_weight[block * local_cols : (block + 1) * local_cols],
            preferred_element_type=jnp.float32,
        )
        summed = summed + partial_value.astype(jnp.bfloat16).astype(jnp.float32)
    return summed.astype(jnp.bfloat16)


def solution(mesh):
    return jax.shard_map(
        on_device,
        mesh=mesh,
        in_specs=(P("shuf", "rep"), P("shuf"), P("shuf", None), P("rep"), P("rep"), P("rep", None)),
        out_specs=P(("shuf", "rep"), None),
        check_vma=False,
    )
```

profile of v0, /device:TPU:32, one launch (start us, length us, event | category | flops | bytes accessed | tf_op | source)
XLA Modules:
  0.0 160.4 jit_solution(14804359981047646363)
XLA Ops:
  0.0 3.3 %convert_reduce_fusion = (f32[256]{0:T(256)S(1)}, f32[256]{0:T(256)S(1)}) fusion(bf16[8192,256]{1,0:T(8,128)(2,1)} %param.6), kind=kLoop, calls=%fused_computation.11 | loop fusion | flops 8388096 | bytes 4196352 | tf_op jit(solution)/shard_map/reduce_sum | solution.py:94
  3.4 0.7 broadcast_in_dim.10
  4.1 11.8 %all-to-all-start.1 = ((f32[64,1,512]{2,1,0:T(1,128)}), f32[64,1,512]{2,1,0:T(1,128)S(1)}, u32[]{:S(2)}, u32[]{:S(2)}) async-start(f32[64,1,512]{2,1,0:T(1,128)} %broadcast_in_dim.10), calls=%async_computation.1 | async-start | bytes 262144 | tf_op jit(solution)/shard_map/all_to_all | solution.py:14
  15.9 4.6 %bitcast_reduce_fusion = (f32[64,256]{1,0:T(8,128)S(1)}, f32[64,256]{1,0:T(8,128)S(1)}) fusion(bf16[8192,256]{1,0:T(8,128)(2,1)} %param.6), kind=kLoop, calls=%fused_computation.9 | loop fusion | flops 8355840 | bytes 4325376 | tf_op jit(solution)/shard_map/reduce_sum | solution.py:92
  20.7 0.2 select_reduce_fusion
  20.9 0.8 scatter_custom_fusion.1
  21.7 0.2 concatenate.23
  21.9 0.9 scatter_custom_fusion
  22.9 0.8 pad_maximum_fusion
  23.7 2.1 %all-to-all-done.1 = f32[64,1,512]{2,1,0:T(1,128)S(1)} async-done(((f32[64,1,512]{2,1,0:T(1,128)}), f32[64,1,512]{2,1,0:T(1,128)S(1)}, u32[]{:S(2)}, u32[]{:S(2)}) %all-to-all-start.1) | async-done | bytes 131104 | tf_op jit(solution)/shard_map/all_to_all | solution.py:14
  25.9 8.2 %all-to-all-start = ((bf16[64,2,513]{2,1,0:T(2,128)(2,1)}), bf16[64,2,513]{2,1,0:T(2,128)(2,1)S(1)}, u32[]{:S(2)}, u32[]{:S(2)}) async-start(bf16[64,2,513]{2,1,0:T(2,128)(2,1)} %pad_maximum_fusion), calls=%async_computation | async-start | bytes 327680 | tf_op jit(solution)/shard_map/all_to_all | solution.py:38
  34.1 0.1 reduce_sum.71
  34.2 10.3 %all-to-all-done = bf16[64,2,513]{2,1,0:T(2,128)(2,1)S(1)} async-done(((bf16[64,2,513]{2,1,0:T(2,128)(2,1)}), bf16[64,2,513]{2,1,0:T(2,128)(2,1)S(1)}, u32[]{:S(2)}, u32[]{:S(2)}) %all-to-all-start) | async-done | bytes 131360 | tf_op jit(solution)/shard_map/all_to_all | solution.py:38
  44.5 0.1 all_to_all.36
  44.9 0.1 fusion.8
  45.0 0.2 convolution_convert_fusion.1
  45.3 0.3 convolution_convert_fusion
  45.6 0.7 all_to_all.38
  46.3 5.5 %all-to-all-start.2 = ((bf16[64,2,512]{2,1,0:T(2,128)(2,1)}), bf16[64,2,512]{2,1,0:T(2,128)(2,1)S(1)}, u32[]{:S(2)}, u32[]{:S(2)}) async-start(bf16[64,2,512]{2,1,0:T(2,128)(2,1)} %all_to_all.38), calls=%async_computation.2 | async-start | bytes 262144 | tf_op jit(solution)/shard_map/all_to_all | solution.py:53
  51.8 10.0 %all-to-all-done.2 = bf16[64,2,512]{2,1,0:T(2,128)(2,1)S(1)} async-done(((bf16[64,2,512]{2,1,0:T(2,128)(2,1)}), bf16[64,2,512]{2,1,0:T(2,128)(2,1)S(1)}, u32[]{:S(2)}, u32[]{:S(2)}) %all-to-all-start.2) | async-done | bytes 131104 | tf_op jit(solution)/shard_map/all_to_all | solution.py:53
  61.9 0.7 gather_fusion
  62.5 0.7 gather_fusion.1
  63.2 3.6 %fusion.1 = bf16[8192,256]{1,0:T(8,128)(2,1)S(1)} fusion(bf16[8192,256]{1,0:T(8,128)(2,1)} %param.6, f32[256]{0:T(256)S(1)} %copy-done.4, f32[64,256]{1,0:T(8,128)S(1)} %broadcast_multiply_fusion, f32[64,256]{1,0:T(8,128)S(1)} %gather_fusion), kind=kLoop, calls=%fused_computation.6 | loop fusion | flops 10485760 | bytes 8520704 | tf_op jit(solution)/shard_map/convert_element_type | solution.py:142
  66.8 53.4 %all_to_all.51 = bf16[4,2048,256]{2,1,0:T(8,128)(2,1)} all-to-all(bf16[4,2048,256]{2,1,0:T(8,128)(2,1)S(1)} %bitcast.45), channel_id=1, replica_groups=mesh['shuf'=64,'rep'=4] {'rep'}, dimensions={0} | all-to-all | bytes 8388608 | tf_op jit(solution)/shard_map/all_to_all | solution.py:146
  120.2 1.6 %broadcast_in_dim.11 = bf16[4,256,1024]{2,1,0:T(8,128)(2,1)} broadcast(bf16[256,1024]{1,0:T(8,128)(2,1)S(1)} %copy-done.1), dimensions={1,2} | broadcast | bytes 2621440 | tf_op jit(solution)/shard_map/broadcast_in_dim | solution.py:15
  121.8 3.8 %all-to-all-start.4 = ((bf16[4,256,1024]{2,1,0:T(8,128)(2,1)}), bf16[4,256,1024]{2,1,0:T(8,128)(2,1)S(1)}, u32[]{:S(2)}, u32[]{:S(2)}) async-start(bf16[4,256,1024]{2,1,0:T(8,128)(2,1)} %broadcast_in_dim.11), calls=%async_computation.4 | async-start | bytes 4194304 | tf_op jit(solution)/shard_map/all_to_all | solution.py:14
  125.6 6.2 %copy.14 = bf16[2048,4,256]{0,2,1:T(8,128)(2,1)} copy(bf16[2048,4,256]{2,0,1:T(8,128)(2,1)} %bitcast.44) | data formatting | bytes 8388608 | tf_op jit(solution)/shard_map/all_to_all | solution.py:146
  131.8 19.0 %all-to-all-done.4 = bf16[4,256,1024]{2,1,0:T(8,128)(2,1)S(1)} async-done(((bf16[4,256,1024]{2,1,0:T(8,128)(2,1)}), bf16[4,256,1024]{2,1,0:T(8,128)(2,1)S(1)}, u32[]{:S(2)}, u32[]{:S(2)}) %all-to-all-start.4) | async-done | bytes 2097184 | tf_op jit(solution)/shard_map/all_to_all | solution.py:14
  150.9 2.7 %fusion.10 = bf16[2048,1024]{1,0:T(8,128)(2,1)S(1)} fusion(bf16[2048,1024]{0,1:T(8,128)(2,1)} %bitcast.40, bf16[4,256,1024]{2,1,0:T(8,128)(2,1)S(1)} %all-to-all-done.4), kind=kOutput, calls=%fused_computation.25 | convolution fusion | flops 1073741824 | bytes 5767168 | tf_op jit(solution)/shard_map/dot_general | solution.py:150
  153.5 1.3 fusion.12
  154.8 1.3 fusion.14
  156.2 4.3 %add_convert_fusion = bf16[2048,1024]{1,0:T(8,128)(2,1)} fusion(bf16[2048,1024]{1,0:T(8,128)(2,1)S(1)} %fusion.10, bf16[2048,1024]{1,0:T(8,128)(2,1)S(1)} %fusion.12, bf16[2048,1024]{1,0:T(8,128)(2,1)S(1)} %fusion.14, bf16[2048,1024]{0,1:T(8,128)(2,1)S(1)} %bitcast.43, bf16[4,256,1024]{2,1,0:T(8,128)(2,1)S(1)} %all-to-all-done.4), kind=kOutput, calls=%fused_computation.14 | convolution fusion | flops 1092616192 | bytes 18350080 | tf_op jit(solution)/shard_map/dot_general | solution.py:150
  (29 shorter events, 0.6 us)
Async XLA Ops:
  0.0 20.5 %copy-start.5 = (s32[64]{0:T(128)S(1)}, s32[64]{0:T(128)}, u32[]{:S(2)}) copy-start(s32[64]{0:T(128)} %param.7) | copy-start | bytes 772
  0.0 20.5 %copy-start.2 = (s32[64,1]{0,1:T(1,128)S(1)}, s32[64,1]{0,1:T(1,128)}, u32[]{:S(2)}) copy-start(s32[64,1]{0,1:T(1,128)} %param.8) | copy-start | bytes 772
  4.1 21.8 %all-to-all-start.1 = ((f32[64,1,512]{2,1,0:T(1,128)}), f32[64,1,512]{2,1,0:T(1,128)S(1)}, u32[]{:S(2)}, u32[]{:S(2)}) async-start(f32[64,1,512]{2,1,0:T(1,128)} %broadcast_in_dim.10), calls=%async_computation.1 | async-start | bytes 262144 | tf_op jit(solution)/shard_map/all_to_all | solution.py:14
  15.8 47.4 %copy-start.3 = (f32[256]{0:T(256)S(1)}, f32[256]{0:T(256)}, u32[]{:S(2)}) copy-start(f32[256]{0:T(256)} %param.9) | copy-start | bytes 3076
  15.8 47.4 %copy-start.4 = (f32[256]{0:T(256)S(1)}, f32[256]{0:T(256)}, u32[]{:S(2)}) copy-start(f32[256]{0:T(256)} %param.10) | copy-start | bytes 3076
  25.9 18.7 %all-to-all-start = ((bf16[64,2,513]{2,1,0:T(2,128)(2,1)}), bf16[64,2,513]{2,1,0:T(2,128)(2,1)S(1)}, u32[]{:S(2)}, u32[]{:S(2)}) async-start(bf16[64,2,513]{2,1,0:T(2,128)(2,1)} %pad_maximum_fusion), calls=%async_computation | async-start | bytes 327680 | tf_op jit(solution)/shard_map/all_to_all | solution.py:38
  46.3 15.5 %all-to-all-start.2 = ((bf16[64,2,512]{2,1,0:T(2,128)(2,1)}), bf16[64,2,512]{2,1,0:T(2,128)(2,1)S(1)}, u32[]{:S(2)}, u32[]{:S(2)}) async-start(bf16[64,2,512]{2,1,0:T(2,128)(2,1)} %all_to_all.38), calls=%async_computation.2 | async-start | bytes 262144 | tf_op jit(solution)/shard_map/all_to_all | solution.py:53
  66.8 53.4 %copy-start.1 = (bf16[256,1024]{1,0:T(8,128)(2,1)S(1)}, bf16[256,1024]{1,0:T(8,128)(2,1)}, u32[]{:S(2)}) copy-start(bf16[256,1024]{1,0:T(8,128)(2,1)} %param.11) | copy-start | bytes 1572868
  121.8 29.0 %all-to-all-start.4 = ((bf16[4,256,1024]{2,1,0:T(8,128)(2,1)}), bf16[4,256,1024]{2,1,0:T(8,128)(2,1)S(1)}, u32[]{:S(2)}, u32[]{:S(2)}) async-start(bf16[4,256,1024]{2,1,0:T(8,128)(2,1)} %broadcast_in_dim.11), calls=%async_computation.4 | async-start | bytes 4194304 | tf_op jit(solution)/shard_map/all_to_all | solution.py:14
  150.9 2.7 %copy-start = (bf16[2048,4,256]{0,2,1:T(8,128)(2,1)S(1)}, bf16[2048,4,256]{0,2,1:T(8,128)(2,1)}, u32[]{:S(2)}) copy-start(bf16[2048,4,256]{0,2,1:T(8,128)(2,1)} %copy.14) | copy-start | bytes 12582916
where the time goes:
time: 161 us; the launch traced here: 160 us
  blocking collectives  53.4 us (33%)
  waiting for transfers between devices  41.5 us (26%)
  starting transfers between devices  29.2 us (18%)
  other arithmetic  14 us (9%)
  local copies, waits for them, and re-layouts  11.8 us (7%)
  matrix products  10.2 us (6%)
    all_to_all x1, blocking collectives, on_device(): lax.all_to_all(standard, 'rep', split_axis=0, concat_axis=1, tiled=True)  53.4 us
    all_to_all x2, waiting for transfers between devices, from_everyone(): lax.all_to_all(jnp.broadcast_to(value[None], (peers, *value.shape)), axis...  21.2 us
    all_to_all x2, starting transfers between devices, from_everyone(): lax.all_to_all(jnp.broadcast_to(value[None], (peers, *value.shape)), axis...  15.5 us
    all_to_all x1, waiting for transfers between devices, side_by_side(): lax.all_to_all(both, axis, split_axis=split_dim, concat_axis=concat_dim,...  10.3 us
    all_to_all x1, waiting for transfers between devices, in_one_piece(): lax.all_to_all(both, axis, split_axis=split_dim, concat_axis=concat_dim,...  10 us
    dot_general x4, matrix products, on_device(): jnp.dot(full_rows[:, block * local_cols:(block + 1) * local_cols], full_w...  9.54 us
    all_to_all x1, starting transfers between devices, side_by_side(): lax.all_to_all(both, axis, split_axis=split_dim, concat_axis=concat_dim,...  8.21 us
    all_to_all x1, local copies, waits for them, and re-layouts, on_device(): lax.all_to_all(standard, 'rep', split_axis=0, concat_axis=1, tiled=True)  6.2 us
  transfers between devices with their start and end apart: 4, of which 4 were waited for; matrix products, arithmetic and copies ran while one was open for 9% of the time, Pallas kernels for 0%

commit v1 on v0

v1 whole, which is shorter than its diff:
```python
import jax
import jax.numpy as jnp
from jax import lax
from jax.experimental import pallas as pl
from jax.experimental.pallas import tpu as pltpu
from jax.sharding import PartitionSpec as P

PRIOR = 256.0
LANES = 128
MSG = 16
F32 = jnp.float32
BF16 = jnp.bfloat16
HIGHEST = lax.Precision.HIGHEST


def iota(shape, dim):
    return lax.broadcasted_iota(jnp.int32, shape, dim)


def exact_dot(one_hot, rows):
    return jnp.dot(one_hot.astype(BF16), rows.astype(BF16), preferred_element_type=F32)


def as_column(row, size, at):
    picked = jnp.where(at == iota((size, size), 1), jnp.broadcast_to(row, (size, size)), 0.0)
    return jnp.sum(picked, axis=1, keepdims=True)


def places(owner_row):
    size = owner_row.shape[1]
    column = as_column(owner_row, size, iota((size, size), 0))
    same = column == jnp.broadcast_to(owner_row, (size, size))
    earlier = iota((size, size), 0) < iota((size, size), 1)
    return jnp.sum(jnp.where(same & earlier, 1.0, 0.0), axis=0, keepdims=True)


def put(scratch, part, peers, at):
    for n in range(part.shape[1] // LANES):
        scratch[pl.ds(at + n, peers, stride=MSG), :] = part[:, n * LANES : (n + 1) * LANES]


def take(scratch, peers, at, count):
    return jnp.concatenate([scratch[pl.ds(at + n, peers, stride=MSG), :] for n in range(count)], axis=1)


def stats_kernel(values, owner, sub, out, mean, var, scratch, *, tiles, peers):
    step = pl.program_id(0)
    rows, cols = values.shape
    here = tiles // pl.num_programs(0)
    wide = values[...].astype(F32).reshape(here, rows // here, cols)
    inverse_rows = 1.0 / (rows // here)
    tile_mean = jnp.sum(wide, axis=1) * inverse_rows
    tile_var = jnp.sum(wide * wide, axis=1) * inverse_rows - tile_mean * tile_mean
    at = pl.multiple_of(step * here, here)
    mean[pl.ds(at, here), :] = tile_mean
    var[pl.ds(at, here), :] = tile_var

    @pl.when(step == pl.num_programs(0) - 1)
    def _():
        all_mean, all_var = mean[...], var[...]
        dev_mean = jnp.sum(all_mean, axis=0, keepdims=True) * (1.0 / tiles)
        apart = all_mean - dev_mean
        dev_var = jnp.sum(all_var + apart * apart, axis=0, keepdims=True) * (1.0 / tiles)
        owner_row = owner[...].astype(F32)
        place = places(owner_row)
        named = jnp.broadcast_to(owner_row, (peers, tiles)) == iota((peers, tiles), 0).astype(F32)
        sub_column = as_column(sub[...].astype(F32), tiles, iota((tiles, tiles), 0))
        sub_wide = jnp.broadcast_to(sub_column + 1.0, (tiles, LANES))
        for slot in range(2):
            hot = jnp.where(named & (place == float(slot)), 1.0, 0.0)
            put(scratch, exact_dot(hot, all_mean), peers, 4 * slot)
            put(scratch, exact_dot(hot, all_var), peers, 4 * slot + 2)
            put(scratch, exact_dot(hot, sub_wide) - 1.0, peers, 14 + slot)
        high = dev_mean.astype(BF16).astype(F32)
        put(scratch, jnp.broadcast_to(high, (peers, cols)), peers, 8)
        put(scratch, jnp.broadcast_to(dev_mean - high, (peers, cols)), peers, 10)
        put(scratch, jnp.broadcast_to(dev_var, (peers, cols)), peers, 12)
        out[...] = scratch[...].astype(BF16)


def owner_kernel(arrived, gain, bias, out, scratch, *, peers, tile_rows):
    scratch[...] = arrived[...].astype(F32)
    dev_mean = take(scratch, peers, 8, 2) + take(scratch, peers, 10, 2)
    mean_all = jnp.sum(dev_mean, axis=0, keepdims=True) * (1.0 / peers)
    apart = dev_mean - mean_all
    var_all = jnp.sum(take(scratch, peers, 12, 2) + apart * apart, axis=0, keepdims=True) * (1.0 / peers)
    hots, firsts, seconds = [], [], []
    for slot in range(2):
        label = take(scratch, peers, 14 + slot, 1)
        hots.append(jnp.where(label == iota((peers, LANES), 1).astype(F32), 1.0, 0.0))
        shifted = take(scratch, peers, 4 * slot, 2) - mean_all
        firsts.append(shifted)
        seconds.append(take(scratch, peers, 4 * slot + 2, 2) + shifted * shifted)
    hot = jnp.concatenate(hots, axis=0)
    data = jnp.concatenate([jnp.concatenate(firsts, axis=0), jnp.concatenate(seconds, axis=0)], axis=1)

    def by_group(rows):
        return lax.dot_general(hot, rows, (((0,), (0,)), ((), ())), precision=HIGHEST, preferred_element_type=F32)

    cols = dev_mean.shape[1]
    sums = by_group(data) * float(tile_rows)
    count = by_group(jnp.ones((2 * peers, LANES), F32)) * float(tile_rows)
    weight = jnp.concatenate([count + PRIOR] * (cols // LANES), axis=1)
    center = sums[:, :cols] / weight
    second = (sums[:, cols:] + PRIOR * var_all) / weight
    inverse = lax.rsqrt(second - center * center + 1e-05)
    scale = (inverse * gain[...]).astype(BF16)
    shift = bias[...] - (center + mean_all) * scale.astype(F32)
    shift_high = shift.astype(BF16)
    shift_low = (shift - shift_high.astype(F32)).astype(BF16)
    for slot in range(2):
        put(scratch, exact_dot(hots[slot], scale), peers, 6 * slot)
        put(scratch, exact_dot(hots[slot], shift_high), peers, 6 * slot + 2)
        put(scratch, exact_dot(hots[slot], shift_low), peers, 6 * slot + 4)
    out[...] = scratch[...].astype(BF16)


def tile_kernel(first, arrived, owner, *refs, tiles, peers, blocks):
    outs, scratch = refs[:-1], refs[-1]
    scratch[...] = arrived[...].astype(F32)
    owner_row = owner[...].astype(F32)
    at = (iota((tiles, tiles), 0) + first[0]) % tiles
    place = as_column(places(owner_row), tiles, at)
    named = as_column(owner_row, tiles, at) == iota((tiles, peers), 1).astype(F32)
    picked = 0.0
    for slot in range(2):
        hot = jnp.where(named & (place == float(slot)), 1.0, 0.0)
        picked = picked + exact_dot(hot, take(scratch, peers, 6 * slot, 6))
    each = tiles // blocks
    for n, out in enumerate(outs):
        out[...] = picked[n * each : (n + 1) * each, :].astype(BF16)


def project_kernel(*refs, blocks, tile_rows):
    values, coeffs, weights = refs[:blocks], refs[blocks : 2 * blocks], refs[2 * blocks : 3 * blocks]
    out, wide = refs[3 * blocks :]
    step = pl.program_id(0)
    rows, cols = values[0].shape

    @pl.when(step == 0)
    def _():
        for n in range(blocks):
            wide[n] = coeffs[n][...].astype(F32)

    tiles = rows // tile_rows
    total = None
    for n in range(blocks):
        parts = []
        for t in range(tiles):
            row = wide[n, pl.ds(step * tiles + t, 1), :]
            value = values[n][t * tile_rows : (t + 1) * tile_rows, :].astype(F32)
            scored = value * row[:, :cols] + (row[:, cols : 2 * cols] + row[:, 2 * cols :])
            parts.append(scored.astype(BF16))
        part = jnp.dot(jnp.concatenate(parts, axis=0), weights[n][...], preferred_element_type=F32)
        total = part if total is None else total + part
    out[...] = total.astype(BF16)


def hop(value, axis, distance):
    size = lax.axis_size(axis)
    return lax.ppermute(value, axis, [(i, (i + distance) % size) for i in range(size)])


def whole(*shape):
    return pl.BlockSpec(shape, lambda *_: (0,) * len(shape))


def on_device(values, subgroup, owners, col_gain, col_bias, out_weight):
    rows, cols = values.shape
    tiles = subgroup.shape[0]
    tile_rows = rows // tiles
    peers, blocks = lax.axis_size("shuf"), lax.axis_size("rep")
    rank = lax.axis_index("rep")
    own_rows = rows // blocks
    outputs = out_weight.shape[1]
    owner_row, sub_row = owners.reshape(1, tiles), subgroup.reshape(1, tiles)

    pieces = [
        lax.dynamic_slice(values, (((rank + d) % blocks) * own_rows, 0), (own_rows, cols))
        for d in range(blocks)
    ]
    mine, sent = pieces[0], pieces[1:]
    moved = [mine]
    for d in range(1, blocks):
        moved.append(hop(sent[d - 1], "rep", d))
    weights = [out_weight]
    for d in range(1, blocks):
        weights.append(hop(out_weight, "rep", d))

    steps = 8
    outgoing = pl.pallas_call(
        lambda *refs: stats_kernel(*refs, tiles=tiles, peers=peers),
        grid=(steps,),
        in_specs=[
            pl.BlockSpec((rows // steps, cols), lambda i: (i, 0)),
            whole(1, tiles),
            whole(1, tiles),
        ],
        out_specs=whole(peers * MSG, LANES),
        out_shape=jax.ShapeDtypeStruct((peers * MSG, LANES), BF16),
        scratch_shapes=[
            pltpu.VMEM((tiles, cols), F32),
            pltpu.VMEM((tiles, cols), F32),
            pltpu.VMEM((peers * MSG, LANES), F32),
        ],
        name="stats",
    )(values, owner_row, sub_row)

    def exchange(message):
        arrived = lax.all_to_all(message.reshape(peers, MSG, LANES), "shuf", 0, 0, tiled=True)
        return arrived.reshape(peers * MSG, LANES)

    arrived = exchange(outgoing)
    answer = pl.pallas_call(
        lambda *refs: owner_kernel(*refs, peers=peers, tile_rows=tile_rows),
        out_shape=jax.ShapeDtypeStruct((peers * MSG, LANES), BF16),
        scratch_shapes=[pltpu.VMEM((peers * MSG, LANES), F32)],
        name="moments",
    )(arrived, col_gain.reshape(1, cols), col_bias.reshape(1, cols))
    returned = exchange(answer)
    each = tiles // blocks
    coeffs = pl.pallas_call(
        lambda *refs: tile_kernel(*refs, tiles=tiles, peers=peers, blocks=blocks),
        in_specs=[
            pl.BlockSpec(memory_space=pltpu.SMEM),
            whole(peers * MSG, LANES),
            whole(1, tiles),
        ],
        out_specs=[whole(each, 3 * cols)] * blocks,
        out_shape=[jax.ShapeDtypeStruct((each, 3 * cols), BF16)] * blocks,
        scratch_shapes=[pltpu.VMEM((peers * MSG, LANES), F32)],
        name="pick",
    )((rank * each).reshape(1), returned, owner_row)
    known = [coeffs[0]]
    for d in range(1, blocks):
        known.append(hop(coeffs[d], "rep", d))

    block = min(512, own_rows)
    return pl.pallas_call(
        lambda *refs: project_kernel(*refs, blocks=blocks, tile_rows=tile_rows),
        grid=(own_rows // block,),
        in_specs=[pl.BlockSpec((block, cols), lambda i: (i, 0))] * blocks
        + [whole(each, 3 * cols)] * blocks
        + [whole(cols, outputs)] * blocks,
        out_specs=pl.BlockSpec((block, outputs), lambda i: (i, 0)),
        out_shape=jax.ShapeDtypeStruct((own_rows, outputs), BF16),
        scratch_shapes=[pltpu.VMEM((blocks, each, 3 * cols), F32)],
        name="project",
    )(*moved, *known, *weights)


def solution(mesh):
    return jax.shard_map(
        on_device,
        mesh=mesh,
        in_specs=(P("shuf", "rep"), P("shuf"), P("shuf", None), P("rep"), P("rep"), P("rep", None)),
        out_specs=P(("shuf", "rep"), None),
        check_vma=False,
    )
```

time: 161 us -> 103 us (0.64)
  blocking collectives: 53.4 us -> 0 us
  Pallas kernels: 0 us -> 19.1 us
  other arithmetic: 14 us -> 0 us
  matrix products: 10.2 us -> 0 us
  local copies, waits for them, and re-layouts: 11.8 us -> 5.89 us
  waiting for transfers between devices: 41.5 us -> 45.9 us
  starting transfers between devices: 29.2 us -> 31.2 us
    all_to_all x1 -> x0, blocking collectives: 53.4 us -> none  [on_device(): lax.all_to_all(standard, 'rep', split_axis=0, concat_axis=1, tiled=True)]
    ppermute x0 -> x9, waiting for transfers between devices: none -> 27.3 us  [hop(): lax.ppermute(value, axis, [(i, (i + distance) % size) for i in range(size)])]
    all_to_all x4 -> x2, waiting for transfers between devices: 41.5 us -> 18.6 us  [exchange(): lax.all_to_all(message.reshape(peers, MSG, LANES), 'shuf', 0, 0, tiled=True)]
    pallas_call x0 -> x4, Pallas kernels: none -> 19.1 us  [the longest x1 8.41 us: on_device(): pl.pallas_call(lambda *refs: project_kernel(*refs, blocks=blocks, tile_ro...]
    ppermute x0 -> x9, starting transfers between devices: none -> 13.2 us  [hop(): lax.ppermute(value, axis, [(i, (i + distance) % size) for i in range(size)])]
    all_to_all x4 -> x2, starting transfers between devices: 29.2 us -> 18 us  [exchange(): lax.all_to_all(message.reshape(peers, MSG, LANES), 'shuf', 0, 0, tiled=True)]
    dot_general x7 -> x0, matrix products: 10.2 us -> none  [the longest x4 9.54 us: on_device(): jnp.dot(full_rows[:, block * local_cols:(block + 1) * local_cols], full_w...]
    reduce_sum x5 -> x0, other arithmetic: 8.39 us -> none  [the longest x1 4.64 us: on_device(): tile_sum = jnp.sum(widened, axis=1)]
  transfers between devices with their start and end apart: 4 -> 11, of which waited for: 4 -> 6; matrix products, arithmetic and copies ran while one was open for 9% -> 4% of each run, Pallas kernels for 0% -> 10%
where the time goes in v1:
time: 103 us; the launch traced here: 102 us
  waiting for transfers between devices  45.9 us (45%)
  starting transfers between devices  31.2 us (30%)
  Pallas kernels  19.1 us (19%)
  local copies, waits for them, and re-layouts  5.89 us (6%)
    ppermute x9, waiting for transfers between devices, hop(): lax.ppermute(value, axis, [(i, (i + distance) % size) for i in range(size)])  27.3 us
    all_to_all x2, waiting for transfers between devices, exchange(): lax.all_to_all(message.reshape(peers, MSG, LANES), 'shuf', 0, 0, tiled=True)  18.6 us
    all_to_all x2, starting transfers between devices, exchange(): lax.all_to_all(message.reshape(peers, MSG, LANES), 'shuf', 0, 0, tiled=True)  18 us
    ppermute x9, starting transfers between devices, hop(): lax.ppermute(value, axis, [(i, (i + distance) % size) for i in range(size)])  13.2 us
    pallas_call x1, Pallas kernels, on_device(): pl.pallas_call(lambda *refs: project_kernel(*refs, blocks=blocks, tile_ro...  8.41 us
    pallas_call x1, Pallas kernels, on_device(): pl.pallas_call(lambda *refs: stats_kernel(*refs, tiles=tiles, peers=peers...  6.12 us
    dynamic_slice x1, local copies, waits for them, and re-layouts, on_device(): lax.dynamic_slice(values, ((rank + d) % blocks * own_rows, 0), (own_rows,...  3.92 us
    pallas_call x1, Pallas kernels, on_device(): pl.pallas_call(lambda *refs: owner_kernel(*refs, peers=peers, tile_rows=t...  2.61 us
  transfers between devices with their start and end apart: 11, of which 6 were waited for; matrix products, arithmetic and copies ran while one was open for 4% of the time, Pallas kernels for 10%

profile of v1, /device:TPU:32, one launch (start us, length us, event | category | flops | bytes accessed | tf_op | source)
XLA Modules:
  0.0 102.1 jit_solution(2946268300377943138)
XLA Ops:
  0.0 3.0 %collective-permute-start.7 = (bf16[256,1024]{1,0:T(8,128)(2,1)}, bf16[256,1024]{1,0:T(8,128)(2,1)}, u32[]{:S(2)}, u32[]{:S(2)}) collective-permute-start(bf16[256,1024]{1,0:T(8,128)(2,1)} %refs_8_.1), channel_id=1, source_target_pairs={{0,2},{1,3},{2,0},{3,1},{4,6},{5,7},{6,4},{7,5},{8,10},{9,11},{10,... | collective-permute-start | bytes 1572872 | tf_op jit(solution)/shard_map/ppermute | solution.py:161
  3.0 3.9 %constant_dynamic-slice_fusion = (bf16[2048,256]{1,0:T(8,128)(2,1)}, bf16[2048,256]{1,0:T(8,128)(2,1)}, bf16[2048,256]{1,0:T(8,128)(2,1)S(1)}, bf16[2048,256]{1,0:T(8,128)(2,1)}) fusion(bf16[8192,256]{1,0:T(8,128)(2,1)} %refs_0_.1, s32[]{:T(128)S(6)} %select_n.38, s32[]{:T(128)S(6)} %select_n.36, s32[]{:T(128)S(6)} %select_n.34, s32[]{:T(128)S(6)} %select_n.32), kind=kLoop, calls=%fused_computation | loop fusion | bytes 8388624 | tf_op jit(solution)/shard_map/dynamic_slice | solution.py:179
  6.9 1.1 %collective-permute-start.2 = (bf16[2048,256]{1,0:T(8,128)(2,1)}, bf16[2048,256]{1,0:T(8,128)(2,1)S(1)}, u32[]{:S(2)}, u32[]{:S(2)}) collective-permute-start(bf16[2048,256]{1,0:T(8,128)(2,1)} %get-tuple-element.13), channel_id=1, source_target_pairs={{0,3},{1,0},{2,1},{3,2},{4,7},{5,4},{6,5},{7,6},{8,11},{9,8},{10,9... | collective-permute-start | bytes 3145736 | tf_op jit(solution)/shard_map/ppermute | solution.py:161
  8.1 6.1 %stats.1 = bf16[1024,128]{1,0:T(8,128)(2,1)} custom-call(bf16[8192,256]{1,0:T(8,128)(2,1)} %refs_0_.1, s32[1,64]{1,0:T(1,128)} %bitcast.13, s32[1,64]{1,0:T(1,128)} %bitcast.17), custom_call_target="tpu_custom_call" | custom-call | tf_op jit(solution)/shard_map/stats/pallas_call | solution.py:191
  14.2 11.8 %all-to-all-start = ((bf16[64,16,128]{2,1,0:T(8,128)(2,1)}), bf16[64,16,128]{2,1,0:T(8,128)(2,1)S(1)}, u32[]{:S(2)}, u32[]{:S(2)}) async-start(bf16[64,16,128]{2,1,0:T(8,128)(2,1)} %bitcast.9), calls=%async_computation | async-start | bytes 524288 | tf_op jit(solution)/shard_map/all_to_all | solution.py:210
  26.0 1.6 %collective-permute-start.1 = (bf16[2048,256]{1,0:T(8,128)(2,1)}, bf16[2048,256]{1,0:T(8,128)(2,1)S(1)}, u32[]{:S(2)}, u32[]{:S(2)}) collective-permute-start(bf16[2048,256]{1,0:T(8,128)(2,1)} %get-tuple-element.14), channel_id=1, source_target_pairs={{0,2},{1,3},{2,0},{3,1},{4,6},{5,7},{6,4},{7,5},{8,10},{9,11},{10,... | collective-permute-start | bytes 3145736 | tf_op jit(solution)/shard_map/ppermute | solution.py:161
  27.6 0.0 collective-permute-start
  27.6 2.0 %collective-permute-start.6 = (bf16[256,1024]{1,0:T(8,128)(2,1)}, bf16[256,1024]{1,0:T(8,128)(2,1)}, u32[]{:S(2)}, u32[]{:S(2)}) collective-permute-start(bf16[256,1024]{1,0:T(8,128)(2,1)} %refs_8_.1), channel_id=1, source_target_pairs={{0,1},{1,2},{2,3},{3,0},{4,5},{5,6},{6,7},{7,4},{8,9},{9,10},{10,1... | collective-permute-start | bytes 1572872 | tf_op jit(solution)/shard_map/ppermute | solution.py:161
  29.5 0.0 collective-permute-done.7.refs_10_
  29.5 1.3 %collective-permute-start.8 = (bf16[256,1024]{1,0:T(8,128)(2,1)}, bf16[256,1024]{1,0:T(8,128)(2,1)}, u32[]{:S(2)}, u32[]{:S(2)}) collective-permute-start(bf16[256,1024]{1,0:T(8,128)(2,1)} %refs_8_.1), channel_id=1, source_target_pairs={{0,3},{1,0},{2,1},{3,2},{4,7},{5,4},{6,5},{7,6},{8,11},{9,8},{10,9... | collective-permute-start | bytes 1572872 | tf_op jit(solution)/shard_map/ppermute | solution.py:161
  30.8 6.8 %all-to-all-done = bf16[64,16,128]{2,1,0:T(8,128)(2,1)S(1)} async-done(((bf16[64,16,128]{2,1,0:T(8,128)(2,1)}), bf16[64,16,128]{2,1,0:T(8,128)(2,1)S(1)}, u32[]{:S(2)}, u32[]{:S(2)}) %all-to-all-start) | async-done | bytes 262176 | tf_op jit(solution)/shard_map/all_to_all | solution.py:210
  37.7 0.7 copy-done.2
  38.4 2.6 %moments.1 = bf16[1024,128]{1,0:T(8,128)(2,1)} custom-call(bf16[1024,128]{1,0:T(8,128)(2,1)} %bitcast.10, f32[1,256]{1,0:T(1,128)} %bitcast.15, f32[1,256]{1,0:T(1,128)} %bitcast.16), custom_call_target="tpu_custom_call" | custom-call | tf_op jit(solution)/shard_map/moments/pallas_call | solution.py:214
  41.0 6.3 %all-to-all-start.1 = ((bf16[64,16,128]{2,1,0:T(8,128)(2,1)}), bf16[64,16,128]{2,1,0:T(8,128)(2,1)S(1)}, u32[]{:S(2)}, u32[]{:S(2)}) async-start(bf16[64,16,128]{2,1,0:T(8,128)(2,1)} %bitcast.12), calls=%async_computation.1 | async-start | bytes 524288 | tf_op jit(solution)/shard_map/all_to_all | solution.py:210
  47.3 11.7 %all-to-all-done.1 = bf16[64,16,128]{2,1,0:T(8,128)(2,1)S(1)} async-done(((bf16[64,16,128]{2,1,0:T(8,128)(2,1)}), bf16[64,16,128]{2,1,0:T(8,128)(2,1)S(1)}, u32[]{:S(2)}, u32[]{:S(2)}) %all-to-all-start.1) | async-done | bytes 262176 | tf_op jit(solution)/shard_map/all_to_all | solution.py:210
  59.0 0.7 copy-done.3
  59.7 2.0 %pick.1 = (bf16[16,768]{1,0:T(8,128)(2,1)}, bf16[16,768]{1,0:T(8,128)(2,1)}, bf16[16,768]{1,0:T(8,128)(2,1)}, bf16[16,768]{1,0:T(8,128)(2,1)}) custom-call(s32[1]{0:T(128)} %bitcast.refs_0_, bf16[1024,128]{1,0:T(8,128)(2,1)} %bitcast.11, s32[1,64]{1,0:T(1,128)} %bitcast.14), custom_call_target="tpu_custom_call" | custom-call | tf_op jit(solution)/shard_map/pick/pallas_call | solution.py:222
  61.7 25.1 %collective-permute-done.6.refs_9_ = bf16[256,1024]{1,0:T(8,128)(2,1)} collective-permute-done((bf16[256,1024]{1,0:T(8,128)(2,1)}, bf16[256,1024]{1,0:T(8,128)(2,1)}, u32[]{:S(2)}, u32[]{:S(2)}) %collective-permute-start.6) | collective-permute-done | bytes 524320 | tf_op jit(solution)/shard_map/ppermute | solution.py:161
  86.8 0.1 collective-permute-start.3
  86.8 0.0 collective-permute-done.8.refs_11_
  86.8 2.0 %collective-permute-start.4 = (bf16[16,768]{1,0:T(8,128)(2,1)}, bf16[16,768]{1,0:T(8,128)(2,1)S(1)}, u32[]{:S(2)}, u32[]{:S(2)}) collective-permute-start(bf16[16,768]{1,0:T(8,128)(2,1)} %get-tuple-element.11), channel_id=1, source_target_pairs={{0,2},{1,3},{2,0},{3,1},{4,6},{5,7},{6,4},{7,5},{8,10},{9,11},{10,... | collective-permute-start | bytes 73736 | tf_op jit(solution)/shard_map/ppermute | solution.py:161
  88.8 0.0 collective-permute-done.2.refs_3_
  88.8 2.1 %collective-permute-start.5 = (bf16[16,768]{1,0:T(8,128)(2,1)}, bf16[16,768]{1,0:T(8,128)(2,1)S(1)}, u32[]{:S(2)}, u32[]{:S(2)}) collective-permute-start(bf16[16,768]{1,0:T(8,128)(2,1)} %get-tuple-element.12), channel_id=1, source_target_pairs={{0,3},{1,0},{2,1},{3,2},{4,7},{5,4},{6,5},{7,6},{8,11},{9,8},{10,9... | collective-permute-start | bytes 73736 | tf_op jit(solution)/shard_map/ppermute | solution.py:161
  90.9 0.0 collective-permute-done.1.refs_2_
  90.9 0.0 collective-permute-done.refs_1_
  90.9 1.1 %collective-permute-done.3.refs_5_ = bf16[16,768]{1,0:T(8,128)(2,1)S(1)} collective-permute-done((bf16[16,768]{1,0:T(8,128)(2,1)}, bf16[16,768]{1,0:T(8,128)(2,1)S(1)}, u32[]{:S(2)}, u32[]{:S(2)}) %collective-permute-start.3) | collective-permute-done | bytes 24608 | tf_op jit(solution)/shard_map/ppermute | solution.py:161
  92.0 0.4 collective-permute-done.4.refs_6_
  92.4 0.8 collective-permute-done.5.refs_7_
  93.1 0.0 copy-done
  93.1 0.0 copy-done.4
  93.2 0.6 copy-done.6
  93.7 8.4 %project.1 = bf16[2048,1024]{1,0:T(8,128)(2,1)} custom-call(bf16[2048,256]{1,0:T(8,128)(2,1)} %get-tuple-element.16.refs_0_, bf16[2048,256]{1,0:T(8,128)(2,1)} %collective-permute-done.refs_1_, bf16[2048,256]{1,0:T(8,128)(2,1)} %copy-done.1, bf16[2048,256]{1,0:T(8,128)(2,1)} %copy-done, bf16[16,768]{1,0:T(8,128)(2,1)} %get-tuple-element.9.refs_4_, ...), custom_call_target="tpu_custom_call" | custom-call | tf_op jit(solution)/shard_map/project/pallas_call | solution.py:239
  (9 shorter events, 0.0 us)
Async XLA Ops:
  0.0 29.5 %collective-permute-start.7 = (bf16[256,1024]{1,0:T(8,128)(2,1)}, bf16[256,1024]{1,0:T(8,128)(2,1)}, u32[]{:S(2)}, u32[]{:S(2)}) collective-permute-start(bf16[256,1024]{1,0:T(8,128)(2,1)} %refs_8_.1), channel_id=1, source_target_pairs={{0,2},{1,3},{2,0},{3,1},{4,6},{5,7},{6,4},{7,5},{8,10},{9,11},{10,... | collective-permute-start | bytes 1572872 | tf_op jit(solution)/shard_map/ppermute | solution.py:161
  6.9 81.9 %collective-permute-start.2 = (bf16[2048,256]{1,0:T(8,128)(2,1)}, bf16[2048,256]{1,0:T(8,128)(2,1)S(1)}, u32[]{:S(2)}, u32[]{:S(2)}) collective-permute-start(bf16[2048,256]{1,0:T(8,128)(2,1)} %get-tuple-element.13), channel_id=1, source_target_pairs={{0,3},{1,0},{2,1},{3,2},{4,7},{5,4},{6,5},{7,6},{8,11},{9,8},{10,9... | collective-permute-start | bytes 3145736 | tf_op jit(solution)/shard_map/ppermute | solution.py:161
  14.2 23.5 %all-to-all-start = ((bf16[64,16,128]{2,1,0:T(8,128)(2,1)}), bf16[64,16,128]{2,1,0:T(8,128)(2,1)S(1)}, u32[]{:S(2)}, u32[]{:S(2)}) async-start(bf16[64,16,128]{2,1,0:T(8,128)(2,1)} %bitcast.9), calls=%async_computation | async-start | bytes 524288 | tf_op jit(solution)/shard_map/all_to_all | solution.py:210
  26.0 65.0 %collective-permute-start.1 = (bf16[2048,256]{1,0:T(8,128)(2,1)}, bf16[2048,256]{1,0:T(8,128)(2,1)S(1)}, u32[]{:S(2)}, u32[]{:S(2)}) collective-permute-start(bf16[2048,256]{1,0:T(8,128)(2,1)} %get-tuple-element.14), channel_id=1, source_target_pairs={{0,2},{1,3},{2,0},{3,1},{4,6},{5,7},{6,4},{7,5},{8,10},{9,11},{10,... | collective-permute-start | bytes 3145736 | tf_op jit(solution)/shard_map/ppermute | solution.py:161
  27.6 63.4 %collective-permute-start = (bf16[2048,256]{1,0:T(8,128)(2,1)S(1)}, bf16[2048,256]{1,0:T(8,128)(2,1)}, u32[]{:S(2)}, u32[]{:S(2)}) collective-permute-start(bf16[2048,256]{1,0:T(8,128)(2,1)S(1)} %get-tuple-element.15), channel_id=1, source_target_pairs={{0,1},{1,2},{2,3},{3,0},{4,5},{5,6},{6,7},{7,4},{8,9},{9,10},{10,1... | collective-permute-start | bytes 3145736 | tf_op jit(solution)/shard_map/ppermute | solution.py:161
  27.6 59.2 %collective-permute-start.6 = (bf16[256,1024]{1,0:T(8,128)(2,1)}, bf16[256,1024]{1,0:T(8,128)(2,1)}, u32[]{:S(2)}, u32[]{:S(2)}) collective-permute-start(bf16[256,1024]{1,0:T(8,128)(2,1)} %refs_8_.1), channel_id=1, source_target_pairs={{0,1},{1,2},{2,3},{3,0},{4,5},{5,6},{6,7},{7,4},{8,9},{9,10},{10,1... | collective-permute-start | bytes 1572872 | tf_op jit(solution)/shard_map/ppermute | solution.py:161
  29.5 57.3 %collective-permute-start.8 = (bf16[256,1024]{1,0:T(8,128)(2,1)}, bf16[256,1024]{1,0:T(8,128)(2,1)}, u32[]{:S(2)}, u32[]{:S(2)}) collective-permute-start(bf16[256,1024]{1,0:T(8,128)(2,1)} %refs_8_.1), channel_id=1, source_target_pairs={{0,3},{1,0},{2,1},{3,2},{4,7},{5,4},{6,5},{7,6},{8,11},{9,8},{10,9... | collective-permute-start | bytes 1572872 | tf_op jit(solution)/shard_map/ppermute | solution.py:161
  37.7 0.7 copy-start.2
  41.0 18.0 %all-to-all-start.1 = ((bf16[64,16,128]{2,1,0:T(8,128)(2,1)}), bf16[64,16,128]{2,1,0:T(8,128)(2,1)S(1)}, u32[]{:S(2)}, u32[]{:S(2)}) async-start(bf16[64,16,128]{2,1,0:T(8,128)(2,1)} %bitcast.12), calls=%async_computation.1 | async-start | bytes 524288 | tf_op jit(solution)/shard_map/all_to_all | solution.py:210
  59.0 0.7 copy-start.3
  86.8 5.2 %collective-permute-start.3 = (bf16[16,768]{1,0:T(8,128)(2,1)}, bf16[16,768]{1,0:T(8,128)(2,1)S(1)}, u32[]{:S(2)}, u32[]{:S(2)}) collective-permute-start(bf16[16,768]{1,0:T(8,128)(2,1)} %get-tuple-element.10), channel_id=1, source_target_pairs={{0,1},{1,2},{2,3},{3,0},{4,5},{5,6},{6,7},{7,4},{8,9},{9,10},{10,1... | collective-permute-start | bytes 73736 | tf_op jit(solution)/shard_map/ppermute | solution.py:161
  86.8 5.5 %collective-permute-start.4 = (bf16[16,768]{1,0:T(8,128)(2,1)}, bf16[16,768]{1,0:T(8,128)(2,1)S(1)}, u32[]{:S(2)}, u32[]{:S(2)}) collective-permute-start(bf16[16,768]{1,0:T(8,128)(2,1)} %get-tuple-element.11), channel_id=1, source_target_pairs={{0,2},{1,3},{2,0},{3,1},{4,6},{5,7},{6,4},{7,5},{8,10},{9,11},{10,... | collective-permute-start | bytes 73736 | tf_op jit(solution)/shard_map/ppermute | solution.py:161
  88.8 4.3 %copy-start = (bf16[2048,256]{1,0:T(8,128)(2,1)}, bf16[2048,256]{1,0:T(8,128)(2,1)S(1)}, u32[]{:S(2)}) copy-start(bf16[2048,256]{1,0:T(8,128)(2,1)S(1)} %collective-permute-done.2.refs_3_) | copy-start | bytes 3145732
  88.8 4.3 %collective-permute-start.5 = (bf16[16,768]{1,0:T(8,128)(2,1)}, bf16[16,768]{1,0:T(8,128)(2,1)S(1)}, u32[]{:S(2)}, u32[]{:S(2)}) collective-permute-start(bf16[16,768]{1,0:T(8,128)(2,1)} %get-tuple-element.12), channel_id=1, source_target_pairs={{0,3},{1,0},{2,1},{3,2},{4,7},{5,4},{6,5},{7,6},{8,11},{9,8},{10,9... | collective-permute-start | bytes 73736 | tf_op jit(solution)/shard_map/ppermute | solution.py:161
  90.9 2.2 %copy-start.1 = (bf16[2048,256]{1,0:T(8,128)(2,1)}, bf16[2048,256]{1,0:T(8,128)(2,1)S(1)}, u32[]{:S(2)}) copy-start(bf16[2048,256]{1,0:T(8,128)(2,1)S(1)} %collective-permute-done.1.refs_2_) | copy-start | bytes 3145732
  92.0 1.1 %copy-start.4 = (bf16[16,768]{1,0:T(8,128)(2,1)}, bf16[16,768]{1,0:T(8,128)(2,1)S(1)}, u32[]{:S(2)}) copy-start(bf16[16,768]{1,0:T(8,128)(2,1)S(1)} %collective-permute-done.3.refs_5_) | copy-start | bytes 73732
  92.4 0.8 copy-start.5
  93.1 0.6 copy-start.6

commit v2 on v1

v2 whole, which is shorter than its diff:
```python
import jax
import jax.numpy as jnp
from jax import lax
from jax.experimental import pallas as pl
from jax.experimental.pallas import tpu as pltpu
from jax.sharding import PartitionSpec as P

GRP_DEV = 32
PRIOR = 256.0
LANES = 128
MSG = 16
F32 = jnp.float32
BF16 = jnp.bfloat16
MIB = 1 << 20


def iota(shape, dim):
    return lax.broadcasted_iota(jnp.int32, shape, dim)


def exact_dot(one_hot, rows):
    return jnp.dot(one_hot.astype(BF16), rows.astype(BF16), preferred_element_type=F32)


def as_column(row, size, at):
    picked = jnp.where(at == iota((size, size), 1), jnp.broadcast_to(row, (size, size)), 0.0)
    return jnp.sum(picked, axis=1, keepdims=True)


def places(owner_row):
    size = owner_row.shape[1]
    column = as_column(owner_row, size, iota((size, size), 0))
    same = column == jnp.broadcast_to(owner_row, (size, size))
    earlier = iota((size, size), 0) < iota((size, size), 1)
    return jnp.sum(jnp.where(same & earlier, 1.0, 0.0), axis=0, keepdims=True)


def put(scratch, part, peers, at):
    for n in range(part.shape[1] // LANES):
        scratch[pl.ds(at + n, peers, stride=MSG), :] = part[:, n * LANES : (n + 1) * LANES]


def take(scratch, peers, at, count):
    return jnp.concatenate([scratch[pl.ds(at + n, peers, stride=MSG), :] for n in range(count)], axis=1)


def cut_kernel(start, *refs, count, rows):
    sources, outs, sems = refs[:count], refs[count : 2 * count], refs[2 * count]
    copies = [
        pltpu.make_async_copy(sources[n].at[pl.ds(pl.multiple_of(start[n], rows[n]), rows[n]), :], outs[n], sems.at[n])
        for n in range(count)
    ]
    for copy in copies:
        copy.start()
    for copy in copies:
        copy.wait()


def stack_kernel(*refs):
    parts, out = refs[:-1], refs[-1]
    rows = parts[0].shape[0]
    for n, part in enumerate(parts):
        out[n * rows : (n + 1) * rows, :] = part[...]


def stats_kernel(values, owner, sub, out, first, second, scratch, *, tiles, peers):
    step = pl.program_id(0)
    rows, cols = values.shape
    here = tiles // pl.num_programs(0)
    tile_rows = rows // here
    chunk = 16

    def one_tile(t, carry):
        low = high = None
        for n in range(tile_rows // chunk):
            at = pl.multiple_of(t * tile_rows + n * chunk, chunk)
            wide = values[pl.ds(at, chunk), :].astype(F32)
            low, high = (wide, wide * wide) if low is None else (low + wide, high + wide * wide)
        at = pl.multiple_of((step * here + t) * 8, 8)
        for n in range(cols // LANES):
            lanes = slice(n * LANES, (n + 1) * LANES)
            first[n, pl.ds(at, 8), :] = low[:8, lanes] + low[8:, lanes]
            second[n, pl.ds(at, 8), :] = high[:8, lanes] + high[8:, lanes]
        return carry

    lax.fori_loop(0, here, one_tile, 0, unroll=2)

    @pl.when(step == pl.num_programs(0) - 1)
    def _():
        def folded(ref):
            halves = []
            for n in range(cols // LANES):
                rows = [ref[n, pl.ds(r, tiles, stride=8), :] for r in range(8)]
                while len(rows) > 1:
                    rows = [a + b for a, b in zip(rows[::2], rows[1::2])]
                halves.append(rows[0])
            return jnp.concatenate(halves, axis=1) * (1.0 / tile_rows)

        all_mean = folded(first)
        all_var = folded(second) - all_mean * all_mean
        dev_mean = jnp.sum(all_mean, axis=0, keepdims=True) * (1.0 / tiles)
        apart = all_mean - dev_mean
        dev_var = jnp.sum(all_var + apart * apart, axis=0, keepdims=True) * (1.0 / tiles)
        owner_row = owner[...].astype(F32)
        place = places(owner_row)
        named = jnp.broadcast_to(owner_row, (peers, tiles)) == iota((peers, tiles), 0).astype(F32)
        sub_column = as_column(sub[...].astype(F32), tiles, iota((tiles, tiles), 0))
        sub_wide = jnp.broadcast_to(sub_column + 1.0, (tiles, LANES))
        hot = jnp.concatenate([jnp.where(named & (place == float(slot)), 1.0, 0.0) for slot in range(2)], axis=0)
        sent = exact_dot(hot, jnp.concatenate([all_mean, all_var, sub_wide], axis=1))
        for slot in range(2):
            here = sent[slot * peers : (slot + 1) * peers, :]
            put(scratch, here[:, : 2 * cols], peers, 4 * slot)
            put(scratch, here[:, 2 * cols :] - 1.0, peers, 14 + slot)
        high = dev_mean.astype(BF16).astype(F32)
        put(scratch, jnp.broadcast_to(high, (peers, cols)), peers, 8)
        put(scratch, jnp.broadcast_to(dev_mean - high, (peers, cols)), peers, 10)
        put(scratch, jnp.broadcast_to(dev_var, (peers, cols)), peers, 12)
        out[...] = scratch[...].astype(BF16)


def owner_kernel(arrived, gain, bias, out, scratch, *, peers, tile_rows):
    scratch[...] = arrived[...].astype(F32)
    dev_mean = take(scratch, peers, 8, 2) + take(scratch, peers, 10, 2)
    mean_all = jnp.sum(dev_mean, axis=0, keepdims=True) * (1.0 / peers)
    apart = dev_mean - mean_all
    var_all = jnp.sum(take(scratch, peers, 12, 2) + apart * apart, axis=0, keepdims=True) * (1.0 / peers)
    cols = dev_mean.shape[1]
    forth, back, firsts, seconds = [], [], [], []
    for slot in range(2):
        label = take(scratch, peers, 14 + slot, 1)
        back.append(jnp.where(label[:, :GRP_DEV] == iota((peers, GRP_DEV), 1).astype(F32), 1.0, 0.0))
        on_diagonal = iota((peers, peers), 0) == iota((peers, peers), 1)
        row = jnp.sum(jnp.where(on_diagonal, label[:, :peers], 0.0), axis=0, keepdims=True)
        wide = jnp.broadcast_to(row, (GRP_DEV, peers))
        forth.append(jnp.where(wide == iota((GRP_DEV, peers), 0).astype(F32), 1.0, 0.0))
        shifted = take(scratch, peers, 4 * slot, 2) - mean_all
        firsts.append(shifted)
        seconds.append(take(scratch, peers, 4 * slot + 2, 2) + shifted * shifted)
    forth = jnp.concatenate(forth, axis=1)
    count = jnp.sum(forth, axis=1, keepdims=True) * float(tile_rows)
    data = jnp.concatenate([jnp.concatenate(firsts, axis=0), jnp.concatenate(seconds, axis=0)], axis=1)
    high = data.astype(BF16).astype(F32)
    middle = (data - high).astype(BF16).astype(F32)
    parts = exact_dot(forth, jnp.concatenate([high, middle, data - high - middle], axis=1))
    sums = (parts[:, : 2 * cols] + parts[:, 2 * cols : 4 * cols] + parts[:, 4 * cols :]) * float(tile_rows)
    portion = 1.0 / (count + PRIOR)
    center = sums[:, :cols] * portion
    second = (sums[:, cols:] + PRIOR * var_all) * portion
    inverse = lax.rsqrt(second - center * center + 1e-05)
    scale = (inverse * gain[...]).astype(BF16).astype(F32)
    shift = bias[...] - (center + mean_all) * scale
    shift_high = shift.astype(BF16).astype(F32)
    reply = exact_dot(
        jnp.concatenate(back, axis=0), jnp.concatenate([scale, shift_high, shift - shift_high], axis=1)
    )
    for slot in range(2):
        put(scratch, reply[slot * peers : (slot + 1) * peers, :], peers, 6 * slot)
    out[...] = scratch[...].astype(BF16)


def tile_kernel(first, arrived, owner, *refs, tiles, peers, blocks):
    outs, scratch = refs[:-1], refs[-1]
    scratch[...] = arrived[...].astype(F32)
    owner_row = owner[...].astype(F32)
    at = (iota((tiles, tiles), 0) + first[0]) % tiles
    place = as_column(places(owner_row), tiles, at)
    named = as_column(owner_row, tiles, at) == iota((tiles, peers), 1).astype(F32)
    hot = jnp.concatenate([jnp.where(named & (place == float(slot)), 1.0, 0.0) for slot in range(2)], axis=1)
    rows = jnp.concatenate([take(scratch, peers, 6 * slot, 6) for slot in range(2)], axis=0)
    picked = exact_dot(hot, rows)
    each = tiles // blocks
    for n, out in enumerate(outs):
        out[...] = picked[n * each : (n + 1) * each, :].astype(BF16)


def project_kernel(place, own, *refs, blocks, tile_rows, slabs):
    moved, coeffs = refs[: blocks - 1], refs[blocks - 1 : 2 * blocks - 1]
    near, far, out, wide, weight = refs[2 * blocks - 1 :]
    step = pl.program_id(0)
    rows, cols = own.shape
    tiles = rows // tile_rows
    slab = near.shape[0] // (slabs * blocks)

    @pl.when(step == 0)
    def _():
        for n in range(blocks):
            wide[n] = coeffs[n][...].astype(F32)
        for e in range(slabs):
            first = lax.rem(place[1] + slabs - e, slabs) * 2
            for n in range(blocks):
                for source, core in ((near, place[2]), (far, 1 - place[2])):
                    at = pl.multiple_of(n * cols + (first + core) * slab, slab)
                    weight[pl.ds(at, slab), :] = source[pl.ds((e * blocks + n) * slab, slab), :]

    strips = []
    for t in range(tiles):
        parts = []
        for n in range(blocks):
            row = wide[n, pl.ds(step * tiles + t, 1), :]
            if n == 0:
                value = own[t * tile_rows : (t + 1) * tile_rows, :]
            else:
                at = pl.multiple_of(step * rows + t * tile_rows, tile_rows)
                value = moved[n - 1][pl.ds(at, tile_rows), :]
            scored = value.astype(F32) * row[:, :cols] + (row[:, cols : 2 * cols] + row[:, 2 * cols :])
            parts.append(scored.astype(BF16))
        strips.append(jnp.concatenate(parts, axis=1))
    out[...] = jnp.dot(jnp.concatenate(strips, axis=0), weight[...], preferred_element_type=F32).astype(BF16)


def hop(value, axis, distance):
    size = lax.axis_size(axis)
    return lax.ppermute(value, axis, [(i, (i + distance) % size) for i in range(size)])


def whole(*shape):
    return pl.BlockSpec(shape, lambda *_: (0,) * len(shape))


IN_VMEM = pl.BlockSpec(memory_space=pltpu.VMEM)
IN_SMEM = pl.BlockSpec(memory_space=pltpu.SMEM)
IN_HBM = pl.BlockSpec(memory_space=pltpu.HBM)


def on_chip(shape, dtype):
    return pltpu.VMEM(shape, dtype)


def limit(mib):
    return pltpu.CompilerParams(vmem_limit_bytes=mib * MIB)


def held(value):
    return pltpu.with_memory_space_constraint(value, pltpu.VMEM)


def off_chip(value):
    return pltpu.with_memory_space_constraint(value, pltpu.HBM)


def cut(start, sources, rows):
    return pl.pallas_call(
        lambda *refs: cut_kernel(*refs, count=len(sources), rows=rows),
        in_specs=[IN_SMEM] + [IN_HBM] * len(sources),
        out_specs=[IN_VMEM] * len(sources),
        out_shape=[on_chip((r, s.shape[1]), s.dtype) for r, s in zip(rows, sources)],
        scratch_shapes=[pltpu.SemaphoreType.DMA((len(sources),))],
        compiler_params=limit(6),
    )(start, *[off_chip(source) for source in sources])


def stacked(parts):
    rows, cols = parts[0].shape
    return pl.pallas_call(
        stack_kernel,
        in_specs=[IN_VMEM] * len(parts),
        out_specs=IN_VMEM,
        out_shape=on_chip((len(parts) * rows, cols), parts[0].dtype),
        compiler_params=limit(6),
    )(*[held(part) for part in parts])


def on_device(values, subgroup, owners, col_gain, col_bias, out_weight):
    rows, cols = values.shape
    tiles = subgroup.shape[0]
    tile_rows = rows // tiles
    peers, blocks = lax.axis_size("shuf"), lax.axis_size("rep")
    rank, index = lax.axis_index("rep"), lax.axis_index("shuf")
    own_rows = rows // blocks
    outputs = out_weight.shape[1]
    owner_row, sub_row = owners.reshape(1, tiles), subgroup.reshape(1, tiles)

    slabs = 4
    depth = peers // (2 * slabs)
    slab_at, core = index // (2 * depth), index % 2
    slab = cols // (2 * slabs)

    def along_slabs(value, e):
        pairs = [(i, (i + e * 2 * depth) % peers) for i in range(peers)]
        return lax.ppermute(value, "shuf", pairs)

    def quarter(d):
        return ((rank + d) % blocks) * own_rows

    moved = {}
    (sent,) = cut(quarter(2).reshape(1), [values], [own_rows])
    moved[2] = hop(sent, "rep", 2)

    steps = 4
    outgoing = pl.pallas_call(
        lambda *refs: stats_kernel(*refs, tiles=tiles, peers=peers),
        grid=(steps,),
        in_specs=[
            pl.BlockSpec((rows // steps, cols), lambda i: (i, 0)),
            whole(1, tiles),
            whole(1, tiles),
        ],
        out_specs=whole(peers * MSG, LANES),
        out_shape=jax.ShapeDtypeStruct((peers * MSG, LANES), BF16),
        scratch_shapes=[
            pltpu.VMEM((cols // LANES, tiles * 8, LANES), F32),
            pltpu.VMEM((cols // LANES, tiles * 8, LANES), F32),
            pltpu.VMEM((peers * MSG, LANES), F32),
        ],
        compiler_params=limit(8),
        name="stats",
    )(off_chip(values), owner_row, sub_row)

    def exchange(message):
        arrived = lax.all_to_all(message.reshape(peers, MSG, LANES), "shuf", 0, 0, tiled=True)
        return held(arrived.reshape(peers * MSG, LANES))

    arrived = exchange(outgoing)

    start = jnp.stack([(slab_at * 2 + core) * slab, quarter(1), quarter(3)])
    own_slab, one, three = cut(start, [out_weight, values, values], [slab, own_rows, own_rows])
    slab_parts = [own_slab]
    for d in range(1, blocks):
        slab_parts.append(hop(own_slab, "rep", d))
    moved[1] = hop(one, "rep", 1)
    moved[3] = hop(three, "rep", 3)

    answer = pl.pallas_call(
        lambda *refs: owner_kernel(*refs, peers=peers, tile_rows=tile_rows),
        in_specs=[IN_VMEM, whole(1, cols), whole(1, cols)],
        out_shape=jax.ShapeDtypeStruct((peers * MSG, LANES), BF16),
        scratch_shapes=[pltpu.VMEM((peers * MSG, LANES), F32)],
        compiler_params=limit(6),
        name="moments",
    )(arrived, col_gain.reshape(1, cols), col_bias.reshape(1, cols))
    returned = exchange(answer)

    one_slab = stacked(slab_parts)
    across = [one_slab]
    for e in range(1, slabs):
        across.append(along_slabs(one_slab, e))
    near = stacked(across)
    far = lax.ppermute(near, "shuf", [(i, i ^ 1) for i in range(peers)])

    each = tiles // blocks
    coeffs = pl.pallas_call(
        lambda *refs: tile_kernel(*refs, tiles=tiles, peers=peers, blocks=blocks),
        in_specs=[IN_SMEM, IN_VMEM, whole(1, tiles)],
        out_specs=[IN_VMEM] * blocks,
        out_shape=[on_chip((each, 3 * cols), BF16)] * blocks,
        scratch_shapes=[pltpu.VMEM((peers * MSG, LANES), F32)],
        compiler_params=limit(4),
        name="pick",
    )((rank * each).reshape(1), returned, owner_row)
    known = {0: coeffs[0]}
    for d in (2, 1, 3):
        known[d] = hop(coeffs[d], "rep", d)

    block = min(512, own_rows)
    inner = [held(moved[d]) for d in range(1, blocks)] + [held(known[d]) for d in range(blocks)]
    inner += [held(near), held(far)]
    return pl.pallas_call(
        lambda *refs: project_kernel(*refs, blocks=blocks, tile_rows=tile_rows, slabs=slabs),
        grid_spec=pltpu.PrefetchScalarGridSpec(
            num_scalar_prefetch=1,
            grid=(own_rows // block,),
            in_specs=[pl.BlockSpec((block, cols), lambda i, place: (place[0] * (own_rows // block) + i, 0))]
            + [IN_VMEM] * len(inner),
            out_specs=pl.BlockSpec((block, outputs), lambda i, place: (i, 0)),
            scratch_shapes=[
                pltpu.VMEM((blocks, each, 3 * cols), F32),
                pltpu.VMEM((blocks * cols, outputs), BF16),
            ],
        ),
        out_shape=jax.ShapeDtypeStruct((own_rows, outputs), BF16),
        compiler_params=limit(24),
        name="project",
    )(jnp.stack([rank, slab_at, core]), off_chip(values), *inner)


def solution(mesh):
    return jax.shard_map(
        on_device,
        mesh=mesh,
        in_specs=(P("shuf", "rep"), P("shuf"), P("shuf", None), P("rep"), P("rep"), P("rep", None)),
        out_specs=P(("shuf", "rep"), None),
        check_vma=False,
    )
```

time: 103 us -> 85.6 us (0.83)
  waiting for transfers between devices: 45.9 us -> 28.3 us
  local copies, waits for them, and re-layouts: 5.89 us -> 1.01 us
  starting transfers between devices: 31.2 us -> 36 us
    ppermute x9, waiting for transfers between devices: 27.3 us -> 8.29 us  [hop(): lax.ppermute(value, axis, [(i, (i + distance) % size) for i in range(size)])]
    ppermute x0 -> x4, starting transfers between devices: none -> 4.78 us  [the longest x3 4.69 us: along_slabs(): return lax.ppermute(value, 'shuf', pairs)]
    pallas_call x0 -> x4, Pallas kernels: none -> 4.44 us  [the longest x2 4.35 us: cut(): pl.pallas_call(lambda *refs: cut_kernel(*refs, count=len(sources), rows=r...]
    dynamic_slice x1 -> x0, local copies, waits for them, and re-layouts: 3.92 us -> none  [on_device(): lax.dynamic_slice(values, ((rank + d) % blocks * own_rows, 0), (own_rows,...]
    pallas_call x1, Pallas kernels: 6.12 us -> 4.49 us  [on_device(): pl.pallas_call(lambda *refs: stats_kernel(*refs, tiles=tiles, peers=peers...]
    pallas_call x1, Pallas kernels: 1.96 us -> 0.38 us  [on_device(): pl.pallas_call(lambda *refs: tile_kernel(*refs, tiles=tiles, peers=peers,...]
    all_to_all x2, waiting for transfers between devices: 18.6 us -> 20 us  [exchange(): lax.all_to_all(message.reshape(peers, MSG, LANES), 'shuf', 0, 0, tiled=True)]
    pallas_call x1, Pallas kernels: 2.61 us -> 1.36 us  [on_device(): pl.pallas_call(lambda *refs: owner_kernel(*refs, peers=peers, tile_rows=t...]
  transfers between devices with their start and end apart: 11 -> 15, of which waited for: 6 -> 8; matrix products, arithmetic and copies ran while one was open for 4% -> 0% of each run, Pallas kernels for 10% -> 9%
where the time goes in v2:
time: 85.6 us; the launch traced here: 85 us
  starting transfers between devices  36 us (42%)
  waiting for transfers between devices  28.3 us (33%)
  Pallas kernels  19.4 us (23%)
  local copies, waits for them, and re-layouts  1.01 us (1%)
    all_to_all x2, waiting for transfers between devices, exchange(): lax.all_to_all(message.reshape(peers, MSG, LANES), 'shuf', 0, 0, tiled=True)  20 us
    all_to_all x2, starting transfers between devices, exchange(): lax.all_to_all(message.reshape(peers, MSG, LANES), 'shuf', 0, 0, tiled=True)  17.1 us
    ppermute x9, starting transfers between devices, hop(): lax.ppermute(value, axis, [(i, (i + distance) % size) for i in range(size)])  14.1 us
    pallas_call x1, Pallas kernels, on_device(): pl.pallas_call(lambda *refs: project_kernel(*refs, blocks=blocks, tile_ro...  8.76 us
    ppermute x9, waiting for transfers between devices, hop(): lax.ppermute(value, axis, [(i, (i + distance) % size) for i in range(size)])  8.29 us
    ppermute x3, starting transfers between devices, along_slabs(): return lax.ppermute(value, 'shuf', pairs)  4.69 us
    pallas_call x1, Pallas kernels, on_device(): pl.pallas_call(lambda *refs: stats_kernel(*refs, tiles=tiles, peers=peers...  4.49 us
    pallas_call x2, Pallas kernels, cut(): pl.pallas_call(lambda *refs: cut_kernel(*refs, count=len(sources), rows=r...  4.35 us
  transfers between devices with their start and end apart: 15, of which 8 were waited for; matrix products, arithmetic and copies ran while one was open for 0% of the time, Pallas kernels for 9%

profile of v2, /device:TPU:32, one launch (start us, length us, event | category | flops | bytes accessed | tf_op | source)
XLA Modules:
  0.0 85.0 jit_solution(1292675264059704428)
XLA Ops:
  0.0 0.1 pad_add_fusion.1.refs_0_
  0.1 3.1 %shard_map.64 = (bf16[32,1024]{1,0:T(8,128)(2,1)S(1)}, bf16[2048,256]{1,0:T(8,128)(2,1)}, bf16[2048,256]{1,0:T(8,128)(2,1)S(1)}) custom-call(s32[3]{0:T(128)S(1)} %pad_add_fusion.1.refs_0_, bf16[256,1024]{1,0:T(8,128)(2,1)} %refs_1_.3, bf16[8192,256]{1,0:T(8,128)(2,1)} %refs_1_.5, bf16[8192,256]{1,0:T(8,128)(2,1)} %refs_1_.5), custom_call_target="tpu_custom_call" | custom-call | tf_op jit(solution)/shard_map/pallas_call | solution.py:243
  3.2 1.0 %copy-done.4 = bf16[2048,256]{1,0:T(8,128)(2,1)} copy-done((bf16[2048,256]{1,0:T(8,128)(2,1)}, bf16[2048,256]{1,0:T(8,128)(2,1)S(1)}, u32[]{:S(2)}) %copy-start.4) | copy-done | bytes 1048600
  4.2 2.8 %collective-permute-start.8 = (bf16[32,1024]{1,0:T(8,128)(2,1)S(1)}, bf16[32,1024]{1,0:T(8,128)(2,1)S(1)}, u32[]{:S(2)}, u32[]{:S(2)}) collective-permute-start(bf16[32,1024]{1,0:T(8,128)(2,1)S(1)} %get-tuple-element.18.refs_0_), channel_id=1, source_target_pairs={{0,3},{1,0},{2,1},{3,2},{4,7},{5,4},{6,5},{7,6},{8,11},{9,8},{10,9... | collective-permute-start | bytes 196616 | tf_op jit(solution)/shard_map/ppermute | solution.py:214
  7.0 0.8 collective-permute-start.7
  7.8 0.9 %collective-permute-start.6 = (bf16[32,1024]{1,0:T(8,128)(2,1)S(1)}, bf16[32,1024]{1,0:T(8,128)(2,1)S(1)}, u32[]{:S(2)}, u32[]{:S(2)}) collective-permute-start(bf16[32,1024]{1,0:T(8,128)(2,1)S(1)} %get-tuple-element.18.refs_0_), channel_id=1, source_target_pairs={{0,1},{1,2},{2,3},{3,0},{4,5},{5,6},{6,7},{7,4},{8,9},{9,10},{10,1... | collective-permute-start | bytes 196616 | tf_op jit(solution)/shard_map/ppermute | solution.py:214
  8.6 0.5 collective-permute-done.8.refs_3_
  9.2 3.5 %collective-permute-done.7.refs_2_ = bf16[32,1024]{1,0:T(8,128)(2,1)S(1)} collective-permute-done((bf16[32,1024]{1,0:T(8,128)(2,1)S(1)}, bf16[32,1024]{1,0:T(8,128)(2,1)S(1)}, u32[]{:S(2)}, u32[]{:S(2)}) %collective-permute-start.7) | collective-permute-done | bytes 65568 | tf_op jit(solution)/shard_map/ppermute | solution.py:214
  12.7 0.7 collective-permute-done.6.refs_1_
  13.5 3.1 %collective-permute-start.11 = (bf16[128,1024]{1,0:T(8,128)(2,1)S(1)}, bf16[128,1024]{1,0:T(8,128)(2,1)S(1)}, u32[]{:S(2)}, u32[]{:S(2)}) collective-permute-start(bf16[128,1024]{1,0:T(8,128)(2,1)S(1)} %shard_map.66.refs_0_), channel_id=1, source_target_pairs={{0,192},{4,196},{8,200},{12,204},{16,208},{20,212},{24,216},{28,22... | collective-permute-start | bytes 786440 | tf_op jit(solution)/shard_map/ppermute | solution.py:281
  16.5 0.6 collective-permute-start.10
  17.2 1.0 %collective-permute-start.9 = (bf16[128,1024]{1,0:T(8,128)(2,1)S(1)}, bf16[128,1024]{1,0:T(8,128)(2,1)S(1)}, u32[]{:S(2)}, u32[]{:S(2)}) collective-permute-start(bf16[128,1024]{1,0:T(8,128)(2,1)S(1)} %shard_map.66.refs_0_), channel_id=1, source_target_pairs={{0,64},{4,68},{8,72},{12,76},{16,80},{20,84},{24,88},{28,92},{32,9... | collective-permute-start | bytes 786440 | tf_op jit(solution)/shard_map/ppermute | solution.py:281
  18.1 1.2 %shard_map.65 = bf16[2048,256]{1,0:T(8,128)(2,1)S(1)} custom-call(s32[1]{0:T(128)} %bitcast.6.refs_0_, bf16[8192,256]{1,0:T(8,128)(2,1)} %refs_1_.5), custom_call_target="tpu_custom_call" | custom-call | tf_op jit(solution)/shard_map/pallas_call | solution.py:243
  19.4 1.4 %collective-permute-start.1 = (bf16[2048,256]{1,0:T(8,128)(2,1)S(1)}, bf16[2048,256]{1,0:T(8,128)(2,1)}, u32[]{:S(2)}, u32[]{:S(2)}) collective-permute-start(bf16[2048,256]{1,0:T(8,128)(2,1)S(1)} %shard_map.65), channel_id=1, source_target_pairs={{0,2},{1,3},{2,0},{3,1},{4,6},{5,7},{6,4},{7,5},{8,10},{9,11},{10,... | collective-permute-start | bytes 3145736 | tf_op jit(solution)/shard_map/ppermute | solution.py:214
  20.8 0.1 collective-permute-start
  20.9 4.5 %stats.1 = bf16[1024,128]{1,0:T(8,128)(2,1)} custom-call(bf16[8192,256]{1,0:T(8,128)(2,1)} %refs_1_.5, s32[1,64]{1,0:T(1,128)S(1)} %bitcast.18, s32[1,64]{1,0:T(1,128)S(1)} %bitcast.22), custom_call_target="tpu_custom_call" | custom-call | tf_op jit(solution)/shard_map/stats/pallas_call | solution.py:291
  25.4 10.8 %all-to-all-start = ((bf16[64,16,128]{2,1,0:T(8,128)(2,1)}), bf16[64,16,128]{2,1,0:T(8,128)(2,1)S(1)}, u32[]{:S(2)}, u32[]{:S(2)}) async-start(bf16[64,16,128]{2,1,0:T(8,128)(2,1)} %bitcast.10), calls=%async_computation | async-start | bytes 524288 | tf_op jit(solution)/shard_map/all_to_all | solution.py:311
  36.3 3.2 %collective-permute-start.2 = (bf16[2048,256]{1,0:T(8,128)(2,1)}, bf16[2048,256]{1,0:T(8,128)(2,1)}, u32[]{:S(2)}, u32[]{:S(2)}) collective-permute-start(bf16[2048,256]{1,0:T(8,128)(2,1)} %copy-done.4), channel_id=1, source_target_pairs={{0,3},{1,0},{2,1},{3,2},{4,7},{5,4},{6,5},{7,6},{8,11},{9,8},{10,9... | collective-permute-start | bytes 3145736 | tf_op jit(solution)/shard_map/ppermute | solution.py:214
  39.6 0.1 collective-permute-start.12
  39.7 8.3 %all-to-all-done = bf16[64,16,128]{2,1,0:T(8,128)(2,1)S(1)} async-done(((bf16[64,16,128]{2,1,0:T(8,128)(2,1)}), bf16[64,16,128]{2,1,0:T(8,128)(2,1)S(1)}, u32[]{:S(2)}, u32[]{:S(2)}) %all-to-all-start) | async-done | bytes 262176 | tf_op jit(solution)/shard_map/all_to_all | solution.py:311
  48.0 1.4 %moments.1 = bf16[1024,128]{1,0:T(8,128)(2,1)} custom-call(bf16[1024,128]{1,0:T(8,128)(2,1)S(1)} %bitcast.16, f32[1,256]{1,0:T(1,128)S(1)} %bitcast.20, f32[1,256]{1,0:T(1,128)S(1)} %bitcast.21), custom_call_target="tpu_custom_call" | custom-call | tf_op jit(solution)/shard_map/moments/pallas_call | solution.py:324
  49.3 6.3 %all-to-all-start.1 = ((bf16[64,16,128]{2,1,0:T(8,128)(2,1)}), bf16[64,16,128]{2,1,0:T(8,128)(2,1)S(1)}, u32[]{:S(2)}, u32[]{:S(2)}) async-start(bf16[64,16,128]{2,1,0:T(8,128)(2,1)} %bitcast.14), calls=%async_computation.1 | async-start | bytes 524288 | tf_op jit(solution)/shard_map/all_to_all | solution.py:311
  55.6 11.7 %all-to-all-done.1 = bf16[64,16,128]{2,1,0:T(8,128)(2,1)S(1)} async-done(((bf16[64,16,128]{2,1,0:T(8,128)(2,1)}), bf16[64,16,128]{2,1,0:T(8,128)(2,1)S(1)}, u32[]{:S(2)}, u32[]{:S(2)}) %all-to-all-start.1) | async-done | bytes 262176 | tf_op jit(solution)/shard_map/all_to_all | solution.py:311
  67.4 0.4 pick.1
  67.7 2.1 %collective-permute-start.3 = (bf16[16,768]{1,0:T(8,128)(2,1)S(1)}, bf16[16,768]{1,0:T(8,128)(2,1)S(1)}, u32[]{:S(2)}, u32[]{:S(2)}) collective-permute-start(bf16[16,768]{1,0:T(8,128)(2,1)S(1)} %get-tuple-element.15), channel_id=1, source_target_pairs={{0,1},{1,2},{2,3},{3,0},{4,5},{5,6},{6,7},{7,4},{8,9},{9,10},{10,1... | collective-permute-start | bytes 73736 | tf_op jit(solution)/shard_map/ppermute | solution.py:214
  69.9 2.5 %collective-permute-start.4 = (bf16[16,768]{1,0:T(8,128)(2,1)S(1)}, bf16[16,768]{1,0:T(8,128)(2,1)S(1)}, u32[]{:S(2)}, u32[]{:S(2)}) collective-permute-start(bf16[16,768]{1,0:T(8,128)(2,1)S(1)} %get-tuple-element.16), channel_id=1, source_target_pairs={{0,2},{1,3},{2,0},{3,1},{4,6},{5,7},{6,4},{7,5},{8,10},{9,11},{10,... | collective-permute-start | bytes 73736 | tf_op jit(solution)/shard_map/ppermute | solution.py:214
  72.4 0.2 collective-permute-start.5
  72.7 0.1 pad_add_fusion.refs_0_
  72.8 0.1 collective-permute-done.3.refs_6_
  72.9 2.4 %collective-permute-done.4.refs_7_ = bf16[16,768]{1,0:T(8,128)(2,1)S(1)} collective-permute-done((bf16[16,768]{1,0:T(8,128)(2,1)S(1)}, bf16[16,768]{1,0:T(8,128)(2,1)S(1)}, u32[]{:S(2)}, u32[]{:S(2)}) %collective-permute-start.4) | collective-permute-done | bytes 24608 | tf_op jit(solution)/shard_map/ppermute | solution.py:214
  75.2 1.0 %collective-permute-done.5.refs_8_ = bf16[16,768]{1,0:T(8,128)(2,1)S(1)} collective-permute-done((bf16[16,768]{1,0:T(8,128)(2,1)S(1)}, bf16[16,768]{1,0:T(8,128)(2,1)S(1)}, u32[]{:S(2)}, u32[]{:S(2)}) %collective-permute-start.5) | collective-permute-done | bytes 24608 | tf_op jit(solution)/shard_map/ppermute | solution.py:214
  76.3 8.8 %project.1 = bf16[2048,1024]{1,0:T(8,128)(2,1)} custom-call(s32[3]{0:T(128)S(1)} %pad_add_fusion.refs_0_, bf16[8192,256]{1,0:T(8,128)(2,1)} %refs_1_.5, bf16[2048,256]{1,0:T(8,128)(2,1)} %collective-permute-done.refs_2_, bf16[2048,256]{1,0:T(8,128)(2,1)} %collective-permute-done.1.refs_3_, bf16[2048,256]{1,0:T(8,128)(2,1)} %collective-permute-done.2.refs_4_, ...), custom_call_target="tpu_custom_call" | custom-call | tf_op jit(solution)/shard_map/project/pallas_call | solution.py:358
  (18 shorter events, 0.1 us)
Async XLA Ops:
  3.2 1.0 %copy-start.4 = (bf16[2048,256]{1,0:T(8,128)(2,1)}, bf16[2048,256]{1,0:T(8,128)(2,1)S(1)}, u32[]{:S(2)}) copy-start(bf16[2048,256]{1,0:T(8,128)(2,1)S(1)} %get-tuple-element.13) | copy-start | bytes 3145732
  4.2 16.7 %copy-start = (s32[64,1]{0,1:T(1,128)S(1)}, s32[64,1]{0,1:T(1,128)}, u32[]{:S(2)}) copy-start(s32[64,1]{0,1:T(1,128)} %param.8) | copy-start | bytes 772
  4.2 16.7 %copy-start.3 = (s32[64]{0:T(128)S(1)}, s32[64]{0:T(128)}, u32[]{:S(2)}) copy-start(s32[64]{0:T(128)} %param.7) | copy-start | bytes 772
  4.2 5.0 %collective-permute-start.8 = (bf16[32,1024]{1,0:T(8,128)(2,1)S(1)}, bf16[32,1024]{1,0:T(8,128)(2,1)S(1)}, u32[]{:S(2)}, u32[]{:S(2)}) collective-permute-start(bf16[32,1024]{1,0:T(8,128)(2,1)S(1)} %get-tuple-element.18.refs_0_), channel_id=1, source_target_pairs={{0,3},{1,0},{2,1},{3,2},{4,7},{5,4},{6,5},{7,6},{8,11},{9,8},{10,9... | collective-permute-start | bytes 196616 | tf_op jit(solution)/shard_map/ppermute | solution.py:214
  7.0 5.8 %collective-permute-start.7 = (bf16[32,1024]{1,0:T(8,128)(2,1)S(1)}, bf16[32,1024]{1,0:T(8,128)(2,1)S(1)}, u32[]{:S(2)}, u32[]{:S(2)}) collective-permute-start(bf16[32,1024]{1,0:T(8,128)(2,1)S(1)} %get-tuple-element.18.refs_0_), channel_id=1, source_target_pairs={{0,2},{1,3},{2,0},{3,1},{4,6},{5,7},{6,4},{7,5},{8,10},{9,11},{10,... | collective-permute-start | bytes 196616 | tf_op jit(solution)/shard_map/ppermute | solution.py:214
  7.8 5.7 %collective-permute-start.6 = (bf16[32,1024]{1,0:T(8,128)(2,1)S(1)}, bf16[32,1024]{1,0:T(8,128)(2,1)S(1)}, u32[]{:S(2)}, u32[]{:S(2)}) collective-permute-start(bf16[32,1024]{1,0:T(8,128)(2,1)S(1)} %get-tuple-element.18.refs_0_), channel_id=1, source_target_pairs={{0,1},{1,2},{2,3},{3,0},{4,5},{5,6},{6,7},{7,4},{8,9},{9,10},{10,1... | collective-permute-start | bytes 196616 | tf_op jit(solution)/shard_map/ppermute | solution.py:214
  13.5 22.8 %collective-permute-start.11 = (bf16[128,1024]{1,0:T(8,128)(2,1)S(1)}, bf16[128,1024]{1,0:T(8,128)(2,1)S(1)}, u32[]{:S(2)}, u32[]{:S(2)}) collective-permute-start(bf16[128,1024]{1,0:T(8,128)(2,1)S(1)} %shard_map.66.refs_0_), channel_id=1, source_target_pairs={{0,192},{4,196},{8,200},{12,204},{16,208},{20,212},{24,216},{28,22... | collective-permute-start | bytes 786440 | tf_op jit(solution)/shard_map/ppermute | solution.py:281
  16.5 22.9 %collective-permute-start.10 = (bf16[128,1024]{1,0:T(8,128)(2,1)S(1)}, bf16[128,1024]{1,0:T(8,128)(2,1)S(1)}, u32[]{:S(2)}, u32[]{:S(2)}) collective-permute-start(bf16[128,1024]{1,0:T(8,128)(2,1)S(1)} %shard_map.66.refs_0_), channel_id=1, source_target_pairs={{0,128},{4,132},{8,136},{12,140},{16,144},{20,148},{24,152},{28,15... | collective-permute-start | bytes 786440 | tf_op jit(solution)/shard_map/ppermute | solution.py:281
  17.2 22.3 %collective-permute-start.9 = (bf16[128,1024]{1,0:T(8,128)(2,1)S(1)}, bf16[128,1024]{1,0:T(8,128)(2,1)S(1)}, u32[]{:S(2)}, u32[]{:S(2)}) collective-permute-start(bf16[128,1024]{1,0:T(8,128)(2,1)S(1)} %shard_map.66.refs_0_), channel_id=1, source_target_pairs={{0,64},{4,68},{8,72},{12,76},{16,80},{20,84},{24,88},{28,92},{32,9... | collective-permute-start | bytes 786440 | tf_op jit(solution)/shard_map/ppermute | solution.py:281
  19.4 28.6 %copy-start.1 = (f32[256]{0:T(256)S(1)}, f32[256]{0:T(256)}, u32[]{:S(2)}) copy-start(f32[256]{0:T(256)} %param.9) | copy-start | bytes 3076
  19.4 28.6 %copy-start.2 = (f32[256]{0:T(256)S(1)}, f32[256]{0:T(256)}, u32[]{:S(2)}) copy-start(f32[256]{0:T(256)} %param.10) | copy-start | bytes 3076
  19.4 50.5 %collective-permute-start.1 = (bf16[2048,256]{1,0:T(8,128)(2,1)S(1)}, bf16[2048,256]{1,0:T(8,128)(2,1)}, u32[]{:S(2)}, u32[]{:S(2)}) collective-permute-start(bf16[2048,256]{1,0:T(8,128)(2,1)S(1)} %shard_map.65), channel_id=1, source_target_pairs={{0,2},{1,3},{2,0},{3,1},{4,6},{5,7},{6,4},{7,5},{8,10},{9,11},{10,... | collective-permute-start | bytes 3145736 | tf_op jit(solution)/shard_map/ppermute | solution.py:214
  20.8 51.6 %collective-permute-start = (bf16[2048,256]{1,0:T(8,128)(2,1)}, bf16[2048,256]{1,0:T(8,128)(2,1)}, u32[]{:S(2)}, u32[]{:S(2)}) collective-permute-start(bf16[2048,256]{1,0:T(8,128)(2,1)} %get-tuple-element.12), channel_id=1, source_target_pairs={{0,1},{1,2},{2,3},{3,0},{4,5},{5,6},{6,7},{7,4},{8,9},{9,10},{10,1... | collective-permute-start | bytes 3145736 | tf_op jit(solution)/shard_map/ppermute | solution.py:214
  25.4 22.6 %all-to-all-start = ((bf16[64,16,128]{2,1,0:T(8,128)(2,1)}), bf16[64,16,128]{2,1,0:T(8,128)(2,1)S(1)}, u32[]{:S(2)}, u32[]{:S(2)}) async-start(bf16[64,16,128]{2,1,0:T(8,128)(2,1)} %bitcast.10), calls=%async_computation | async-start | bytes 524288 | tf_op jit(solution)/shard_map/all_to_all | solution.py:311
  36.3 36.5 %collective-permute-start.2 = (bf16[2048,256]{1,0:T(8,128)(2,1)}, bf16[2048,256]{1,0:T(8,128)(2,1)}, u32[]{:S(2)}, u32[]{:S(2)}) collective-permute-start(bf16[2048,256]{1,0:T(8,128)(2,1)} %copy-done.4), channel_id=1, source_target_pairs={{0,3},{1,0},{2,1},{3,2},{4,7},{5,4},{6,5},{7,6},{8,11},{9,8},{10,9... | collective-permute-start | bytes 3145736 | tf_op jit(solution)/shard_map/ppermute | solution.py:214
  39.6 36.7 %collective-permute-start.12 = (bf16[512,1024]{1,0:T(8,128)(2,1)S(1)}, bf16[512,1024]{1,0:T(8,128)(2,1)S(1)}, u32[]{:S(2)}, u32[]{:S(2)}) collective-permute-start(bf16[512,1024]{1,0:T(8,128)(2,1)S(1)} %shard_map.67.refs_9_), channel_id=1, source_target_pairs={{0,4},{4,0},{8,12},{12,8},{16,20},{20,16},{24,28},{28,24},{32,36},... | collective-permute-start | bytes 3145736 | tf_op jit(solution)/shard_map/ppermute | solution.py:339
  49.3 18.0 %all-to-all-start.1 = ((bf16[64,16,128]{2,1,0:T(8,128)(2,1)}), bf16[64,16,128]{2,1,0:T(8,128)(2,1)S(1)}, u32[]{:S(2)}, u32[]{:S(2)}) async-start(bf16[64,16,128]{2,1,0:T(8,128)(2,1)} %bitcast.14), calls=%async_computation.1 | async-start | bytes 524288 | tf_op jit(solution)/shard_map/all_to_all | solution.py:311
  67.7 5.1 %collective-permute-start.3 = (bf16[16,768]{1,0:T(8,128)(2,1)S(1)}, bf16[16,768]{1,0:T(8,128)(2,1)S(1)}, u32[]{:S(2)}, u32[]{:S(2)}) collective-permute-start(bf16[16,768]{1,0:T(8,128)(2,1)S(1)} %get-tuple-element.15), channel_id=1, source_target_pairs={{0,1},{1,2},{2,3},{3,0},{4,5},{5,6},{6,7},{7,4},{8,9},{9,10},{10,1... | collective-permute-start | bytes 73736 | tf_op jit(solution)/shard_map/ppermute | solution.py:214
  69.9 5.3 %collective-permute-start.4 = (bf16[16,768]{1,0:T(8,128)(2,1)S(1)}, bf16[16,768]{1,0:T(8,128)(2,1)S(1)}, u32[]{:S(2)}, u32[]{:S(2)}) collective-permute-start(bf16[16,768]{1,0:T(8,128)(2,1)S(1)} %get-tuple-element.16), channel_id=1, source_target_pairs={{0,2},{1,3},{2,0},{3,1},{4,6},{5,7},{6,4},{7,5},{8,10},{9,11},{10,... | collective-permute-start | bytes 73736 | tf_op jit(solution)/shard_map/ppermute | solution.py:214
  72.4 3.8 %collective-permute-start.5 = (bf16[16,768]{1,0:T(8,128)(2,1)S(1)}, bf16[16,768]{1,0:T(8,128)(2,1)S(1)}, u32[]{:S(2)}, u32[]{:S(2)}) collective-permute-start(bf16[16,768]{1,0:T(8,128)(2,1)S(1)} %get-tuple-element.17), channel_id=1, source_target_pairs={{0,3},{1,0},{2,1},{3,2},{4,7},{5,4},{6,5},{7,6},{8,11},{9,8},{10,9... | collective-permute-start | bytes 73736 | tf_op jit(solution)/shard_map/ppermute | solution.py:214

commit v3 on v2

--- a/solution.py
+++ b/solution.py
@@ -57,10 +57,15 @@
 
 
 def stack_kernel(*refs):
-    parts, out = refs[:-1], refs[-1]
+    parts, out, sems = refs[:-2], refs[-2], refs[-1]
     rows = parts[0].shape[0]
-    for n, part in enumerate(parts):
-        out[n * rows : (n + 1) * rows, :] = part[...]
+    copies = [
+        pltpu.make_async_copy(part, out.at[n * rows : (n + 1) * rows, :], sems.at[n]) for n, part in enumerate(parts)
+    ]
+    for copy in copies:
+        copy.start()
+    for copy in copies:
+        copy.wait()
 
 
 def stats_kernel(values, owner, sub, out, first, second, scratch, *, tiles, peers):
@@ -119,7 +124,12 @@
         out[...] = scratch[...].astype(BF16)
 
 
-def owner_kernel(arrived, gain, bias, out, scratch, *, peers, tile_rows):
+def pair_kernel(gain, bias, out):
+    out[0:1, :] = gain[...]
+    out[1:2, :] = bias[...]
+
+
+def owner_kernel(arrived, both, out, scratch, *, peers, tile_rows):
     scratch[...] = arrived[...].astype(F32)
     dev_mean = take(scratch, peers, 8, 2) + take(scratch, peers, 10, 2)
     mean_all = jnp.sum(dev_mean, axis=0, keepdims=True) * (1.0 / peers)
@@ -148,8 +158,8 @@
     center = sums[:, :cols] * portion
     second = (sums[:, cols:] + PRIOR * var_all) * portion
     inverse = lax.rsqrt(second - center * center + 1e-05)
-    scale = (inverse * gain[...]).astype(BF16).astype(F32)
-    shift = bias[...] - (center + mean_all) * scale
+    scale = (inverse * both[0:1, :]).astype(BF16).astype(F32)
+    shift = both[1:2, :] - (center + mean_all) * scale
     shift_high = shift.astype(BF16).astype(F32)
     reply = exact_dot(
         jnp.concatenate(back, axis=0), jnp.concatenate([scale, shift_high, shift - shift_high], axis=1)
@@ -174,36 +184,47 @@
         out[...] = picked[n * each : (n + 1) * each, :].astype(BF16)
 
 
-def project_kernel(place, own, *refs, blocks, tile_rows, slabs):
-    moved, coeffs = refs[: blocks - 1], refs[blocks - 1 : 2 * blocks - 1]
-    near, far, out, wide, weight = refs[2 * blocks - 1 :]
+def project_kernel(place, *refs, blocks, tile_rows, slabs):
+    moved, coeffs = refs[:blocks], refs[blocks : 2 * blocks]
+    near, far, out, wide, weight, sems = refs[2 * blocks :]
     step = pl.program_id(0)
-    rows, cols = own.shape
+    rows, cols = moved[0].shape
     tiles = rows // tile_rows
     slab = near.shape[0] // (slabs * blocks)
 
-    @pl.when(step == 0)
-    def _():
-        for n in range(blocks):
-            wide[n] = coeffs[n][...].astype(F32)
+    def weight_copies():
+        copies = []
         for e in range(slabs):
             first = lax.rem(place[1] + slabs - e, slabs) * 2
             for n in range(blocks):
-                for source, core in ((near, place[2]), (far, 1 - place[2])):
+                for which, (source, core) in enumerate(((near, place[2]), (far, 1 - place[2]))):
                     at = pl.multiple_of(n * cols + (first + core) * slab, slab)
-                    weight[pl.ds(at, slab), :] = source[pl.ds((e * blocks + n) * slab, slab), :]
+                    copies.append(
+                        pltpu.make_async_copy(
+                            source.at[pl.ds((e * blocks + n) * slab, slab), :],
+                            weight.at[pl.ds(at, slab), :],
+                            sems.at[(e * blocks + n) * 2 + which],
+                        )
+                    )
+        return copies
+
+    @pl.when(step == 0)
+    def _():
+        copies = weight_copies()
+        for copy in copies:
+            copy.start()
+        for n in range(blocks):
+            wide[n] = coeffs[n][...].astype(F32)
+        for copy in copies:
+            copy.wait()
 
     strips = []
     for t in range(tiles):
         parts = []
         for n in range(blocks):
             row = wide[n, pl.ds(step * tiles + t, 1), :]
-            if n == 0:
-                value = own[t * tile_rows : (t + 1) * tile_rows, :]
-            else:
-                at = pl.multiple_of(step * rows + t * tile_rows, tile_rows)
-                value = moved[n - 1][pl.ds(at, tile_rows), :]
-            scored = value.astype(F32) * row[:, :cols] + (row[:, cols : 2 * cols] + row[:, 2 * cols :])
+            value = moved[n][t * tile_rows : (t + 1) * tile_rows, :].astype(F32)
+            scored = value * row[:, :cols] + (row[:, cols : 2 * cols] + row[:, 2 * cols :])
             parts.append(scored.astype(BF16))
         strips.append(jnp.concatenate(parts, axis=1))
     out[...] = jnp.dot(jnp.concatenate(strips, axis=0), weight[...], preferred_element_type=F32).astype(BF16)
@@ -223,10 +244,6 @@
 IN_HBM = pl.BlockSpec(memory_space=pltpu.HBM)
 
 
-def on_chip(shape, dtype):
-    return pltpu.VMEM(shape, dtype)
-
-
 def limit(mib):
     return pltpu.CompilerParams(vmem_limit_bytes=mib * MIB)
 
@@ -239,12 +256,13 @@
     return pltpu.with_memory_space_constraint(value, pltpu.HBM)
 
 
-def cut(start, sources, rows):
+def cut(start, sources, rows, on_chip_from=0):
+    kept = [pltpu.HBM] * on_chip_from + [pltpu.VMEM] * (len(sources) - on_chip_from)
     return pl.pallas_call(
         lambda *refs: cut_kernel(*refs, count=len(sources), rows=rows),
         in_specs=[IN_SMEM] + [IN_HBM] * len(sources),
-        out_specs=[IN_VMEM] * len(sources),
-        out_shape=[on_chip((r, s.shape[1]), s.dtype) for r, s in zip(rows, sources)],
+        out_specs=[pl.BlockSpec(memory_space=k) for k in kept],
+        out_shape=[k((r, s.shape[1]), s.dtype) for k, r, s in zip(kept, rows, sources)],
         scratch_shapes=[pltpu.SemaphoreType.DMA((len(sources),))],
         compiler_params=limit(6),
     )(start, *[off_chip(source) for source in sources])
@@ -254,11 +272,12 @@
     rows, cols = parts[0].shape
     return pl.pallas_call(
         stack_kernel,
-        in_specs=[IN_VMEM] * len(parts),
-        out_specs=IN_VMEM,
-        out_shape=on_chip((len(parts) * rows, cols), parts[0].dtype),
+        in_specs=[pl.BlockSpec(memory_space=pl.ANY)] * len(parts),
+        out_specs=IN_HBM,
+        out_shape=pltpu.HBM((len(parts) * rows, cols), parts[0].dtype),
+        scratch_shapes=[pltpu.SemaphoreType.DMA((len(parts),))],
         compiler_params=limit(6),
-    )(*[held(part) for part in parts])
+    )(*parts)
 
 
 def on_device(values, subgroup, owners, col_gain, col_bias, out_weight):
@@ -284,8 +303,8 @@
         return ((rank + d) % blocks) * own_rows
 
     moved = {}
-    (sent,) = cut(quarter(2).reshape(1), [values], [own_rows])
-    moved[2] = hop(sent, "rep", 2)
+    (two,) = cut(quarter(2).reshape(1), [values], [own_rows], 1)
+    moved[2] = hop(two, "rep", 2)
 
     steps = 4
     outgoing = pl.pallas_call(
@@ -321,14 +340,20 @@
     moved[1] = hop(one, "rep", 1)
     moved[3] = hop(three, "rep", 3)
 
+    both = pl.pallas_call(
+        pair_kernel,
+        out_shape=jax.ShapeDtypeStruct((2, cols), F32),
+        compiler_params=limit(1),
+        name="pair",
+    )(col_gain.reshape(1, cols), col_bias.reshape(1, cols))
     answer = pl.pallas_call(
         lambda *refs: owner_kernel(*refs, peers=peers, tile_rows=tile_rows),
-        in_specs=[IN_VMEM, whole(1, cols), whole(1, cols)],
+        in_specs=[IN_VMEM, whole(2, cols)],
         out_shape=jax.ShapeDtypeStruct((peers * MSG, LANES), BF16),
         scratch_shapes=[pltpu.VMEM((peers * MSG, LANES), F32)],
         compiler_params=limit(6),
         name="moments",
-    )(arrived, col_gain.reshape(1, cols), col_bias.reshape(1, cols))
+    )(arrived, both)
     returned = exchange(answer)
 
     one_slab = stacked(slab_parts)
@@ -343,7 +368,7 @@
         lambda *refs: tile_kernel(*refs, tiles=tiles, peers=peers, blocks=blocks),
         in_specs=[IN_SMEM, IN_VMEM, whole(1, tiles)],
         out_specs=[IN_VMEM] * blocks,
-        out_shape=[on_chip((each, 3 * cols), BF16)] * blocks,
+        out_shape=[pltpu.VMEM((each, 3 * cols), BF16)] * blocks,
         scratch_shapes=[pltpu.VMEM((peers * MSG, LANES), F32)],
         compiler_params=limit(4),
         name="pick",
@@ -353,25 +378,34 @@
         known[d] = hop(coeffs[d], "rep", d)
 
     block = min(512, own_rows)
-    inner = [held(moved[d]) for d in range(1, blocks)] + [held(known[d]) for d in range(blocks)]
-    inner += [held(near), held(far)]
+    blocked = pl.BlockSpec((block, cols), lambda i, place: (i, 0))
     return pl.pallas_call(
         lambda *refs: project_kernel(*refs, blocks=blocks, tile_rows=tile_rows, slabs=slabs),
         grid_spec=pltpu.PrefetchScalarGridSpec(
             num_scalar_prefetch=1,
             grid=(own_rows // block,),
             in_specs=[pl.BlockSpec((block, cols), lambda i, place: (place[0] * (own_rows // block) + i, 0))]
-            + [IN_VMEM] * len(inner),
+            + [blocked] * (blocks - 1)
+            + [IN_VMEM] * blocks
+            + [IN_HBM] * 2,
             out_specs=pl.BlockSpec((block, outputs), lambda i, place: (i, 0)),
             scratch_shapes=[
                 pltpu.VMEM((blocks, each, 3 * cols), F32),
                 pltpu.VMEM((blocks * cols, outputs), BF16),
+                pltpu.SemaphoreType.DMA((2 * slabs * blocks,)),
             ],
         ),
         out_shape=jax.ShapeDtypeStruct((own_rows, outputs), BF16),
         compiler_params=limit(24),
         name="project",
-    )(jnp.stack([rank, slab_at, core]), off_chip(values), *inner)
+    )(
+        jnp.stack([rank, slab_at, core]),
+        off_chip(values),
+        *[off_chip(moved[d]) for d in range(1, blocks)],
+        *[held(known[d]) for d in range(blocks)],
+        off_chip(near),
+        off_chip(far),
+    )
 
 
 def solution(mesh):

time: 85.6 us -> 117 us (1.37)
  Pallas kernels: 19.4 us -> 52.9 us
    pallas_call x2, Pallas kernels: 4.35 us -> 35 us  [cut(): pl.pallas_call(lambda *refs: cut_kernel(*refs, count=len(sources), rows=r...]
    pallas_call x2 -> x3, Pallas kernels: 0.09 us -> 1.72 us  [the longest x2 1.72 us: stacked(): pl.pallas_call(stack_kernel, in_specs=[pl.BlockSpec(memory_space=pl.ANY)]...]
    pallas_call x1, Pallas kernels: 8.76 us -> 9.95 us  [on_device(): pl.pallas_call(lambda *refs: project_kernel(*refs, blocks=blocks, tile_ro...]
  transfers between devices with their start and end apart: 15 -> 15, of which waited for: 8 -> 8; matrix products, arithmetic and copies ran while one was open for 0% -> 0% of each run, Pallas kernels for 9% -> 34%
where the time goes in v3:
time: 117 us
  Pallas kernels  52.9 us (45%)
  starting transfers between devices  36.1 us (31%)
  waiting for transfers between devices  27.4 us (23%)
    pallas_call x2, Pallas kernels, cut(): pl.pallas_call(lambda *refs: cut_kernel(*refs, count=len(sources), rows=r...  35 us
    all_to_all x2, waiting for transfers between devices, exchange(): lax.all_to_all(message.reshape(peers, MSG, LANES), 'shuf', 0, 0, tiled=True)  19 us
    all_to_all x2, starting transfers between devices, exchange(): lax.all_to_all(message.reshape(peers, MSG, LANES), 'shuf', 0, 0, tiled=True)  17.1 us
    ppermute x9, starting transfers between devices, hop(): lax.ppermute(value, axis, [(i, (i + distance) % size) for i in range(size)])  14.2 us
    pallas_call x1, Pallas kernels, on_device(): pl.pallas_call(lambda *refs: project_kernel(*refs, blocks=blocks, tile_ro...  9.95 us
    ppermute x9, waiting for transfers between devices, hop(): lax.ppermute(value, axis, [(i, (i + distance) % size) for i in range(size)])  8.3 us
    ppermute x3, starting transfers between devices, along_slabs(): return lax.ppermute(value, 'shuf', pairs)  4.69 us
    pallas_call x1, Pallas kernels, on_device(): pl.pallas_call(lambda *refs: stats_kernel(*refs, tiles=tiles, peers=peers...  4.47 us
  transfers between devices with their start and end apart: 15, of which 8 were waited for; matrix products, arithmetic and copies ran while one was open for 0% of the time, Pallas kernels for 34%

profile of v3, /device:TPU:32, one launch (start us, length us, event | category | flops | bytes accessed | tf_op | source)
XLA Modules:
  0.0 116.7 jit_solution(17565207068829458028)
XLA Ops:
  0.1 2.1 %shard_map.64 = (bf16[32,1024]{1,0:T(8,128)(2,1)S(1)}, bf16[2048,256]{1,0:T(8,128)(2,1)S(1)}, bf16[2048,256]{1,0:T(8,128)(2,1)S(1)}) custom-call(s32[3]{0:T(128)S(1)} %pad_add_fusion.1.refs_0_, bf16[256,1024]{1,0:T(8,128)(2,1)} %refs_1_.3, bf16[8192,256]{1,0:T(8,128)(2,1)} %refs_1_.5, bf16[8192,256]{1,0:T(8,128)(2,1)} %refs_1_.5), custom_call_target="tpu_custom_call" | custom-call | tf_op jit(solution)/shard_map/pallas_call | solution.py:261
  2.3 2.8 %collective-permute-start.8 = (bf16[32,1024]{1,0:T(8,128)(2,1)S(1)}, bf16[32,1024]{1,0:T(8,128)(2,1)S(1)}, u32[]{:S(2)}, u32[]{:S(2)}) collective-permute-start(bf16[32,1024]{1,0:T(8,128)(2,1)S(1)} %get-tuple-element.18.refs_0_), channel_id=1, source_target_pairs={{0,3},{1,0},{2,1},{3,2},{4,7},{5,4},{6,5},{7,6},{8,11},{9,8},{10,9... | collective-permute-start | bytes 196616 | tf_op jit(solution)/shard_map/ppermute | solution.py:235
  5.1 0.8 collective-permute-start.7
  5.9 0.9 collective-permute-start.6
  6.8 0.5 collective-permute-done.8.refs_3_
  7.3 3.5 %collective-permute-done.7.refs_2_ = bf16[32,1024]{1,0:T(8,128)(2,1)S(1)} collective-permute-done((bf16[32,1024]{1,0:T(8,128)(2,1)S(1)}, bf16[32,1024]{1,0:T(8,128)(2,1)S(1)}, u32[]{:S(2)}, u32[]{:S(2)}) %collective-permute-start.7) | collective-permute-done | bytes 65568 | tf_op jit(solution)/shard_map/ppermute | solution.py:235
  10.9 0.7 collective-permute-done.6.refs_1_
  11.6 0.7 shard_map.66.refs_0_
  12.3 3.1 %collective-permute-start.11 = (bf16[128,1024]{1,0:T(8,128)(2,1)}, bf16[128,1024]{1,0:T(8,128)(2,1)S(1)}, u32[]{:S(2)}, u32[]{:S(2)}) collective-permute-start(bf16[128,1024]{1,0:T(8,128)(2,1)} %shard_map.66.refs_0_), channel_id=1, source_target_pairs={{0,192},{4,196},{8,200},{12,204},{16,208},{20,212},{24,216},{28,22... | collective-permute-start | bytes 786440 | tf_op jit(solution)/shard_map/ppermute | solution.py:300
  15.4 0.6 collective-permute-start.10
  16.0 1.0 collective-permute-start.9
  17.0 32.9 %shard_map.65 = bf16[2048,256]{1,0:T(8,128)(2,1)} custom-call(s32[1]{0:T(128)} %bitcast.6.refs_0_, bf16[8192,256]{1,0:T(8,128)(2,1)} %refs_1_.5), custom_call_target="tpu_custom_call" | custom-call | tf_op jit(solution)/shard_map/pallas_call | solution.py:261
  49.9 1.4 %collective-permute-start.1 = (bf16[2048,256]{1,0:T(8,128)(2,1)}, bf16[2048,256]{1,0:T(8,128)(2,1)}, u32[]{:S(2)}, u32[]{:S(2)}) collective-permute-start(bf16[2048,256]{1,0:T(8,128)(2,1)} %shard_map.65), channel_id=1, source_target_pairs={{0,2},{1,3},{2,0},{3,1},{4,6},{5,7},{6,4},{7,5},{8,10},{9,11},{10,... | collective-permute-start | bytes 3145736 | tf_op jit(solution)/shard_map/ppermute | solution.py:235
  51.3 0.1 collective-permute-start
  51.4 4.5 %stats.1 = bf16[1024,128]{1,0:T(8,128)(2,1)} custom-call(bf16[8192,256]{1,0:T(8,128)(2,1)} %refs_1_.5, s32[1,64]{1,0:T(1,128)S(1)} %bitcast.18, s32[1,64]{1,0:T(1,128)S(1)} %bitcast.22), custom_call_target="tpu_custom_call" | custom-call | tf_op jit(solution)/shard_map/stats/pallas_call | solution.py:310
  55.9 10.8 %all-to-all-start = ((bf16[64,16,128]{2,1,0:T(8,128)(2,1)}), bf16[64,16,128]{2,1,0:T(8,128)(2,1)S(1)}, u32[]{:S(2)}, u32[]{:S(2)}) async-start(bf16[64,16,128]{2,1,0:T(8,128)(2,1)} %bitcast.10), calls=%async_computation | async-start | bytes 524288 | tf_op jit(solution)/shard_map/all_to_all | solution.py:330
  66.7 3.2 %collective-permute-start.2 = (bf16[2048,256]{1,0:T(8,128)(2,1)S(1)}, bf16[2048,256]{1,0:T(8,128)(2,1)}, u32[]{:S(2)}, u32[]{:S(2)}) collective-permute-start(bf16[2048,256]{1,0:T(8,128)(2,1)S(1)} %get-tuple-element.13), channel_id=1, source_target_pairs={{0,3},{1,0},{2,1},{3,2},{4,7},{5,4},{6,5},{7,6},{8,11},{9,8},{10,9... | collective-permute-start | bytes 3145736 | tf_op jit(solution)/shard_map/ppermute | solution.py:235
  70.0 1.0 shard_map.67.refs_9_
  71.0 0.1 collective-permute-start.12
  71.1 7.3 %all-to-all-done = bf16[64,16,128]{2,1,0:T(8,128)(2,1)S(1)} async-done(((bf16[64,16,128]{2,1,0:T(8,128)(2,1)}), bf16[64,16,128]{2,1,0:T(8,128)(2,1)S(1)}, u32[]{:S(2)}, u32[]{:S(2)}) %all-to-all-start) | async-done | bytes 262176 | tf_op jit(solution)/shard_map/all_to_all | solution.py:330
  78.4 1.3 %moments.1 = bf16[1024,128]{1,0:T(8,128)(2,1)} custom-call(bf16[1024,128]{1,0:T(8,128)(2,1)S(1)} %bitcast.16, f32[2,256]{1,0:T(2,128)S(1)} %pair.1.refs_1_), custom_call_target="tpu_custom_call" | custom-call | tf_op jit(solution)/shard_map/moments/pallas_call | solution.py:349
  79.8 6.3 %all-to-all-start.1 = ((bf16[64,16,128]{2,1,0:T(8,128)(2,1)}), bf16[64,16,128]{2,1,0:T(8,128)(2,1)S(1)}, u32[]{:S(2)}, u32[]{:S(2)}) async-start(bf16[64,16,128]{2,1,0:T(8,128)(2,1)} %bitcast.14), calls=%async_computation.1 | async-start | bytes 524288 | tf_op jit(solution)/shard_map/all_to_all | solution.py:330
  86.1 11.7 %all-to-all-done.1 = bf16[64,16,128]{2,1,0:T(8,128)(2,1)S(1)} async-done(((bf16[64,16,128]{2,1,0:T(8,128)(2,1)}), bf16[64,16,128]{2,1,0:T(8,128)(2,1)S(1)}, u32[]{:S(2)}, u32[]{:S(2)}) %all-to-all-start.1) | async-done | bytes 262176 | tf_op jit(solution)/shard_map/all_to_all | solution.py:330
  97.8 0.4 pick.1
  98.2 2.1 %collective-permute-start.3 = (bf16[16,768]{1,0:T(8,128)(2,1)S(1)}, bf16[16,768]{1,0:T(8,128)(2,1)S(1)}, u32[]{:S(2)}, u32[]{:S(2)}) collective-permute-start(bf16[16,768]{1,0:T(8,128)(2,1)S(1)} %get-tuple-element.15), channel_id=1, source_target_pairs={{0,1},{1,2},{2,3},{3,0},{4,5},{5,6},{6,7},{7,4},{8,9},{9,10},{10,1... | collective-permute-start | bytes 73736 | tf_op jit(solution)/shard_map/ppermute | solution.py:235
  100.3 2.5 %collective-permute-start.4 = (bf16[16,768]{1,0:T(8,128)(2,1)S(1)}, bf16[16,768]{1,0:T(8,128)(2,1)S(1)}, u32[]{:S(2)}, u32[]{:S(2)}) collective-permute-start(bf16[16,768]{1,0:T(8,128)(2,1)S(1)} %get-tuple-element.16), channel_id=1, source_target_pairs={{0,2},{1,3},{2,0},{3,1},{4,6},{5,7},{6,4},{7,5},{8,10},{9,11},{10,... | collective-permute-start | bytes 73736 | tf_op jit(solution)/shard_map/ppermute | solution.py:235
  102.9 0.2 collective-permute-start.5
  103.1 0.1 pad_add_fusion.refs_0_
  103.2 0.1 collective-permute-done.3.refs_6_
  103.3 2.4 %collective-permute-done.4.refs_7_ = bf16[16,768]{1,0:T(8,128)(2,1)S(1)} collective-permute-done((bf16[16,768]{1,0:T(8,128)(2,1)S(1)}, bf16[16,768]{1,0:T(8,128)(2,1)S(1)}, u32[]{:S(2)}, u32[]{:S(2)}) %collective-permute-start.4) | collective-permute-done | bytes 24608 | tf_op jit(solution)/shard_map/ppermute | solution.py:235
  105.7 1.0 collective-permute-done.5.refs_8_
  106.7 10.0 %project.1 = bf16[2048,1024]{1,0:T(8,128)(2,1)} custom-call(s32[3]{0:T(128)S(1)} %pad_add_fusion.refs_0_, bf16[8192,256]{1,0:T(8,128)(2,1)} %refs_1_.5, bf16[2048,256]{1,0:T(8,128)(2,1)} %collective-permute-done.refs_2_, bf16[2048,256]{1,0:T(8,128)(2,1)} %collective-permute-done.1.refs_3_, bf16[2048,256]{1,0:T(8,128)(2,1)} %collective-permute-done.2.refs_4_, ...), custom_call_target="tpu_custom_call" | custom-call | tf_op jit(solution)/shard_map/project/pallas_call | solution.py:382
  (19 shorter events, 0.1 us)
Async XLA Ops:
  2.2 49.2 %copy-start.1 = (s32[64,1]{0,1:T(1,128)S(1)}, s32[64,1]{0,1:T(1,128)}, u32[]{:S(2)}) copy-start(s32[64,1]{0,1:T(1,128)} %param.8) | copy-start | bytes 772
  2.2 49.2 %copy-start.4 = (s32[64]{0:T(128)S(1)}, s32[64]{0:T(128)}, u32[]{:S(2)}) copy-start(s32[64]{0:T(128)} %param.7) | copy-start | bytes 772
  2.3 5.1 %collective-permute-start.8 = (bf16[32,1024]{1,0:T(8,128)(2,1)S(1)}, bf16[32,1024]{1,0:T(8,128)(2,1)S(1)}, u32[]{:S(2)}, u32[]{:S(2)}) collective-permute-start(bf16[32,1024]{1,0:T(8,128)(2,1)S(1)} %get-tuple-element.18.refs_0_), channel_id=1, source_target_pairs={{0,3},{1,0},{2,1},{3,2},{4,7},{5,4},{6,5},{7,6},{8,11},{9,8},{10,9... | collective-permute-start | bytes 196616 | tf_op jit(solution)/shard_map/ppermute | solution.py:235
  5.1 5.8 %collective-permute-start.7 = (bf16[32,1024]{1,0:T(8,128)(2,1)S(1)}, bf16[32,1024]{1,0:T(8,128)(2,1)S(1)}, u32[]{:S(2)}, u32[]{:S(2)}) collective-permute-start(bf16[32,1024]{1,0:T(8,128)(2,1)S(1)} %get-tuple-element.18.refs_0_), channel_id=1, source_target_pairs={{0,2},{1,3},{2,0},{3,1},{4,6},{5,7},{6,4},{7,5},{8,10},{9,11},{10,... | collective-permute-start | bytes 196616 | tf_op jit(solution)/shard_map/ppermute | solution.py:235
  5.9 5.7 %collective-permute-start.6 = (bf16[32,1024]{1,0:T(8,128)(2,1)S(1)}, bf16[32,1024]{1,0:T(8,128)(2,1)S(1)}, u32[]{:S(2)}, u32[]{:S(2)}) collective-permute-start(bf16[32,1024]{1,0:T(8,128)(2,1)S(1)} %get-tuple-element.18.refs_0_), channel_id=1, source_target_pairs={{0,1},{1,2},{2,3},{3,0},{4,5},{5,6},{6,7},{7,4},{8,9},{9,10},{10,1... | collective-permute-start | bytes 196616 | tf_op jit(solution)/shard_map/ppermute | solution.py:235
  12.3 54.4 %collective-permute-start.11 = (bf16[128,1024]{1,0:T(8,128)(2,1)}, bf16[128,1024]{1,0:T(8,128)(2,1)S(1)}, u32[]{:S(2)}, u32[]{:S(2)}) collective-permute-start(bf16[128,1024]{1,0:T(8,128)(2,1)} %shard_map.66.refs_0_), channel_id=1, source_target_pairs={{0,192},{4,196},{8,200},{12,204},{16,208},{20,212},{24,216},{28,22... | collective-permute-start | bytes 786440 | tf_op jit(solution)/shard_map/ppermute | solution.py:300
  15.4 54.6 %collective-permute-start.10 = (bf16[128,1024]{1,0:T(8,128)(2,1)}, bf16[128,1024]{1,0:T(8,128)(2,1)S(1)}, u32[]{:S(2)}, u32[]{:S(2)}) collective-permute-start(bf16[128,1024]{1,0:T(8,128)(2,1)} %shard_map.66.refs_0_), channel_id=1, source_target_pairs={{0,128},{4,132},{8,136},{12,140},{16,144},{20,148},{24,152},{28,15... | collective-permute-start | bytes 786440 | tf_op jit(solution)/shard_map/ppermute | solution.py:300
  16.0 53.9 %collective-permute-start.9 = (bf16[128,1024]{1,0:T(8,128)(2,1)}, bf16[128,1024]{1,0:T(8,128)(2,1)S(1)}, u32[]{:S(2)}, u32[]{:S(2)}) collective-permute-start(bf16[128,1024]{1,0:T(8,128)(2,1)} %shard_map.66.refs_0_), channel_id=1, source_target_pairs={{0,64},{4,68},{8,72},{12,76},{16,80},{20,84},{24,88},{28,92},{32,9... | collective-permute-start | bytes 786440 | tf_op jit(solution)/shard_map/ppermute | solution.py:300
  17.0 53.0 %copy-start = (bf16[128,1024]{1,0:T(8,128)(2,1)S(1)}, bf16[128,1024]{1,0:T(8,128)(2,1)}, u32[]{:S(2)}) copy-start(bf16[128,1024]{1,0:T(8,128)(2,1)} %shard_map.66.refs_0_) | copy-start | bytes 786436
  49.9 21.2 %copy-start.2 = (f32[256]{0:T(256)S(1)}, f32[256]{0:T(256)}, u32[]{:S(2)}) copy-start(f32[256]{0:T(256)} %param.9) | copy-start | bytes 3076
  49.9 21.2 %copy-start.3 = (f32[256]{0:T(256)S(1)}, f32[256]{0:T(256)}, u32[]{:S(2)}) copy-start(f32[256]{0:T(256)} %param.10) | copy-start | bytes 3076
  49.9 50.4 %collective-permute-start.1 = (bf16[2048,256]{1,0:T(8,128)(2,1)}, bf16[2048,256]{1,0:T(8,128)(2,1)}, u32[]{:S(2)}, u32[]{:S(2)}) collective-permute-start(bf16[2048,256]{1,0:T(8,128)(2,1)} %shard_map.65), channel_id=1, source_target_pairs={{0,2},{1,3},{2,0},{3,1},{4,6},{5,7},{6,4},{7,5},{8,10},{9,11},{10,... | collective-permute-start | bytes 3145736 | tf_op jit(solution)/shard_map/ppermute | solution.py:235
  51.3 51.6 %collective-permute-start = (bf16[2048,256]{1,0:T(8,128)(2,1)S(1)}, bf16[2048,256]{1,0:T(8,128)(2,1)}, u32[]{:S(2)}, u32[]{:S(2)}) collective-permute-start(bf16[2048,256]{1,0:T(8,128)(2,1)S(1)} %get-tuple-element.12), channel_id=1, source_target_pairs={{0,1},{1,2},{2,3},{3,0},{4,5},{5,6},{6,7},{7,4},{8,9},{9,10},{10,1... | collective-permute-start | bytes 3145736 | tf_op jit(solution)/shard_map/ppermute | solution.py:235
  55.9 22.6 %all-to-all-start = ((bf16[64,16,128]{2,1,0:T(8,128)(2,1)}), bf16[64,16,128]{2,1,0:T(8,128)(2,1)S(1)}, u32[]{:S(2)}, u32[]{:S(2)}) async-start(bf16[64,16,128]{2,1,0:T(8,128)(2,1)} %bitcast.10), calls=%async_computation | async-start | bytes 524288 | tf_op jit(solution)/shard_map/all_to_all | solution.py:330
  66.7 36.5 %collective-permute-start.2 = (bf16[2048,256]{1,0:T(8,128)(2,1)S(1)}, bf16[2048,256]{1,0:T(8,128)(2,1)}, u32[]{:S(2)}, u32[]{:S(2)}) collective-permute-start(bf16[2048,256]{1,0:T(8,128)(2,1)S(1)} %get-tuple-element.13), channel_id=1, source_target_pairs={{0,3},{1,0},{2,1},{3,2},{4,7},{5,4},{6,5},{7,6},{8,11},{9,8},{10,9... | collective-permute-start | bytes 3145736 | tf_op jit(solution)/shard_map/ppermute | solution.py:235
  71.0 35.7 %collective-permute-start.12 = (bf16[512,1024]{1,0:T(8,128)(2,1)}, bf16[512,1024]{1,0:T(8,128)(2,1)}, u32[]{:S(2)}, u32[]{:S(2)}) collective-permute-start(bf16[512,1024]{1,0:T(8,128)(2,1)} %shard_map.67.refs_9_), channel_id=1, source_target_pairs={{0,4},{4,0},{8,12},{12,8},{16,20},{20,16},{24,28},{28,24},{32,36},... | collective-permute-start | bytes 3145736 | tf_op jit(solution)/shard_map/ppermute | solution.py:364
  79.8 18.0 %all-to-all-start.1 = ((bf16[64,16,128]{2,1,0:T(8,128)(2,1)}), bf16[64,16,128]{2,1,0:T(8,128)(2,1)S(1)}, u32[]{:S(2)}, u32[]{:S(2)}) async-start(bf16[64,16,128]{2,1,0:T(8,128)(2,1)} %bitcast.14), calls=%async_computation.1 | async-start | bytes 524288 | tf_op jit(solution)/shard_map/all_to_all | solution.py:330
  98.2 5.1 %collective-permute-start.3 = (bf16[16,768]{1,0:T(8,128)(2,1)S(1)}, bf16[16,768]{1,0:T(8,128)(2,1)S(1)}, u32[]{:S(2)}, u32[]{:S(2)}) collective-permute-start(bf16[16,768]{1,0:T(8,128)(2,1)S(1)} %get-tuple-element.15), channel_id=1, source_target_pairs={{0,1},{1,2},{2,3},{3,0},{4,5},{5,6},{6,7},{7,4},{8,9},{9,10},{10,1... | collective-permute-start | bytes 73736 | tf_op jit(solution)/shard_map/ppermute | solution.py:235
  100.3 5.3 %collective-permute-start.4 = (bf16[16,768]{1,0:T(8,128)(2,1)S(1)}, bf16[16,768]{1,0:T(8,128)(2,1)S(1)}, u32[]{:S(2)}, u32[]{:S(2)}) collective-permute-start(bf16[16,768]{1,0:T(8,128)(2,1)S(1)} %get-tuple-element.16), channel_id=1, source_target_pairs={{0,2},{1,3},{2,0},{3,1},{4,6},{5,7},{6,4},{7,5},{8,10},{9,11},{10,... | collective-permute-start | bytes 73736 | tf_op jit(solution)/shard_map/ppermute | solution.py:235
  102.9 3.8 %collective-permute-start.5 = (bf16[16,768]{1,0:T(8,128)(2,1)S(1)}, bf16[16,768]{1,0:T(8,128)(2,1)S(1)}, u32[]{:S(2)}, u32[]{:S(2)}) collective-permute-start(bf16[16,768]{1,0:T(8,128)(2,1)S(1)} %get-tuple-element.17), channel_id=1, source_target_pairs={{0,3},{1,0},{2,1},{3,2},{4,7},{5,4},{6,5},{7,6},{8,11},{9,8},{10,9... | collective-permute-start | bytes 73736 | tf_op jit(solution)/shard_map/ppermute | solution.py:235

commit v4 on v3

--- a/solution.py
+++ b/solution.py
@@ -44,28 +44,67 @@
     return jnp.concatenate([scratch[pl.ds(at + n, peers, stride=MSG), :] for n in range(count)], axis=1)
 
 
-def cut_kernel(start, *refs, count, rows):
-    sources, outs, sems = refs[:count], refs[count : 2 * count], refs[2 * count]
-    copies = [
-        pltpu.make_async_copy(sources[n].at[pl.ds(pl.multiple_of(start[n], rows[n]), rows[n]), :], outs[n], sems.at[n])
-        for n in range(count)
-    ]
+def run(copies):
     for copy in copies:
         copy.start()
     for copy in copies:
         copy.wait()
 
 
+def row_copies(starts, sources, outs, sems, rows):
+    return [
+        pltpu.make_async_copy(source.at[pl.ds(pl.multiple_of(start, rows), rows), :], out, sems.at[n])
+        for n, (start, source, out) in enumerate(zip(starts, sources, outs))
+    ]
+
+
+def cut_kernel(info, source, out, sems, *, rows, start):
+    run(row_copies([start(info)], [source], [out], sems, rows))
+
+
+def cut13_kernel(info, values, *refs, rows, blocks, pieces):
+    outs, held_rows, sems_in, sems_out = refs[:2], refs[2], refs[3], refs[4]
+    size = rows // pieces
+    inward, outward = [], []
+    for q, d in enumerate((1, 3)):
+        for p in range(pieces):
+            n = q * pieces + p
+            at = pl.multiple_of(lax.rem(info[0] + d, blocks) * rows + p * size, size)
+            inward.append(pltpu.make_async_copy(values.at[pl.ds(at, size), :], held_rows.at[n], sems_in.at[n]))
+            outward.append(pltpu.make_async_copy(held_rows.at[n], outs[q].at[pl.ds(p * size, size), :], sems_out.at[n]))
+    for copy in inward:
+        copy.start()
+    for copy, onward in zip(inward, outward):
+        copy.wait()
+        onward.start()
+    for onward in outward:
+        onward.wait()
+
+
 def stack_kernel(*refs):
     parts, out, sems = refs[:-2], refs[-2], refs[-1]
     rows = parts[0].shape[0]
-    copies = [
-        pltpu.make_async_copy(part, out.at[n * rows : (n + 1) * rows, :], sems.at[n]) for n, part in enumerate(parts)
-    ]
-    for copy in copies:
-        copy.start()
-    for copy in copies:
-        copy.wait()
+    run(
+        [
+            pltpu.make_async_copy(part, out.at[n * rows : (n + 1) * rows, :], sems.at[n])
+            for n, part in enumerate(parts)
+        ]
+    )
+
+
+def assemble_kernel(info, *refs, blocks, slabs, cols):
+    parts, out, sems = refs[: 2 * slabs], refs[-2], refs[-1]
+    slab = parts[0].shape[0] // blocks
+    copies = []
+    for e in range(slabs):
+        first = lax.rem(info[1] + slabs - e, slabs) * 2
+        for c in range(2):
+            number = first + (info[2] if c == 0 else 1 - info[2])
+            for n in range(blocks):
+                at = pl.multiple_of(n * cols + number * slab, slab)
+                source = parts[2 * e + c].at[pl.ds(n * slab, slab), :]
+                copies.append(pltpu.make_async_copy(source, out.at[pl.ds(at, slab), :], sems.at[len(copies)]))
+    run(copies)
 
 
 def stats_kernel(values, owner, sub, out, first, second, scratch, *, tiles, peers):
@@ -169,11 +208,11 @@
     out[...] = scratch[...].astype(BF16)
 
 
-def tile_kernel(first, arrived, owner, *refs, tiles, peers, blocks):
+def tile_kernel(info, arrived, owner, *refs, tiles, peers, blocks):
     outs, scratch = refs[:-1], refs[-1]
     scratch[...] = arrived[...].astype(F32)
     owner_row = owner[...].astype(F32)
-    at = (iota((tiles, tiles), 0) + first[0]) % tiles
+    at = (iota((tiles, tiles), 0) + info[0] * (tiles // blocks)) % tiles
     place = as_column(places(owner_row), tiles, at)
     named = as_column(owner_row, tiles, at) == iota((tiles, peers), 1).astype(F32)
     hot = jnp.concatenate([jnp.where(named & (place == float(slot)), 1.0, 0.0) for slot in range(2)], axis=1)
@@ -184,39 +223,16 @@
         out[...] = picked[n * each : (n + 1) * each, :].astype(BF16)
 
 
-def project_kernel(place, *refs, blocks, tile_rows, slabs):
-    moved, coeffs = refs[:blocks], refs[blocks : 2 * blocks]
-    near, far, out, wide, weight, sems = refs[2 * blocks :]
+def project_kernel(info, *refs, blocks, tile_rows):
+    moved, coeffs, (weight, out, wide) = refs[:blocks], refs[blocks : 2 * blocks], refs[2 * blocks :]
     step = pl.program_id(0)
     rows, cols = moved[0].shape
     tiles = rows // tile_rows
-    slab = near.shape[0] // (slabs * blocks)
-
-    def weight_copies():
-        copies = []
-        for e in range(slabs):
-            first = lax.rem(place[1] + slabs - e, slabs) * 2
-            for n in range(blocks):
-                for which, (source, core) in enumerate(((near, place[2]), (far, 1 - place[2]))):
-                    at = pl.multiple_of(n * cols + (first + core) * slab, slab)
-                    copies.append(
-                        pltpu.make_async_copy(
-                            source.at[pl.ds((e * blocks + n) * slab, slab), :],
-                            weight.at[pl.ds(at, slab), :],
-                            sems.at[(e * blocks + n) * 2 + which],
-                        )
-                    )
-        return copies
 
     @pl.when(step == 0)
     def _():
-        copies = weight_copies()
-        for copy in copies:
-            copy.start()
         for n in range(blocks):
             wide[n] = coeffs[n][...].astype(F32)
-        for copy in copies:
-            copy.wait()
 
     strips = []
     for t in range(tiles):
@@ -256,28 +272,30 @@
     return pltpu.with_memory_space_constraint(value, pltpu.HBM)
 
 
-def cut(start, sources, rows, on_chip_from=0):
-    kept = [pltpu.HBM] * on_chip_from + [pltpu.VMEM] * (len(sources) - on_chip_from)
+IN_ANY = pl.BlockSpec(memory_space=pl.ANY)
+
+
+def cut(info, source, rows, start):
     return pl.pallas_call(
-        lambda *refs: cut_kernel(*refs, count=len(sources), rows=rows),
-        in_specs=[IN_SMEM] + [IN_HBM] * len(sources),
-        out_specs=[pl.BlockSpec(memory_space=k) for k in kept],
-        out_shape=[k((r, s.shape[1]), s.dtype) for k, r, s in zip(kept, rows, sources)],
-        scratch_shapes=[pltpu.SemaphoreType.DMA((len(sources),))],
-        compiler_params=limit(6),
-    )(start, *[off_chip(source) for source in sources])
+        lambda *refs: cut_kernel(*refs, rows=rows, start=start),
+        in_specs=[IN_SMEM, IN_HBM],
+        out_specs=IN_VMEM,
+        out_shape=pltpu.VMEM((rows, source.shape[1]), source.dtype),
+        scratch_shapes=[pltpu.SemaphoreType.DMA((1,))],
+        compiler_params=limit(2),
+    )(info, off_chip(source))
 
 
 def stacked(parts):
     rows, cols = parts[0].shape
     return pl.pallas_call(
         stack_kernel,
-        in_specs=[pl.BlockSpec(memory_space=pl.ANY)] * len(parts),
-        out_specs=IN_HBM,
-        out_shape=pltpu.HBM((len(parts) * rows, cols), parts[0].dtype),
+        in_specs=[IN_VMEM] * len(parts),
+        out_specs=IN_VMEM,
+        out_shape=pltpu.VMEM((len(parts) * rows, cols), parts[0].dtype),
         scratch_shapes=[pltpu.SemaphoreType.DMA((len(parts),))],
-        compiler_params=limit(6),
-    )(*parts)
+        compiler_params=limit(2),
+    )(*[held(part) for part in parts])
 
 
 def on_device(values, subgroup, owners, col_gain, col_bias, out_weight):
@@ -290,20 +308,16 @@
     outputs = out_weight.shape[1]
     owner_row, sub_row = owners.reshape(1, tiles), subgroup.reshape(1, tiles)
 
-    slabs = 4
-    depth = peers // (2 * slabs)
-    slab_at, core = index // (2 * depth), index % 2
+    slabs = 2
+    depth = max(1, peers // 8)
+    info = jnp.stack([rank, (index // (2 * depth)) % slabs, index % 2])
     slab = cols // (2 * slabs)
 
-    def along_slabs(value, e):
-        pairs = [(i, (i + e * 2 * depth) % peers) for i in range(peers)]
-        return lax.ppermute(value, "shuf", pairs)
-
-    def quarter(d):
-        return ((rank + d) % blocks) * own_rows
+    def trade(value, distance):
+        return lax.ppermute(value, "shuf", [(i, i ^ distance) for i in range(peers)])
 
     moved = {}
-    (two,) = cut(quarter(2).reshape(1), [values], [own_rows], 1)
+    two = cut(info, values, own_rows, lambda ref: lax.rem(ref[0] + 2, blocks) * own_rows)
     moved[2] = hop(two, "rep", 2)
 
     steps = 4
@@ -332,11 +346,24 @@
 
     arrived = exchange(outgoing)
 
-    start = jnp.stack([(slab_at * 2 + core) * slab, quarter(1), quarter(3)])
-    own_slab, one, three = cut(start, [out_weight, values, values], [slab, own_rows, own_rows])
+    own_slab = cut(info, out_weight, slab, lambda ref: (ref[1] * 2 + ref[2]) * slab)
     slab_parts = [own_slab]
     for d in range(1, blocks):
         slab_parts.append(hop(own_slab, "rep", d))
+    pieces = 4
+    one, three = pl.pallas_call(
+        lambda *refs: cut13_kernel(*refs, rows=own_rows, blocks=blocks, pieces=pieces),
+        in_specs=[IN_SMEM, IN_HBM],
+        out_specs=[IN_HBM] * 2,
+        out_shape=[pltpu.HBM((own_rows, cols), BF16)] * 2,
+        scratch_shapes=[
+            pltpu.VMEM((2 * pieces, own_rows // pieces, cols), BF16),
+            pltpu.SemaphoreType.DMA((2 * pieces,)),
+            pltpu.SemaphoreType.DMA((2 * pieces,)),
+        ],
+        compiler_params=limit(4),
+        name="cut13",
+    )(info, off_chip(values))
     moved[1] = hop(one, "rep", 1)
     moved[3] = hop(three, "rep", 3)
 
@@ -356,12 +383,19 @@
     )(arrived, both)
     returned = exchange(answer)
 
-    one_slab = stacked(slab_parts)
-    across = [one_slab]
-    for e in range(1, slabs):
-        across.append(along_slabs(one_slab, e))
-    near = stacked(across)
-    far = lax.ppermute(near, "shuf", [(i, i ^ 1) for i in range(peers)])
+    parts = [stacked(slab_parts)]
+    parts.append(trade(parts[0], 1))
+    parts.append(trade(parts[0], 2 * depth))
+    parts.append(trade(parts[2], 1))
+    weight = pl.pallas_call(
+        lambda *refs: assemble_kernel(*refs, blocks=blocks, slabs=slabs, cols=cols),
+        in_specs=[IN_SMEM] + [IN_ANY] * len(parts),
+        out_specs=IN_VMEM,
+        out_shape=pltpu.VMEM((blocks * cols, outputs), BF16),
+        scratch_shapes=[pltpu.SemaphoreType.DMA((2 * slabs * blocks,))],
+        compiler_params=limit(2),
+        name="assemble",
+    )(info, *parts)
 
     each = tiles // blocks
     coeffs = pl.pallas_call(
@@ -372,39 +406,32 @@
         scratch_shapes=[pltpu.VMEM((peers * MSG, LANES), F32)],
         compiler_params=limit(4),
         name="pick",
-    )((rank * each).reshape(1), returned, owner_row)
+    )(info, returned, owner_row)
     known = {0: coeffs[0]}
     for d in (2, 1, 3):
         known[d] = hop(coeffs[d], "rep", d)
 
     block = min(512, own_rows)
-    blocked = pl.BlockSpec((block, cols), lambda i, place: (i, 0))
     return pl.pallas_call(
-        lambda *refs: project_kernel(*refs, blocks=blocks, tile_rows=tile_rows, slabs=slabs),
+        lambda *refs: project_kernel(*refs, blocks=blocks, tile_rows=tile_rows),
         grid_spec=pltpu.PrefetchScalarGridSpec(
             num_scalar_prefetch=1,
             grid=(own_rows // block,),
-            in_specs=[pl.BlockSpec((block, cols), lambda i, place: (place[0] * (own_rows // block) + i, 0))]
-            + [blocked] * (blocks - 1)
-            + [IN_VMEM] * blocks
-            + [IN_HBM] * 2,
-            out_specs=pl.BlockSpec((block, outputs), lambda i, place: (i, 0)),
-            scratch_shapes=[
-                pltpu.VMEM((blocks, each, 3 * cols), F32),
-                pltpu.VMEM((blocks * cols, outputs), BF16),
-                pltpu.SemaphoreType.DMA((2 * slabs * blocks,)),
-            ],
+            in_specs=[pl.BlockSpec((block, cols), lambda i, info: (info[0] * (own_rows // block) + i, 0))]
+            + [pl.BlockSpec((block, cols), lambda i, info: (i, 0))] * (blocks - 1)
+            + [IN_VMEM] * (blocks + 1),
+            out_specs=pl.BlockSpec((block, outputs), lambda i, info: (i, 0)),
+            scratch_shapes=[pltpu.VMEM((blocks, each, 3 * cols), F32)],
         ),
         out_shape=jax.ShapeDtypeStruct((own_rows, outputs), BF16),
         compiler_params=limit(24),
         name="project",
     )(
-        jnp.stack([rank, slab_at, core]),
+        info,
         off_chip(values),
         *[off_chip(moved[d]) for d in range(1, blocks)],
         *[held(known[d]) for d in range(blocks)],
-        off_chip(near),
-        off_chip(far),
+        held(weight),
     )
 
 

time: 117 us -> 100 us (0.85)
  Pallas kernels: 52.9 us -> 24.6 us
  blocking collectives: 0 us -> 17.8 us
  starting transfers between devices: 36.1 us -> 29.1 us
    pallas_call x4 -> x5, Pallas kernels: 36.7 us -> 10.3 us  [the longest x1 3.43 us: on_device(): pl.pallas_call(lambda *refs: assemble_kernel(*refs, blocks=blocks, slabs=...]
    all_to_all x0 -> x1, blocking collectives: none -> 17.8 us  [exchange(): lax.all_to_all(message.reshape(peers, MSG, LANES), 'shuf', 0, 0, tiled=True)]
    ppermute x9, waiting for transfers between devices: 8.3 us -> 23 us  [hop(): lax.ppermute(value, axis, [(i, (i + distance) % size) for i in range(size)])]
    all_to_all x2 -> x1, waiting for transfers between devices: 19 us -> 4.41 us  [exchange(): lax.all_to_all(message.reshape(peers, MSG, LANES), 'shuf', 0, 0, tiled=True)]
    all_to_all x2 -> x1, starting transfers between devices: 17.1 us -> 11.5 us  [exchange(): lax.all_to_all(message.reshape(peers, MSG, LANES), 'shuf', 0, 0, tiled=True)]
    ppermute x4 -> x3, starting transfers between devices: 4.78 us -> 2.17 us  [trade(): lax.ppermute(value, 'shuf', [(i, i ^ distance) for i in range(peers)])]
    pallas_call x1, Pallas kernels: 9.95 us -> 8.21 us  [on_device(): pl.pallas_call(lambda *refs: project_kernel(*refs, blocks=blocks, tile_ro...]
    ppermute x9, starting transfers between devices: 14.2 us -> 15.5 us  [hop(): lax.ppermute(value, axis, [(i, (i + distance) % size) for i in range(size)])]
  transfers between devices with their start and end apart: 15 -> 13, of which waited for: 8 -> 3; matrix products, arithmetic and copies ran while one was open for 0% -> 0% of each run, Pallas kernels for 34% -> 15%
where the time goes in v4:
time: 100 us; the launch traced here: 99.2 us
  starting transfers between devices  29.1 us (29%)
  waiting for transfers between devices  27.4 us (27%)
  Pallas kernels  24.6 us (25%)
  blocking collectives  17.8 us (18%)
    ppermute x9, waiting for transfers between devices, hop(): lax.ppermute(value, axis, [(i, (i + distance) % size) for i in range(size)])  23 us
    all_to_all x1, blocking collectives, exchange(): lax.all_to_all(message.reshape(peers, MSG, LANES), 'shuf', 0, 0, tiled=True)  17.8 us
    ppermute x9, starting transfers between devices, hop(): lax.ppermute(value, axis, [(i, (i + distance) % size) for i in range(size)])  15.5 us
    all_to_all x1, starting transfers between devices, exchange(): lax.all_to_all(message.reshape(peers, MSG, LANES), 'shuf', 0, 0, tiled=True)  11.5 us
    pallas_call x1, Pallas kernels, on_device(): pl.pallas_call(lambda *refs: project_kernel(*refs, blocks=blocks, tile_ro...  8.21 us
    pallas_call x1, Pallas kernels, on_device(): pl.pallas_call(lambda *refs: stats_kernel(*refs, tiles=tiles, peers=peers...  4.51 us
    all_to_all x1, waiting for transfers between devices, exchange(): lax.all_to_all(message.reshape(peers, MSG, LANES), 'shuf', 0, 0, tiled=True)  4.41 us
    pallas_call x1, Pallas kernels, on_device(): pl.pallas_call(lambda *refs: assemble_kernel(*refs, blocks=blocks, slabs=...  3.43 us
  transfers between devices with their start and end apart: 13, of which 3 were waited for; matrix products, arithmetic and copies ran while one was open for 0% of the time, Pallas kernels for 15%

profile of v4, /device:TPU:32, one launch (start us, length us, event | category | flops | bytes accessed | tf_op | source)
XLA Modules:
  0.0 99.2 jit_solution(15046834561221385370)
XLA Ops:
  0.0 0.1 pad_add_fusion.refs_0_
  0.1 1.5 %shard_map.65.refs_0_ = bf16[64,1024]{1,0:T(8,128)(2,1)S(1)} custom-call(s32[3]{0:T(128)S(1)} %pad_add_fusion.refs_0_, bf16[256,1024]{1,0:T(8,128)(2,1)} %refs_1_.6), custom_call_target="tpu_custom_call" | custom-call | tf_op jit(solution)/shard_map/pallas_call | solution.py:279
  1.5 2.8 %collective-permute-start.8 = (bf16[64,1024]{1,0:T(8,128)(2,1)S(1)}, bf16[64,1024]{1,0:T(8,128)(2,1)S(1)}, u32[]{:S(2)}, u32[]{:S(2)}) collective-permute-start(bf16[64,1024]{1,0:T(8,128)(2,1)S(1)} %shard_map.65.refs_0_), channel_id=1, source_target_pairs={{0,3},{1,0},{2,1},{3,2},{4,7},{5,4},{6,5},{7,6},{8,11},{9,8},{10,9... | collective-permute-start | bytes 393224 | tf_op jit(solution)/shard_map/ppermute | solution.py:251
  4.4 0.8 collective-permute-start.7
  5.2 0.9 collective-permute-start.6
  6.1 1.8 %shard_map.64 = bf16[2048,256]{1,0:T(8,128)(2,1)S(1)} custom-call(s32[3]{0:T(128)S(1)} %pad_add_fusion.refs_0_, bf16[8192,256]{1,0:T(8,128)(2,1)} %refs_1_.7), custom_call_target="tpu_custom_call" | custom-call | tf_op jit(solution)/shard_map/pallas_call | solution.py:279
  7.9 1.9 %collective-permute-start.1 = (bf16[2048,256]{1,0:T(8,128)(2,1)S(1)}, bf16[2048,256]{1,0:T(8,128)(2,1)}, u32[]{:S(2)}, u32[]{:S(2)}) collective-permute-start(bf16[2048,256]{1,0:T(8,128)(2,1)S(1)} %shard_map.64), channel_id=1, source_target_pairs={{0,2},{1,3},{2,0},{3,1},{4,6},{5,7},{6,4},{7,5},{8,10},{9,11},{10,... | collective-permute-start | bytes 3145736 | tf_op jit(solution)/shard_map/ppermute | solution.py:251
  9.8 22.7 %collective-permute-done.8.refs_3_ = bf16[64,1024]{1,0:T(8,128)(2,1)S(1)} collective-permute-done((bf16[64,1024]{1,0:T(8,128)(2,1)S(1)}, bf16[64,1024]{1,0:T(8,128)(2,1)S(1)}, u32[]{:S(2)}, u32[]{:S(2)}) %collective-permute-start.8) | collective-permute-done | bytes 131104 | tf_op jit(solution)/shard_map/ppermute | solution.py:251
  32.5 0.0 collective-permute-done.7.refs_2_
  32.5 0.0 collective-permute-done.6.refs_1_
  32.5 0.7 shard_map.66.refs_1_
  33.2 1.7 %collective-permute-start.10 = (bf16[256,1024]{1,0:T(8,128)(2,1)S(1)}, bf16[256,1024]{1,0:T(8,128)(2,1)S(1)}, u32[]{:S(2)}, u32[]{:S(2)}) collective-permute-start(bf16[256,1024]{1,0:T(8,128)(2,1)S(1)} %shard_map.66.refs_1_), channel_id=1, source_target_pairs={{0,64},{4,68},{8,72},{12,76},{16,80},{20,84},{24,88},{28,92},{32,9... | collective-permute-start | bytes 1572872 | tf_op jit(solution)/shard_map/ppermute | solution.py:317
  34.9 4.5 %stats.1 = bf16[1024,128]{1,0:T(8,128)(2,1)} custom-call(bf16[8192,256]{1,0:T(8,128)(2,1)} %refs_1_.7, s32[1,64]{1,0:T(1,128)S(1)} %bitcast.14, s32[1,64]{1,0:T(1,128)S(1)} %bitcast.18), custom_call_target="tpu_custom_call" | custom-call | tf_op jit(solution)/shard_map/stats/pallas_call | solution.py:324
  39.4 11.5 %all-to-all-start = ((bf16[64,16,128]{2,1,0:T(8,128)(2,1)}), bf16[64,16,128]{2,1,0:T(8,128)(2,1)S(1)}, u32[]{:S(2)}, u32[]{:S(2)}) async-start(bf16[64,16,128]{2,1,0:T(8,128)(2,1)} %bitcast.5), calls=%async_computation | async-start | bytes 524288 | tf_op jit(solution)/shard_map/all_to_all | solution.py:344
  50.8 2.9 %cut13.1 = (bf16[2048,256]{1,0:T(8,128)(2,1)}, bf16[2048,256]{1,0:T(8,128)(2,1)}) custom-call(s32[3]{0:T(128)S(1)} %pad_add_fusion.refs_0_, bf16[8192,256]{1,0:T(8,128)(2,1)} %refs_1_.7), custom_call_target="tpu_custom_call" | custom-call | tf_op jit(solution)/shard_map/cut13/pallas_call | solution.py:354
  53.8 0.1 collective-permute-start
  53.9 3.7 %collective-permute-start.2 = (bf16[2048,256]{1,0:T(8,128)(2,1)}, bf16[2048,256]{1,0:T(8,128)(2,1)}, u32[]{:S(2)}, u32[]{:S(2)}) collective-permute-start(bf16[2048,256]{1,0:T(8,128)(2,1)} %get-tuple-element.12), channel_id=1, source_target_pairs={{0,3},{1,0},{2,1},{3,2},{4,7},{5,4},{6,5},{7,6},{8,11},{9,8},{10,9... | collective-permute-start | bytes 3145736 | tf_op jit(solution)/shard_map/ppermute | solution.py:251
  57.6 0.0 collective-permute-start.9
  57.6 0.0 collective-permute-done.10.refs_3_
  57.6 0.5 collective-permute-start.11
  58.1 4.4 %all-to-all-done = bf16[64,16,128]{2,1,0:T(8,128)(2,1)S(1)} async-done(((bf16[64,16,128]{2,1,0:T(8,128)(2,1)}), bf16[64,16,128]{2,1,0:T(8,128)(2,1)S(1)}, u32[]{:S(2)}, u32[]{:S(2)}) %all-to-all-start) | async-done | bytes 262176 | tf_op jit(solution)/shard_map/all_to_all | solution.py:344
  62.6 0.6 moments.1
  63.2 17.8 %all_to_all.10 = bf16[64,16,128]{2,1,0:T(8,128)(2,1)S(1)} all-to-all(bf16[64,16,128]{2,1,0:T(8,128)(2,1)S(1)} %bitcast.13), channel_id=1, replica_groups=mesh['shuf'=64,'rep'=4] {'shuf'}, dimensions={0} | all-to-all | bytes 524288 | tf_op jit(solution)/shard_map/all_to_all | solution.py:344
  81.0 0.9 pick.1
  82.0 0.0 collective-permute-done.9.refs_2_
  82.0 0.1 collective-permute-start.3
  82.1 0.0 collective-permute-done.1.refs_3_
  82.1 5.1 %collective-permute-start.4 = (bf16[16,768]{1,0:T(8,128)(2,1)S(1)}, bf16[16,768]{1,0:T(8,128)(2,1)S(1)}, u32[]{:S(2)}, u32[]{:S(2)}) collective-permute-start(bf16[16,768]{1,0:T(8,128)(2,1)S(1)} %get-tuple-element.15), channel_id=1, source_target_pairs={{0,2},{1,3},{2,0},{3,1},{4,6},{5,7},{6,4},{7,5},{8,10},{9,11},{10,... | collective-permute-start | bytes 73736 | tf_op jit(solution)/shard_map/ppermute | solution.py:251
  87.2 0.0 collective-permute-start.5
  87.2 3.4 %assemble.1.refs_9_ = bf16[1024,1024]{1,0:T(8,128)(2,1)S(1)} custom-call(s32[3]{0:T(128)S(1)} %pad_add_fusion.refs_0_, bf16[256,1024]{1,0:T(8,128)(2,1)S(1)} %shard_map.66.refs_1_, bf16[256,1024]{1,0:T(8,128)(2,1)S(1)} %collective-permute-done.9.refs_2_, bf16[256,1024]{1,0:T(8,128)(2,1)S(1)} %collective-permute-done.10.refs_3_, ...), custom_call_target="tpu_custom_call" | custom-call | tf_op jit(solution)/shard_map/assemble/pallas_call | solution.py:390
  90.7 0.3 collective-permute-done.5.refs_8_
  91.0 8.2 %project.1 = bf16[2048,1024]{1,0:T(8,128)(2,1)} custom-call(s32[3]{0:T(128)S(1)} %pad_add_fusion.refs_0_, bf16[8192,256]{1,0:T(8,128)(2,1)} %refs_1_.7, bf16[2048,256]{1,0:T(8,128)(2,1)} %collective-permute-done.refs_2_, bf16[2048,256]{1,0:T(8,128)(2,1)} %collective-permute-done.1.refs_3_, bf16[2048,256]{1,0:T(8,128)(2,1)} %collective-permute-done.2.refs_4_, ...), custom_call_target="tpu_custom_call" | custom-call | tf_op jit(solution)/shard_map/project/pallas_call | solution.py:415
  (14 shorter events, 0.0 us)
Async XLA Ops:
  0.0 34.8 %copy-start = (s32[64,1]{0,1:T(1,128)S(1)}, s32[64,1]{0,1:T(1,128)}, u32[]{:S(2)}) copy-start(s32[64,1]{0,1:T(1,128)} %param.8) | copy-start | bytes 772
  0.0 34.8 %copy-start.3 = (s32[64]{0:T(128)S(1)}, s32[64]{0:T(128)}, u32[]{:S(2)}) copy-start(s32[64]{0:T(128)} %param.7) | copy-start | bytes 772
  1.5 30.9 %collective-permute-start.8 = (bf16[64,1024]{1,0:T(8,128)(2,1)S(1)}, bf16[64,1024]{1,0:T(8,128)(2,1)S(1)}, u32[]{:S(2)}, u32[]{:S(2)}) collective-permute-start(bf16[64,1024]{1,0:T(8,128)(2,1)S(1)} %shard_map.65.refs_0_), channel_id=1, source_target_pairs={{0,3},{1,0},{2,1},{3,2},{4,7},{5,4},{6,5},{7,6},{8,11},{9,8},{10,9... | collective-permute-start | bytes 393224 | tf_op jit(solution)/shard_map/ppermute | solution.py:251
  4.4 28.1 %collective-permute-start.7 = (bf16[64,1024]{1,0:T(8,128)(2,1)S(1)}, bf16[64,1024]{1,0:T(8,128)(2,1)S(1)}, u32[]{:S(2)}, u32[]{:S(2)}) collective-permute-start(bf16[64,1024]{1,0:T(8,128)(2,1)S(1)} %shard_map.65.refs_0_), channel_id=1, source_target_pairs={{0,2},{1,3},{2,0},{3,1},{4,6},{5,7},{6,4},{7,5},{8,10},{9,11},{10,... | collective-permute-start | bytes 393224 | tf_op jit(solution)/shard_map/ppermute | solution.py:251
  5.2 27.3 %collective-permute-start.6 = (bf16[64,1024]{1,0:T(8,128)(2,1)S(1)}, bf16[64,1024]{1,0:T(8,128)(2,1)S(1)}, u32[]{:S(2)}, u32[]{:S(2)}) collective-permute-start(bf16[64,1024]{1,0:T(8,128)(2,1)S(1)} %shard_map.65.refs_0_), channel_id=1, source_target_pairs={{0,1},{1,2},{2,3},{3,0},{4,5},{5,6},{6,7},{7,4},{8,9},{9,10},{10,1... | collective-permute-start | bytes 393224 | tf_op jit(solution)/shard_map/ppermute | solution.py:251
  7.9 74.2 %collective-permute-start.1 = (bf16[2048,256]{1,0:T(8,128)(2,1)S(1)}, bf16[2048,256]{1,0:T(8,128)(2,1)}, u32[]{:S(2)}, u32[]{:S(2)}) collective-permute-start(bf16[2048,256]{1,0:T(8,128)(2,1)S(1)} %shard_map.64), channel_id=1, source_target_pairs={{0,2},{1,3},{2,0},{3,1},{4,6},{5,7},{6,4},{7,5},{8,10},{9,11},{10,... | collective-permute-start | bytes 3145736 | tf_op jit(solution)/shard_map/ppermute | solution.py:251
  33.2 24.4 %collective-permute-start.10 = (bf16[256,1024]{1,0:T(8,128)(2,1)S(1)}, bf16[256,1024]{1,0:T(8,128)(2,1)S(1)}, u32[]{:S(2)}, u32[]{:S(2)}) collective-permute-start(bf16[256,1024]{1,0:T(8,128)(2,1)S(1)} %shard_map.66.refs_1_), channel_id=1, source_target_pairs={{0,64},{4,68},{8,72},{12,76},{16,80},{20,84},{24,88},{28,92},{32,9... | collective-permute-start | bytes 1572872 | tf_op jit(solution)/shard_map/ppermute | solution.py:317
  34.8 23.3 %copy-start.1 = (f32[256]{0:T(256)S(1)}, f32[256]{0:T(256)}, u32[]{:S(2)}) copy-start(f32[256]{0:T(256)} %param.9) | copy-start | bytes 3076
  34.8 23.3 %copy-start.2 = (f32[256]{0:T(256)S(1)}, f32[256]{0:T(256)}, u32[]{:S(2)}) copy-start(f32[256]{0:T(256)} %param.10) | copy-start | bytes 3076
  39.4 23.2 %all-to-all-start = ((bf16[64,16,128]{2,1,0:T(8,128)(2,1)}), bf16[64,16,128]{2,1,0:T(8,128)(2,1)S(1)}, u32[]{:S(2)}, u32[]{:S(2)}) async-start(bf16[64,16,128]{2,1,0:T(8,128)(2,1)} %bitcast.5), calls=%async_computation | async-start | bytes 524288 | tf_op jit(solution)/shard_map/all_to_all | solution.py:344
  53.8 36.8 %collective-permute-start = (bf16[2048,256]{1,0:T(8,128)(2,1)}, bf16[2048,256]{1,0:T(8,128)(2,1)}, u32[]{:S(2)}, u32[]{:S(2)}) collective-permute-start(bf16[2048,256]{1,0:T(8,128)(2,1)} %get-tuple-element.11), channel_id=1, source_target_pairs={{0,1},{1,2},{2,3},{3,0},{4,5},{5,6},{6,7},{7,4},{8,9},{9,10},{10,1... | collective-permute-start | bytes 3145736 | tf_op jit(solution)/shard_map/ppermute | solution.py:251
  53.9 36.8 %collective-permute-start.2 = (bf16[2048,256]{1,0:T(8,128)(2,1)}, bf16[2048,256]{1,0:T(8,128)(2,1)}, u32[]{:S(2)}, u32[]{:S(2)}) collective-permute-start(bf16[2048,256]{1,0:T(8,128)(2,1)} %get-tuple-element.12), channel_id=1, source_target_pairs={{0,3},{1,0},{2,1},{3,2},{4,7},{5,4},{6,5},{7,6},{8,11},{9,8},{10,9... | collective-permute-start | bytes 3145736 | tf_op jit(solution)/shard_map/ppermute | solution.py:251
  57.6 24.3 %collective-permute-start.9 = (bf16[256,1024]{1,0:T(8,128)(2,1)S(1)}, bf16[256,1024]{1,0:T(8,128)(2,1)S(1)}, u32[]{:S(2)}, u32[]{:S(2)}) collective-permute-start(bf16[256,1024]{1,0:T(8,128)(2,1)S(1)} %shard_map.66.refs_1_), channel_id=1, source_target_pairs={{0,4},{4,0},{8,12},{12,8},{16,20},{20,16},{24,28},{28,24},{32,36},... | collective-permute-start | bytes 1572872 | tf_op jit(solution)/shard_map/ppermute | solution.py:317
  57.6 29.6 %collective-permute-start.11 = (bf16[256,1024]{1,0:T(8,128)(2,1)S(1)}, bf16[256,1024]{1,0:T(8,128)(2,1)S(1)}, u32[]{:S(2)}, u32[]{:S(2)}) collective-permute-start(bf16[256,1024]{1,0:T(8,128)(2,1)S(1)} %collective-permute-done.10.refs_3_), channel_id=1, source_target_pairs={{0,4},{4,0},{8,12},{12,8},{16,20},{20,16},{24,28},{28,24},{32,36},... | collective-permute-start | bytes 1572872 | tf_op jit(solution)/shard_map/ppermute | solution.py:317
  82.0 8.7 %collective-permute-start.3 = (bf16[16,768]{1,0:T(8,128)(2,1)S(1)}, bf16[16,768]{1,0:T(8,128)(2,1)S(1)}, u32[]{:S(2)}, u32[]{:S(2)}) collective-permute-start(bf16[16,768]{1,0:T(8,128)(2,1)S(1)} %get-tuple-element.14), channel_id=1, source_target_pairs={{0,1},{1,2},{2,3},{3,0},{4,5},{5,6},{6,7},{7,4},{8,9},{9,10},{10,1... | collective-permute-start | bytes 73736 | tf_op jit(solution)/shard_map/ppermute | solution.py:251
  82.1 8.6 %collective-permute-start.4 = (bf16[16,768]{1,0:T(8,128)(2,1)S(1)}, bf16[16,768]{1,0:T(8,128)(2,1)S(1)}, u32[]{:S(2)}, u32[]{:S(2)}) collective-permute-start(bf16[16,768]{1,0:T(8,128)(2,1)S(1)} %get-tuple-element.15), channel_id=1, source_target_pairs={{0,2},{1,3},{2,0},{3,1},{4,6},{5,7},{6,4},{7,5},{8,10},{9,11},{10,... | collective-permute-start | bytes 73736 | tf_op jit(solution)/shard_map/ppermute | solution.py:251
  87.2 3.8 %collective-permute-start.5 = (bf16[16,768]{1,0:T(8,128)(2,1)S(1)}, bf16[16,768]{1,0:T(8,128)(2,1)S(1)}, u32[]{:S(2)}, u32[]{:S(2)}) collective-permute-start(bf16[16,768]{1,0:T(8,128)(2,1)S(1)} %get-tuple-element.16), channel_id=1, source_target_pairs={{0,3},{1,0},{2,1},{3,2},{4,7},{5,4},{6,5},{7,6},{8,11},{9,8},{10,9... | collective-permute-start | bytes 73736 | tf_op jit(solution)/shard_map/ppermute | solution.py:251

commit v5 on v4

--- a/solution.py
+++ b/solution.py
@@ -4,6 +4,7 @@
 from jax.experimental import pallas as pl
 from jax.experimental.pallas import tpu as pltpu
 from jax.sharding import PartitionSpec as P
+
 
 GRP_DEV = 32
 PRIOR = 256.0
@@ -58,59 +59,54 @@
     ]
 
 
-def cut_kernel(info, source, out, sems, *, rows, start):
-    run(row_copies([start(info)], [source], [out], sems, rows))
-
-
-def cut13_kernel(info, values, *refs, rows, blocks, pieces):
-    outs, held_rows, sems_in, sems_out = refs[:2], refs[2], refs[3], refs[4]
-    size = rows // pieces
-    inward, outward = [], []
-    for q, d in enumerate((1, 3)):
-        for p in range(pieces):
-            n = q * pieces + p
-            at = pl.multiple_of(lax.rem(info[0] + d, blocks) * rows + p * size, size)
-            inward.append(pltpu.make_async_copy(values.at[pl.ds(at, size), :], held_rows.at[n], sems_in.at[n]))
-            outward.append(pltpu.make_async_copy(held_rows.at[n], outs[q].at[pl.ds(p * size, size), :], sems_out.at[n]))
-    for copy in inward:
+def cut_kernel(info, values, weight, out_rows, out_slab, sems, *, rows, slab, blocks):
+    run(
+        row_copies([info[2] * slab], [weight], [out_slab], sems, slab)
+        + row_copies([lax.rem(info[0] + 2, blocks) * rows], [values], [out_rows], sems.at[1:], rows)
+    )
+
+
+def stack_kernel(*refs):
+    parts, out = refs[:-1], refs[-1]
+    rows = parts[0].shape[0]
+    for n, part in enumerate(parts):
+        out[n * rows : (n + 1) * rows, :] = part[...]
+
+
+def assemble_kernel(info, near, far, out, sems, *, blocks, cols):
+    half = near.shape[0] // blocks
+
+    def rows_of(n, number):
+        return out.at[pl.ds(pl.multiple_of(n * cols + number * half, half), half), :]
+
+    copies = [
+        pltpu.make_async_copy(near.at[pl.ds(n * half, half), :], rows_of(n, info[2]), sems.at[n])
+        for n in range(blocks)
+    ]
+    for copy in copies:
         copy.start()
-    for copy, onward in zip(inward, outward):
+    for n in range(blocks):
+        rows_of(n, 1 - info[2])[...] = far[n * half : (n + 1) * half, :]
+    for copy in copies:
         copy.wait()
-        onward.start()
-    for onward in outward:
-        onward.wait()
-
-
-def stack_kernel(*refs):
-    parts, out, sems = refs[:-2], refs[-2], refs[-1]
-    rows = parts[0].shape[0]
-    run(
-        [
-            pltpu.make_async_copy(part, out.at[n * rows : (n + 1) * rows, :], sems.at[n])
-            for n, part in enumerate(parts)
-        ]
-    )
-
-
-def assemble_kernel(info, *refs, blocks, slabs, cols):
-    parts, out, sems = refs[: 2 * slabs], refs[-2], refs[-1]
-    slab = parts[0].shape[0] // blocks
-    copies = []
-    for e in range(slabs):
-        first = lax.rem(info[1] + slabs - e, slabs) * 2
-        for c in range(2):
-            number = first + (info[2] if c == 0 else 1 - info[2])
-            for n in range(blocks):
-                at = pl.multiple_of(n * cols + number * slab, slab)
-                source = parts[2 * e + c].at[pl.ds(n * slab, slab), :]
-                copies.append(pltpu.make_async_copy(source, out.at[pl.ds(at, slab), :], sems.at[len(copies)]))
-    run(copies)
-
-
-def stats_kernel(values, owner, sub, out, first, second, scratch, *, tiles, peers):
+
+
+def quarter_of(step, rank, blocks):
+    return lax.rem(rank + jnp.where(step == 0, 1, jnp.where(step == 1, 3, jnp.where(step == 2, 0, 2))), blocks)
+
+
+def stats_kernel(info, values, owner, sub, out, one, three, first, second, scratch, sems, *, tiles, peers):
     step = pl.program_id(0)
     rows, cols = values.shape
-    here = tiles // pl.num_programs(0)
+    blocks = 4
+    here = tiles // blocks
+    quarter = quarter_of(step, info[0], blocks)
+    for n, sent in enumerate((one, three)):
+
+        @pl.when(step == n)
+        def _():
+            pltpu.make_async_copy(values, sent, sems.at[n]).start()
+
     tile_rows = rows // here
     chunk = 16
 
@@ -120,7 +116,7 @@
             at = pl.multiple_of(t * tile_rows + n * chunk, chunk)
             wide = values[pl.ds(at, chunk), :].astype(F32)
             low, high = (wide, wide * wide) if low is None else (low + wide, high + wide * wide)
-        at = pl.multiple_of((step * here + t) * 8, 8)
+        at = pl.multiple_of((quarter * here + t) * 8, 8)
         for n in range(cols // LANES):
             lanes = slice(n * LANES, (n + 1) * LANES)
             first[n, pl.ds(at, 8), :] = low[:8, lanes] + low[8:, lanes]
@@ -128,6 +124,11 @@
         return carry
 
     lax.fori_loop(0, here, one_tile, 0, unroll=2)
+    for n, sent in enumerate((one, three)):
+
+        @pl.when(step == n)
+        def _():
+            pltpu.make_async_copy(values, sent, sems.at[n]).wait()
 
     @pl.when(step == pl.num_programs(0) - 1)
     def _():
@@ -275,27 +276,15 @@
 IN_ANY = pl.BlockSpec(memory_space=pl.ANY)
 
 
-def cut(info, source, rows, start):
-    return pl.pallas_call(
-        lambda *refs: cut_kernel(*refs, rows=rows, start=start),
-        in_specs=[IN_SMEM, IN_HBM],
-        out_specs=IN_VMEM,
-        out_shape=pltpu.VMEM((rows, source.shape[1]), source.dtype),
-        scratch_shapes=[pltpu.SemaphoreType.DMA((1,))],
-        compiler_params=limit(2),
-    )(info, off_chip(source))
-
-
 def stacked(parts):
     rows, cols = parts[0].shape
     return pl.pallas_call(
         stack_kernel,
-        in_specs=[IN_VMEM] * len(parts),
-        out_specs=IN_VMEM,
-        out_shape=pltpu.VMEM((len(parts) * rows, cols), parts[0].dtype),
-        scratch_shapes=[pltpu.SemaphoreType.DMA((len(parts),))],
-        compiler_params=limit(2),
-    )(*[held(part) for part in parts])
+        in_specs=[whole(rows, cols)] * len(parts),
+        out_specs=whole(len(parts) * rows, cols),
+        out_shape=pltpu.HBM((len(parts) * rows, cols), parts[0].dtype),
+        compiler_params=limit(8),
+    )(*parts)
 
 
 def on_device(values, subgroup, owners, col_gain, col_bias, out_weight):
@@ -308,37 +297,41 @@
     outputs = out_weight.shape[1]
     owner_row, sub_row = owners.reshape(1, tiles), subgroup.reshape(1, tiles)
 
-    slabs = 2
-    depth = max(1, peers // 8)
-    info = jnp.stack([rank, (index // (2 * depth)) % slabs, index % 2])
-    slab = cols // (2 * slabs)
-
-    def trade(value, distance):
-        return lax.ppermute(value, "shuf", [(i, i ^ distance) for i in range(peers)])
+    info = jnp.stack([rank, index, index % 2])
+    slab = cols // 2
 
     moved = {}
-    two = cut(info, values, own_rows, lambda ref: lax.rem(ref[0] + 2, blocks) * own_rows)
+    two, own_slab = pl.pallas_call(
+        lambda *refs: cut_kernel(*refs, rows=own_rows, slab=slab, blocks=blocks),
+        in_specs=[IN_SMEM, IN_HBM, IN_HBM],
+        out_specs=[IN_VMEM] * 2,
+        out_shape=[pltpu.VMEM((own_rows, cols), BF16), pltpu.VMEM((slab, outputs), BF16)],
+        scratch_shapes=[pltpu.SemaphoreType.DMA((2,))],
+        compiler_params=limit(2),
+        name="cut",
+    )(info, off_chip(values), off_chip(out_weight))
     moved[2] = hop(two, "rep", 2)
 
-    steps = 4
-    outgoing = pl.pallas_call(
+    in_order = pl.BlockSpec((own_rows, cols), lambda i, info: (quarter_of(i, info[0], blocks), 0))
+    outgoing, one, three = pl.pallas_call(
         lambda *refs: stats_kernel(*refs, tiles=tiles, peers=peers),
-        grid=(steps,),
-        in_specs=[
-            pl.BlockSpec((rows // steps, cols), lambda i: (i, 0)),
-            whole(1, tiles),
-            whole(1, tiles),
-        ],
-        out_specs=whole(peers * MSG, LANES),
-        out_shape=jax.ShapeDtypeStruct((peers * MSG, LANES), BF16),
-        scratch_shapes=[
-            pltpu.VMEM((cols // LANES, tiles * 8, LANES), F32),
-            pltpu.VMEM((cols // LANES, tiles * 8, LANES), F32),
-            pltpu.VMEM((peers * MSG, LANES), F32),
-        ],
+        grid_spec=pltpu.PrefetchScalarGridSpec(
+            num_scalar_prefetch=1,
+            grid=(blocks,),
+            in_specs=[in_order, whole(1, tiles), whole(1, tiles)],
+            out_specs=[whole(peers * MSG, LANES), IN_HBM, IN_HBM],
+            scratch_shapes=[
+                pltpu.VMEM((cols // LANES, tiles * 8, LANES), F32),
+                pltpu.VMEM((cols // LANES, tiles * 8, LANES), F32),
+                pltpu.VMEM((peers * MSG, LANES), F32),
+                pltpu.SemaphoreType.DMA((2,)),
+            ],
+        ),
+        out_shape=[jax.ShapeDtypeStruct((peers * MSG, LANES), BF16)]
+        + [pltpu.HBM((own_rows, cols), BF16)] * 2,
         compiler_params=limit(8),
         name="stats",
-    )(off_chip(values), owner_row, sub_row)
+    )(info, off_chip(values), owner_row, sub_row)
 
     def exchange(message):
         arrived = lax.all_to_all(message.reshape(peers, MSG, LANES), "shuf", 0, 0, tiled=True)
@@ -346,24 +339,9 @@
 
     arrived = exchange(outgoing)
 
-    own_slab = cut(info, out_weight, slab, lambda ref: (ref[1] * 2 + ref[2]) * slab)
     slab_parts = [own_slab]
     for d in range(1, blocks):
         slab_parts.append(hop(own_slab, "rep", d))
-    pieces = 4
-    one, three = pl.pallas_call(
-        lambda *refs: cut13_kernel(*refs, rows=own_rows, blocks=blocks, pieces=pieces),
-        in_specs=[IN_SMEM, IN_HBM],
-        out_specs=[IN_HBM] * 2,
-        out_shape=[pltpu.HBM((own_rows, cols), BF16)] * 2,
-        scratch_shapes=[
-            pltpu.VMEM((2 * pieces, own_rows // pieces, cols), BF16),
-            pltpu.SemaphoreType.DMA((2 * pieces,)),
-            pltpu.SemaphoreType.DMA((2 * pieces,)),
-        ],
-        compiler_params=limit(4),
-        name="cut13",
-    )(info, off_chip(values))
     moved[1] = hop(one, "rep", 1)
     moved[3] = hop(three, "rep", 3)
 
@@ -383,19 +361,17 @@
     )(arrived, both)
     returned = exchange(answer)
 
-    parts = [stacked(slab_parts)]
-    parts.append(trade(parts[0], 1))
-    parts.append(trade(parts[0], 2 * depth))
-    parts.append(trade(parts[2], 1))
+    near = stacked(slab_parts)
+    far = lax.ppermute(near, "shuf", [(i, i ^ 1) for i in range(peers)])
     weight = pl.pallas_call(
-        lambda *refs: assemble_kernel(*refs, blocks=blocks, slabs=slabs, cols=cols),
-        in_specs=[IN_SMEM] + [IN_ANY] * len(parts),
+        lambda *refs: assemble_kernel(*refs, blocks=blocks, cols=cols),
+        in_specs=[IN_SMEM, IN_HBM, IN_VMEM],
         out_specs=IN_VMEM,
         out_shape=pltpu.VMEM((blocks * cols, outputs), BF16),
-        scratch_shapes=[pltpu.SemaphoreType.DMA((2 * slabs * blocks,))],
+        scratch_shapes=[pltpu.SemaphoreType.DMA((blocks,))],
         compiler_params=limit(2),
         name="assemble",
-    )(info, *parts)
+    )(info, off_chip(near), held(far))
 
     each = tiles // blocks
     coeffs = pl.pallas_call(

time: 100 us -> 107 us (1.070)
  waiting for transfers between devices: 27.4 us -> 40.1 us
  Pallas kernels: 24.6 us -> 20.9 us
  starting transfers between devices: 29.1 us -> 27.2 us
    ppermute x9, waiting for transfers between devices: 23 us -> 32.2 us  [hop(): lax.ppermute(value, axis, [(i, (i + distance) % size) for i in range(size)])]
    pallas_call x5 -> x3, Pallas kernels: 10.3 us -> 4.69 us  [the longest x1 1.88 us: on_device(): pl.pallas_call(lambda *refs: cut_kernel(*refs, rows=own_rows, slab=slab,...]
    all_to_all x1, waiting for transfers between devices: 4.41 us -> 7.88 us  [exchange(): lax.all_to_all(message.reshape(peers, MSG, LANES), 'shuf', 0, 0, tiled=True)]
    ppermute x3 -> x1, starting transfers between devices: 2.17 us -> 0.01 us  [on_device(): far = lax.ppermute(near, 'shuf', [(i, i ^ 1) for i in range(peers)])]
    pallas_call x1, Pallas kernels: 4.51 us -> 6.45 us  [on_device(): pl.pallas_call(lambda *refs: stats_kernel(*refs, tiles=tiles, peers=peers...]
  transfers between devices with their start and end apart: 13 -> 11, of which waited for: 3 -> 4; matrix products, arithmetic and copies ran while one was open for 0% -> 0% of each run, Pallas kernels for 15% -> 10%
where the time goes in v5:
time: 107 us; the launch traced here: 106 us
  waiting for transfers between devices  40.1 us (37%)
  starting transfers between devices  27.2 us (25%)
  Pallas kernels  20.9 us (20%)
  blocking collectives  17.8 us (17%)
    ppermute x9, waiting for transfers between devices, hop(): lax.ppermute(value, axis, [(i, (i + distance) % size) for i in range(size)])  32.2 us
    all_to_all x1, blocking collectives, exchange(): lax.all_to_all(message.reshape(peers, MSG, LANES), 'shuf', 0, 0, tiled=True)  17.8 us
    ppermute x9, starting transfers between devices, hop(): lax.ppermute(value, axis, [(i, (i + distance) % size) for i in range(size)])  15.4 us
    all_to_all x1, starting transfers between devices, exchange(): lax.all_to_all(message.reshape(peers, MSG, LANES), 'shuf', 0, 0, tiled=True)  11.9 us
    pallas_call x1, Pallas kernels, on_device(): pl.pallas_call(lambda *refs: project_kernel(*refs, blocks=blocks, tile_ro...  8.21 us
    all_to_all x1, waiting for transfers between devices, exchange(): lax.all_to_all(message.reshape(peers, MSG, LANES), 'shuf', 0, 0, tiled=True)  7.88 us
    pallas_call x1, Pallas kernels, on_device(): pl.pallas_call(lambda *refs: stats_kernel(*refs, tiles=tiles, peers=peers...  6.45 us
  transfers between devices with their start and end apart: 11, of which 4 were waited for; matrix products, arithmetic and copies ran while one was open for 0% of the time, Pallas kernels for 10%

profile of v5, /device:TPU:32, one launch (start us, length us, event | category | flops | bytes accessed | tf_op | source)
XLA Modules:
  0.0 106.3 jit_solution(18403737678578131124)
XLA Ops:
  0.0 0.1 pad_add_fusion.refs_0_
  0.1 1.9 %cut.1 = (bf16[2048,256]{1,0:T(8,128)(2,1)S(1)}, bf16[128,1024]{1,0:T(8,128)(2,1)S(1)}) custom-call(s32[3]{0:T(128)S(1)} %pad_add_fusion.refs_0_, bf16[8192,256]{1,0:T(8,128)(2,1)} %refs_1_.5, bf16[256,1024]{1,0:T(8,128)(2,1)} %refs_2_.1), custom_call_target="tpu_custom_call" | custom-call | tf_op jit(solution)/shard_map/cut/pallas_call | solution.py:304
  2.0 0.0 copy-start.1
  2.0 0.0 copy-start.2
  2.0 2.8 %collective-permute-start.8 = (bf16[128,1024]{1,0:T(8,128)(2,1)S(1)}, bf16[128,1024]{1,0:T(8,128)(2,1)S(1)}, u32[]{:S(2)}, u32[]{:S(2)}) collective-permute-start(bf16[128,1024]{1,0:T(8,128)(2,1)S(1)} %get-tuple-element.22.refs_0_), channel_id=1, source_target_pairs={{0,3},{1,0},{2,1},{3,2},{4,7},{5,4},{6,5},{7,6},{8,11},{9,8},{10,9... | collective-permute-start | bytes 786440 | tf_op jit(solution)/shard_map/ppermute | solution.py:252
  4.8 0.8 collective-permute-start.7
  5.6 0.9 collective-permute-start.6
  6.5 1.8 %collective-permute-start.1 = (bf16[2048,256]{1,0:T(8,128)(2,1)S(1)}, bf16[2048,256]{1,0:T(8,128)(2,1)S(1)}, u32[]{:S(2)}, u32[]{:S(2)}) collective-permute-start(bf16[2048,256]{1,0:T(8,128)(2,1)S(1)} %get-tuple-element.15), channel_id=1, source_target_pairs={{0,2},{1,3},{2,0},{3,1},{4,6},{5,7},{6,4},{7,5},{8,10},{9,11},{10,... | collective-permute-start | bytes 3145736 | tf_op jit(solution)/shard_map/ppermute | solution.py:252
  8.4 30.2 %collective-permute-done.8.refs_3_ = bf16[128,1024]{1,0:T(8,128)(2,1)S(1)} collective-permute-done((bf16[128,1024]{1,0:T(8,128)(2,1)S(1)}, bf16[128,1024]{1,0:T(8,128)(2,1)S(1)}, u32[]{:S(2)}, u32[]{:S(2)}) %collective-permute-start.8) | collective-permute-done | bytes 262176 | tf_op jit(solution)/shard_map/ppermute | solution.py:252
  38.5 0.0 collective-permute-done.7.refs_2_
  38.5 0.0 collective-permute-done.6.refs_1_
  38.5 1.0 shard_map.64.refs_1_
  39.6 0.0 collective-permute-start.9
  39.6 6.4 %stats.1 = (bf16[1024,128]{1,0:T(8,128)(2,1)}, bf16[2048,256]{1,0:T(8,128)(2,1)}, bf16[2048,256]{1,0:T(8,128)(2,1)}) custom-call(s32[3]{0:T(128)S(1)} %pad_add_fusion.refs_0_, bf16[8192,256]{1,0:T(8,128)(2,1)} %refs_1_.5, s32[1,64]{1,0:T(1,128)S(1)} %bitcast.14, s32[1,64]{1,0:T(1,128)S(1)} %bitcast.18), custom_call_target="tpu_custom_call" | custom-call | tf_op jit(solution)/shard_map/stats/pallas_call | solution.py:316
  46.0 11.9 %all-to-all-start = ((bf16[64,16,128]{2,1,0:T(8,128)(2,1)}), bf16[64,16,128]{2,1,0:T(8,128)(2,1)S(1)}, u32[]{:S(2)}, u32[]{:S(2)}) async-start(bf16[64,16,128]{2,1,0:T(8,128)(2,1)} %bitcast.5), calls=%async_computation | async-start | bytes 524288 | tf_op jit(solution)/shard_map/all_to_all | solution.py:337
  57.9 0.1 collective-permute-start
  58.0 3.7 %collective-permute-start.2 = (bf16[2048,256]{1,0:T(8,128)(2,1)}, bf16[2048,256]{1,0:T(8,128)(2,1)}, u32[]{:S(2)}, u32[]{:S(2)}) collective-permute-start(bf16[2048,256]{1,0:T(8,128)(2,1)} %get-tuple-element.16), channel_id=1, source_target_pairs={{0,3},{1,0},{2,1},{3,2},{4,7},{5,4},{6,5},{7,6},{8,11},{9,8},{10,9... | collective-permute-start | bytes 3145736 | tf_op jit(solution)/shard_map/ppermute | solution.py:252
  61.8 7.9 %all-to-all-done = bf16[64,16,128]{2,1,0:T(8,128)(2,1)S(1)} async-done(((bf16[64,16,128]{2,1,0:T(8,128)(2,1)}), bf16[64,16,128]{2,1,0:T(8,128)(2,1)S(1)}, u32[]{:S(2)}, u32[]{:S(2)}) %all-to-all-start) | async-done | bytes 262176 | tf_op jit(solution)/shard_map/all_to_all | solution.py:337
  69.6 0.6 moments.1
  70.3 17.8 %all_to_all.10 = bf16[64,16,128]{2,1,0:T(8,128)(2,1)S(1)} all-to-all(bf16[64,16,128]{2,1,0:T(8,128)(2,1)S(1)} %bitcast.13), channel_id=1, replica_groups=mesh['shuf'=64,'rep'=4] {'shuf'}, dimensions={0} | all-to-all | bytes 524288 | tf_op jit(solution)/shard_map/all_to_all | solution.py:337
  88.1 0.9 pick.1
  89.0 0.1 collective-permute-start.3
  89.1 0.0 collective-permute-done.1.refs_3_
  89.1 5.1 %collective-permute-start.4 = (bf16[16,768]{1,0:T(8,128)(2,1)S(1)}, bf16[16,768]{1,0:T(8,128)(2,1)S(1)}, u32[]{:S(2)}, u32[]{:S(2)}) collective-permute-start(bf16[16,768]{1,0:T(8,128)(2,1)S(1)} %get-tuple-element.20), channel_id=1, source_target_pairs={{0,2},{1,3},{2,0},{3,1},{4,6},{5,7},{6,4},{7,5},{8,10},{9,11},{10,... | collective-permute-start | bytes 73736 | tf_op jit(solution)/shard_map/ppermute | solution.py:252
  94.2 0.0 collective-permute-done.9.refs_2_
  94.2 0.0 collective-permute-start.5
  94.2 1.8 %assemble.1.refs_9_ = bf16[1024,1024]{1,0:T(8,128)(2,1)S(1)} custom-call(s32[3]{0:T(128)S(1)} %pad_add_fusion.refs_0_, bf16[512,1024]{1,0:T(8,128)(2,1)} %shard_map.64.refs_1_, bf16[512,1024]{1,0:T(8,128)(2,1)S(1)} %collective-permute-done.9.refs_2_), custom_call_target="tpu_custom_call" | custom-call | tf_op jit(solution)/shard_map/assemble/pallas_call | solution.py:366
  96.0 0.0 collective-permute-done.refs_2_
  96.0 0.0 collective-permute-done.3.refs_6_
  96.1 0.2 collective-permute-done.4.refs_7_
  96.3 1.8 %collective-permute-done.5.refs_8_ = bf16[16,768]{1,0:T(8,128)(2,1)S(1)} collective-permute-done((bf16[16,768]{1,0:T(8,128)(2,1)S(1)}, bf16[16,768]{1,0:T(8,128)(2,1)S(1)}, u32[]{:S(2)}, u32[]{:S(2)}) %collective-permute-start.5) | collective-permute-done | bytes 24608 | tf_op jit(solution)/shard_map/ppermute | solution.py:252
  98.1 8.2 %project.1 = bf16[2048,1024]{1,0:T(8,128)(2,1)} custom-call(s32[3]{0:T(128)S(1)} %pad_add_fusion.refs_0_, bf16[8192,256]{1,0:T(8,128)(2,1)} %refs_1_.5, bf16[2048,256]{1,0:T(8,128)(2,1)} %collective-permute-done.refs_2_, bf16[2048,256]{1,0:T(8,128)(2,1)} %copy-done.4, bf16[2048,256]{1,0:T(8,128)(2,1)} %collective-permute-done.2.refs_4_, ...), custom_call_target="tpu_custom_call" | custom-call | tf_op jit(solution)/shard_map/project/pallas_call | solution.py:391
  (10 shorter events, 0.0 us)
Async XLA Ops:
  0.0 39.6 %copy-start = (s32[64,1]{0,1:T(1,128)S(1)}, s32[64,1]{0,1:T(1,128)}, u32[]{:S(2)}) copy-start(s32[64,1]{0,1:T(1,128)} %param.8) | copy-start | bytes 772
  0.0 39.6 %copy-start.3 = (s32[64]{0:T(128)S(1)}, s32[64]{0:T(128)}, u32[]{:S(2)}) copy-start(s32[64]{0:T(128)} %param.7) | copy-start | bytes 772
  2.0 59.8 %copy-start.1 = (f32[256]{0:T(256)S(1)}, f32[256]{0:T(256)}, u32[]{:S(2)}) copy-start(f32[256]{0:T(256)} %param.9) | copy-start | bytes 3076
  2.0 59.8 %copy-start.2 = (f32[256]{0:T(256)S(1)}, f32[256]{0:T(256)}, u32[]{:S(2)}) copy-start(f32[256]{0:T(256)} %param.10) | copy-start | bytes 3076
  2.0 36.5 %collective-permute-start.8 = (bf16[128,1024]{1,0:T(8,128)(2,1)S(1)}, bf16[128,1024]{1,0:T(8,128)(2,1)S(1)}, u32[]{:S(2)}, u32[]{:S(2)}) collective-permute-start(bf16[128,1024]{1,0:T(8,128)(2,1)S(1)} %get-tuple-element.22.refs_0_), channel_id=1, source_target_pairs={{0,3},{1,0},{2,1},{3,2},{4,7},{5,4},{6,5},{7,6},{8,11},{9,8},{10,9... | collective-permute-start | bytes 786440 | tf_op jit(solution)/shard_map/ppermute | solution.py:252
  4.8 33.7 %collective-permute-start.7 = (bf16[128,1024]{1,0:T(8,128)(2,1)S(1)}, bf16[128,1024]{1,0:T(8,128)(2,1)S(1)}, u32[]{:S(2)}, u32[]{:S(2)}) collective-permute-start(bf16[128,1024]{1,0:T(8,128)(2,1)S(1)} %get-tuple-element.22.refs_0_), channel_id=1, source_target_pairs={{0,2},{1,3},{2,0},{3,1},{4,6},{5,7},{6,4},{7,5},{8,10},{9,11},{10,... | collective-permute-start | bytes 786440 | tf_op jit(solution)/shard_map/ppermute | solution.py:252
  5.6 32.9 %collective-permute-start.6 = (bf16[128,1024]{1,0:T(8,128)(2,1)S(1)}, bf16[128,1024]{1,0:T(8,128)(2,1)S(1)}, u32[]{:S(2)}, u32[]{:S(2)}) collective-permute-start(bf16[128,1024]{1,0:T(8,128)(2,1)S(1)} %get-tuple-element.22.refs_0_), channel_id=1, source_target_pairs={{0,1},{1,2},{2,3},{3,0},{4,5},{5,6},{6,7},{7,4},{8,9},{9,10},{10,1... | collective-permute-start | bytes 786440 | tf_op jit(solution)/shard_map/ppermute | solution.py:252
  6.5 82.6 %collective-permute-start.1 = (bf16[2048,256]{1,0:T(8,128)(2,1)S(1)}, bf16[2048,256]{1,0:T(8,128)(2,1)S(1)}, u32[]{:S(2)}, u32[]{:S(2)}) collective-permute-start(bf16[2048,256]{1,0:T(8,128)(2,1)S(1)} %get-tuple-element.15), channel_id=1, source_target_pairs={{0,2},{1,3},{2,0},{3,1},{4,6},{5,7},{6,4},{7,5},{8,10},{9,11},{10,... | collective-permute-start | bytes 3145736 | tf_op jit(solution)/shard_map/ppermute | solution.py:252
  39.6 54.7 %collective-permute-start.9 = (bf16[512,1024]{1,0:T(8,128)(2,1)}, bf16[512,1024]{1,0:T(8,128)(2,1)S(1)}, u32[]{:S(2)}, u32[]{:S(2)}) collective-permute-start(bf16[512,1024]{1,0:T(8,128)(2,1)} %shard_map.64.refs_1_), channel_id=1, source_target_pairs={{0,4},{4,0},{8,12},{12,8},{16,20},{20,16},{24,28},{28,24},{32,36},... | collective-permute-start | bytes 3145736 | tf_op jit(solution)/shard_map/ppermute | solution.py:365
  46.0 23.6 %all-to-all-start = ((bf16[64,16,128]{2,1,0:T(8,128)(2,1)}), bf16[64,16,128]{2,1,0:T(8,128)(2,1)S(1)}, u32[]{:S(2)}, u32[]{:S(2)}) async-start(bf16[64,16,128]{2,1,0:T(8,128)(2,1)} %bitcast.5), calls=%async_computation | async-start | bytes 524288 | tf_op jit(solution)/shard_map/all_to_all | solution.py:337
  57.9 38.1 %collective-permute-start = (bf16[2048,256]{1,0:T(8,128)(2,1)}, bf16[2048,256]{1,0:T(8,128)(2,1)}, u32[]{:S(2)}, u32[]{:S(2)}) collective-permute-start(bf16[2048,256]{1,0:T(8,128)(2,1)} %get-tuple-element.14), channel_id=1, source_target_pairs={{0,1},{1,2},{2,3},{3,0},{4,5},{5,6},{6,7},{7,4},{8,9},{9,10},{10,1... | collective-permute-start | bytes 3145736 | tf_op jit(solution)/shard_map/ppermute | solution.py:252
  58.0 38.0 %collective-permute-start.2 = (bf16[2048,256]{1,0:T(8,128)(2,1)}, bf16[2048,256]{1,0:T(8,128)(2,1)}, u32[]{:S(2)}, u32[]{:S(2)}) collective-permute-start(bf16[2048,256]{1,0:T(8,128)(2,1)} %get-tuple-element.16), channel_id=1, source_target_pairs={{0,3},{1,0},{2,1},{3,2},{4,7},{5,4},{6,5},{7,6},{8,11},{9,8},{10,9... | collective-permute-start | bytes 3145736 | tf_op jit(solution)/shard_map/ppermute | solution.py:252
  89.0 7.0 %collective-permute-start.3 = (bf16[16,768]{1,0:T(8,128)(2,1)S(1)}, bf16[16,768]{1,0:T(8,128)(2,1)S(1)}, u32[]{:S(2)}, u32[]{:S(2)}) collective-permute-start(bf16[16,768]{1,0:T(8,128)(2,1)S(1)} %get-tuple-element.19), channel_id=1, source_target_pairs={{0,1},{1,2},{2,3},{3,0},{4,5},{5,6},{6,7},{7,4},{8,9},{9,10},{10,1... | collective-permute-start | bytes 73736 | tf_op jit(solution)/shard_map/ppermute | solution.py:252
  89.1 8.9 %copy-start.4 = (bf16[2048,256]{1,0:T(8,128)(2,1)}, bf16[2048,256]{1,0:T(8,128)(2,1)S(1)}, u32[]{:S(2)}) copy-start(bf16[2048,256]{1,0:T(8,128)(2,1)S(1)} %collective-permute-done.1.refs_3_) | copy-start | bytes 3145732
  89.1 7.2 %collective-permute-start.4 = (bf16[16,768]{1,0:T(8,128)(2,1)S(1)}, bf16[16,768]{1,0:T(8,128)(2,1)S(1)}, u32[]{:S(2)}, u32[]{:S(2)}) collective-permute-start(bf16[16,768]{1,0:T(8,128)(2,1)S(1)} %get-tuple-element.20), channel_id=1, source_target_pairs={{0,2},{1,3},{2,0},{3,1},{4,6},{5,7},{6,4},{7,5},{8,10},{9,11},{10,... | collective-permute-start | bytes 73736 | tf_op jit(solution)/shard_map/ppermute | solution.py:252
  94.2 3.8 %collective-permute-start.5 = (bf16[16,768]{1,0:T(8,128)(2,1)S(1)}, bf16[16,768]{1,0:T(8,128)(2,1)S(1)}, u32[]{:S(2)}, u32[]{:S(2)}) collective-permute-start(bf16[16,768]{1,0:T(8,128)(2,1)S(1)} %get-tuple-element.21), channel_id=1, source_target_pairs={{0,3},{1,0},{2,1},{3,2},{4,7},{5,4},{6,5},{7,6},{8,11},{9,8},{10,9... | collective-permute-start | bytes 73736 | tf_op jit(solution)/shard_map/ppermute | solution.py:252

commit v6 on v5

--- a/solution.py
+++ b/solution.py
@@ -52,60 +52,76 @@
         copy.wait()
 
 
-def row_copies(starts, sources, outs, sems, rows):
-    return [
-        pltpu.make_async_copy(source.at[pl.ds(pl.multiple_of(start, rows), rows), :], out, sems.at[n])
-        for n, (start, source, out) in enumerate(zip(starts, sources, outs))
+def cut_kernel(values, weight, out, sems, *, rows, blocks):
+    half, cols = weight.shape[0] // 2, values.shape[1]
+    first = pl.multiple_of(lax.rem(lax.axis_index("rep") + 2, blocks) * rows, rows)
+    mine = pl.multiple_of(lax.rem(lax.axis_index("shuf"), 2) * half, half)
+    copies = [
+        pltpu.make_async_copy(values.at[pl.ds(first, rows), :], out.at[pl.ds(blocks * half, rows), :], sems.at[blocks])
     ]
-
-
-def cut_kernel(info, values, weight, out_rows, out_slab, sems, *, rows, slab, blocks):
-    run(
-        row_copies([info[2] * slab], [weight], [out_slab], sems, slab)
-        + row_copies([lax.rem(info[0] + 2, blocks) * rows], [values], [out_rows], sems.at[1:], rows)
-    )
+    for n in range(blocks):
+        source = weight.at[pl.ds(mine, half), pl.ds(n * cols, cols)]
+        copies.append(pltpu.make_async_copy(source, out.at[pl.ds(n * half, half), :], sems.at[n]))
+    run(copies)
 
 
 def stack_kernel(*refs):
     parts, out = refs[:-1], refs[-1]
-    rows = parts[0].shape[0]
+    rows, cols = parts[0].shape
+    count = out.shape[1] // cols
+    half = rows // count
     for n, part in enumerate(parts):
-        out[n * rows : (n + 1) * rows, :] = part[...]
-
-
-def assemble_kernel(info, near, far, out, sems, *, blocks, cols):
+        for c in range(count):
+            out[n * half : (n + 1) * half, c * cols : (c + 1) * cols] = part[c * half : (c + 1) * half, :]
+
+
+def assemble_kernel(near, far, out, sems, *, blocks, cols):
     half = near.shape[0] // blocks
+    core = lax.rem(lax.axis_index("shuf"), 2)
 
     def rows_of(n, number):
         return out.at[pl.ds(pl.multiple_of(n * cols + number * half, half), half), :]
 
     copies = [
-        pltpu.make_async_copy(near.at[pl.ds(n * half, half), :], rows_of(n, info[2]), sems.at[n])
-        for n in range(blocks)
+        pltpu.make_async_copy(near.at[pl.ds(n * half, half), :], rows_of(n, core), sems.at[n]) for n in range(blocks)
     ]
     for copy in copies:
         copy.start()
     for n in range(blocks):
-        rows_of(n, 1 - info[2])[...] = far[n * half : (n + 1) * half, :]
+        rows_of(n, 1 - core)[...] = far[n * half : (n + 1) * half, :]
     for copy in copies:
         copy.wait()
 
 
-def quarter_of(step, rank, blocks):
+def quarter_of(step, blocks):
+    rank = lax.axis_index("rep")
     return lax.rem(rank + jnp.where(step == 0, 1, jnp.where(step == 1, 3, jnp.where(step == 2, 0, 2))), blocks)
 
 
-def stats_kernel(info, values, owner, sub, out, one, three, first, second, scratch, sems, *, tiles, peers):
+def stats_kernel(values, weight, owner, sub, out, *refs, tiles, peers):
+    sent, (first, second, scratch, sems) = refs[:4], refs[4:]
     step = pl.program_id(0)
     rows, cols = values.shape
     blocks = 4
+    half, part = weight.shape[0], rows // 2
     here = tiles // blocks
-    quarter = quarter_of(step, info[0], blocks)
-    for n, sent in enumerate((one, three)):
+    quarter = quarter_of(step, blocks)
+
+    def copies(n):
+        early, late = sent[2 * n : 2 * n + 2]
+        for c in range(blocks):
+            source = weight.at[:, pl.ds(c * cols, cols)]
+            yield pltpu.make_async_copy(source, early.at[pl.ds(c * half, half), :], sems.at[n, c])
+        source = values.at[pl.ds(0, part), :]
+        yield pltpu.make_async_copy(source, early.at[pl.ds(blocks * half, part), :], sems.at[n, blocks])
+        yield pltpu.make_async_copy(values.at[pl.ds(part, part), :], late, sems.at[n, blocks + 1])
+
+    for n in range(2):
 
         @pl.when(step == n)
         def _():
-            pltpu.make_async_copy(values, sent, sems.at[n]).start()
+            for copy in copies(n):
+                copy.start()
 
     tile_rows = rows // here
     chunk = 16
@@ -124,11 +140,12 @@
         return carry
 
     lax.fori_loop(0, here, one_tile, 0, unroll=2)
-    for n, sent in enumerate((one, three)):
+    for n in range(2):
 
         @pl.when(step == n)
         def _():
-            pltpu.make_async_copy(values, sent, sems.at[n]).wait()
+            for copy in copies(n):
+                copy.wait()
 
     @pl.when(step == pl.num_programs(0) - 1)
     def _():
@@ -209,11 +226,11 @@
     out[...] = scratch[...].astype(BF16)
 
 
-def tile_kernel(info, arrived, owner, *refs, tiles, peers, blocks):
+def tile_kernel(arrived, owner, *refs, tiles, peers, blocks):
     outs, scratch = refs[:-1], refs[-1]
     scratch[...] = arrived[...].astype(F32)
     owner_row = owner[...].astype(F32)
-    at = (iota((tiles, tiles), 0) + info[0] * (tiles // blocks)) % tiles
+    at = (iota((tiles, tiles), 0) + lax.axis_index("rep") * (tiles // blocks)) % tiles
     place = as_column(places(owner_row), tiles, at)
     named = as_column(owner_row, tiles, at) == iota((tiles, peers), 1).astype(F32)
     hot = jnp.concatenate([jnp.where(named & (place == float(slot)), 1.0, 0.0) for slot in range(2)], axis=1)
@@ -224,8 +241,8 @@
         out[...] = picked[n * each : (n + 1) * each, :].astype(BF16)
 
 
-def project_kernel(info, *refs, blocks, tile_rows):
-    moved, coeffs, (weight, out, wide) = refs[:blocks], refs[blocks : 2 * blocks], refs[2 * blocks :]
+def project_kernel(*refs, blocks, tile_rows, tile_at):
+    moved, coeffs, weight, (out, wide) = refs[:blocks], refs[blocks : 2 * blocks], refs[2 * blocks], refs[-2:]
     step = pl.program_id(0)
     rows, cols = moved[0].shape
     tiles = rows // tile_rows
@@ -239,7 +256,7 @@
     for t in range(tiles):
         parts = []
         for n in range(blocks):
-            row = wide[n, pl.ds(step * tiles + t, 1), :]
+            row = wide[n, pl.ds(tile_at + step * tiles + t, 1), :]
             value = moved[n][t * tile_rows : (t + 1) * tile_rows, :].astype(F32)
             scored = value * row[:, :cols] + (row[:, cols : 2 * cols] + row[:, 2 * cols :])
             parts.append(scored.astype(BF16))
@@ -276,62 +293,49 @@
 IN_ANY = pl.BlockSpec(memory_space=pl.ANY)
 
 
-def stacked(parts):
-    rows, cols = parts[0].shape
-    return pl.pallas_call(
-        stack_kernel,
-        in_specs=[whole(rows, cols)] * len(parts),
-        out_specs=whole(len(parts) * rows, cols),
-        out_shape=pltpu.HBM((len(parts) * rows, cols), parts[0].dtype),
-        compiler_params=limit(8),
-    )(*parts)
-
-
 def on_device(values, subgroup, owners, col_gain, col_bias, out_weight):
     rows, cols = values.shape
     tiles = subgroup.shape[0]
     tile_rows = rows // tiles
     peers, blocks = lax.axis_size("shuf"), lax.axis_size("rep")
-    rank, index = lax.axis_index("rep"), lax.axis_index("shuf")
     own_rows = rows // blocks
     outputs = out_weight.shape[1]
     owner_row, sub_row = owners.reshape(1, tiles), subgroup.reshape(1, tiles)
 
-    info = jnp.stack([rank, index, index % 2])
-    slab = cols // 2
-
     moved = {}
-    two, own_slab = pl.pallas_call(
-        lambda *refs: cut_kernel(*refs, rows=own_rows, slab=slab, blocks=blocks),
-        in_specs=[IN_SMEM, IN_HBM, IN_HBM],
-        out_specs=[IN_VMEM] * 2,
-        out_shape=[pltpu.VMEM((own_rows, cols), BF16), pltpu.VMEM((slab, outputs), BF16)],
-        scratch_shapes=[pltpu.SemaphoreType.DMA((2,))],
+    two = pl.pallas_call(
+        lambda *refs: cut_kernel(*refs, rows=own_rows, blocks=blocks),
+        in_specs=[IN_HBM, IN_HBM],
+        out_specs=IN_VMEM,
+        out_shape=pltpu.VMEM((2 * cols + own_rows, cols), BF16),
+        scratch_shapes=[pltpu.SemaphoreType.DMA((blocks + 1,))],
         compiler_params=limit(2),
         name="cut",
-    )(info, off_chip(values), off_chip(out_weight))
+    )(off_chip(values), off_chip(out_weight))
     moved[2] = hop(two, "rep", 2)
 
-    in_order = pl.BlockSpec((own_rows, cols), lambda i, info: (quarter_of(i, info[0], blocks), 0))
-    outgoing, one, three = pl.pallas_call(
+    part = own_rows // 2
+    outgoing, one, one_late, three, three_late = pl.pallas_call(
         lambda *refs: stats_kernel(*refs, tiles=tiles, peers=peers),
-        grid_spec=pltpu.PrefetchScalarGridSpec(
-            num_scalar_prefetch=1,
-            grid=(blocks,),
-            in_specs=[in_order, whole(1, tiles), whole(1, tiles)],
-            out_specs=[whole(peers * MSG, LANES), IN_HBM, IN_HBM],
-            scratch_shapes=[
-                pltpu.VMEM((cols // LANES, tiles * 8, LANES), F32),
-                pltpu.VMEM((cols // LANES, tiles * 8, LANES), F32),
-                pltpu.VMEM((peers * MSG, LANES), F32),
-                pltpu.SemaphoreType.DMA((2,)),
-            ],
-        ),
-        out_shape=[jax.ShapeDtypeStruct((peers * MSG, LANES), BF16)]
-        + [pltpu.HBM((own_rows, cols), BF16)] * 2,
+        grid=(blocks,),
+        in_specs=[
+            pl.BlockSpec((own_rows, cols), lambda i: (quarter_of(i, blocks), 0)),
+            pl.BlockSpec((cols // 2, outputs), lambda i: (lax.rem(lax.axis_index("shuf"), 2), 0)),
+            whole(1, tiles),
+            whole(1, tiles),
+        ],
+        out_specs=[whole(peers * MSG, LANES)] + [IN_HBM] * 4,
+        scratch_shapes=[
+            pltpu.VMEM((cols // LANES, tiles * 8, LANES), F32),
+            pltpu.VMEM((cols // LANES, tiles * 8, LANES), F32),
+            pltpu.VMEM((peers * MSG, LANES), F32),
+            pltpu.SemaphoreType.DMA((2, blocks + 2)),
+        ],
+        out_shape=[pltpu.HBM((peers * MSG, LANES), BF16)]
+        + [pltpu.HBM((2 * cols + part, cols), BF16), pltpu.HBM((part, cols), BF16)] * 2,
         compiler_params=limit(8),
         name="stats",
-    )(info, off_chip(values), owner_row, sub_row)
+    )(off_chip(values), off_chip(out_weight), owner_row, sub_row)
 
     def exchange(message):
         arrived = lax.all_to_all(message.reshape(peers, MSG, LANES), "shuf", 0, 0, tiled=True)
@@ -339,11 +343,11 @@
 
     arrived = exchange(outgoing)
 
-    slab_parts = [own_slab]
-    for d in range(1, blocks):
-        slab_parts.append(hop(own_slab, "rep", d))
-    moved[1] = hop(one, "rep", 1)
-    moved[3] = hop(three, "rep", 3)
+    late = {}
+    for d, early_rows in ((1, one), (3, three)):
+        moved[d] = hop(early_rows, "rep", d)
+    for d, late_rows in ((1, one_late), (3, three_late)):
+        late[d] = hop(late_rows, "rep", d)
 
     both = pl.pallas_call(
         pair_kernel,
@@ -354,61 +358,82 @@
     answer = pl.pallas_call(
         lambda *refs: owner_kernel(*refs, peers=peers, tile_rows=tile_rows),
         in_specs=[IN_VMEM, whole(2, cols)],
-        out_shape=jax.ShapeDtypeStruct((peers * MSG, LANES), BF16),
+        out_shape=pltpu.HBM((peers * MSG, LANES), BF16),
         scratch_shapes=[pltpu.VMEM((peers * MSG, LANES), F32)],
         compiler_params=limit(6),
         name="moments",
     )(arrived, both)
     returned = exchange(answer)
 
-    near = stacked(slab_parts)
+    near = pl.pallas_call(
+        stack_kernel,
+        grid=(1,),
+        in_specs=[whole(2 * cols, cols)] * blocks,
+        out_specs=whole(blocks * cols // 2, outputs),
+        out_shape=pltpu.HBM((blocks * cols // 2, outputs), BF16),
+        compiler_params=limit(8),
+        name="stack",
+    )(two, moved[1], moved[2], moved[3])
     far = lax.ppermute(near, "shuf", [(i, i ^ 1) for i in range(peers)])
     weight = pl.pallas_call(
         lambda *refs: assemble_kernel(*refs, blocks=blocks, cols=cols),
-        in_specs=[IN_SMEM, IN_HBM, IN_VMEM],
+        in_specs=[IN_HBM, IN_VMEM],
         out_specs=IN_VMEM,
         out_shape=pltpu.VMEM((blocks * cols, outputs), BF16),
         scratch_shapes=[pltpu.SemaphoreType.DMA((blocks,))],
         compiler_params=limit(2),
         name="assemble",
-    )(info, off_chip(near), held(far))
+    )(off_chip(near), held(far))
 
     each = tiles // blocks
     coeffs = pl.pallas_call(
         lambda *refs: tile_kernel(*refs, tiles=tiles, peers=peers, blocks=blocks),
-        in_specs=[IN_SMEM, IN_VMEM, whole(1, tiles)],
+        in_specs=[IN_VMEM, whole(1, tiles)],
         out_specs=[IN_VMEM] * blocks,
         out_shape=[pltpu.VMEM((each, 3 * cols), BF16)] * blocks,
         scratch_shapes=[pltpu.VMEM((peers * MSG, LANES), F32)],
         compiler_params=limit(4),
         name="pick",
-    )(info, returned, owner_row)
+    )(returned, owner_row)
     known = {0: coeffs[0]}
     for d in (2, 1, 3):
         known[d] = hop(coeffs[d], "rep", d)
 
-    block = min(512, own_rows)
-    return pl.pallas_call(
-        lambda *refs: project_kernel(*refs, blocks=blocks, tile_rows=tile_rows),
-        grid_spec=pltpu.PrefetchScalarGridSpec(
-            num_scalar_prefetch=1,
-            grid=(own_rows // block,),
-            in_specs=[pl.BlockSpec((block, cols), lambda i, info: (info[0] * (own_rows // block) + i, 0))]
-            + [pl.BlockSpec((block, cols), lambda i, info: (i, 0))] * (blocks - 1)
-            + [IN_VMEM] * (blocks + 1),
-            out_specs=pl.BlockSpec((block, outputs), lambda i, info: (i, 0)),
-            scratch_shapes=[pltpu.VMEM((blocks, each, 3 * cols), F32)],
-        ),
-        out_shape=jax.ShapeDtypeStruct((own_rows, outputs), BF16),
-        compiler_params=limit(24),
-        name="project",
-    )(
-        info,
-        off_chip(values),
-        *[off_chip(moved[d]) for d in range(1, blocks)],
-        *[held(known[d]) for d in range(blocks)],
-        held(weight),
-    )
+    block = min(256, part)
+    steps = part // block
+    skipped = 2 * cols // block
+    result = []
+    for n in range(2):
+        at = n * steps
+        messages = [(moved[1], skipped), (moved[2], skipped), (moved[3], skipped)]
+        if n == 1:
+            messages = [(late[1], 0), (moved[2], skipped + at), (late[3], 0)]
+        result = [
+            pl.pallas_call(
+                lambda *refs: project_kernel(
+                    *refs, blocks=blocks, tile_rows=tile_rows, tile_at=at * block // tile_rows
+                ),
+                grid=(steps,),
+                in_specs=[
+                    pl.BlockSpec((block, cols), lambda i: (lax.axis_index("rep") * (2 * steps) + at + i, 0))
+                ]
+                + [pl.BlockSpec((block, cols), lambda i, first=first: (first + i, 0)) for _, first in messages]
+                + [IN_VMEM] * (blocks + 1)
+                + [IN_HBM] * n,
+                out_specs=pl.BlockSpec((block, outputs), lambda i: (at + i, 0)),
+                scratch_shapes=[pltpu.VMEM((blocks, each, 3 * cols), F32)],
+                out_shape=jax.ShapeDtypeStruct((own_rows, outputs), BF16),
+                input_output_aliases={2 * blocks + 1: 0} if n else {},
+                compiler_params=limit(24),
+            )(
+                off_chip(values),
+                *[off_chip(message) if message is late[1] or message is late[3] else message for message, _ in messages],
+                *[held(known[d]) for d in range(blocks)],
+                held(weight),
+                *[off_chip(array) for array in result],
+            )
+        ]
+    return result[0]
 
 
 def solution(mesh):

time: 107 us -> 115 us (1.075)
  blocking collectives: 17.8 us -> 0 us
  waiting for transfers between devices: 40.1 us -> 56.5 us
  starting transfers between devices: 27.2 us -> 33.5 us
  Pallas kernels: 20.9 us -> 23.2 us
    all_to_all x1 -> x0, blocking collectives: 17.8 us -> none  [exchange(): lax.all_to_all(message.reshape(peers, MSG, LANES), 'shuf', 0, 0, tiled=True)]
    all_to_all x1 -> x2, waiting for transfers between devices: 7.88 us -> 20.1 us  [exchange(): lax.all_to_all(message.reshape(peers, MSG, LANES), 'shuf', 0, 0, tiled=True)]
    all_to_all x1 -> x2, starting transfers between devices: 11.9 us -> 18.2 us  [exchange(): lax.all_to_all(message.reshape(peers, MSG, LANES), 'shuf', 0, 0, tiled=True)]
    ppermute x9 -> x8, waiting for transfers between devices: 32.2 us -> 36.4 us  [hop(): lax.ppermute(value, axis, [(i, (i + distance) % size) for i in range(size)])]
    pallas_call x1 -> x2, Pallas kernels: 8.21 us -> 10.3 us  [on_device(): pl.pallas_call(lambda *refs: project_kernel(*refs, blocks=blocks, tile_ro...]
    ppermute x9 -> x8, starting transfers between devices: 15.4 us -> 15.3 us  [hop(): lax.ppermute(value, axis, [(i, (i + distance) % size) for i in range(size)])]
  transfers between devices with their start and end apart: 11 -> 11, of which waited for: 4 -> 4; matrix products, arithmetic and copies ran while one was open for 0% -> 0% of each run, Pallas kernels for 10% -> 14%
where the time goes in v6:
time: 115 us; the launch traced here: 113 us
  waiting for transfers between devices  56.5 us (49%)
  starting transfers between devices  33.5 us (29%)
  Pallas kernels  23.2 us (20%)
    ppermute x8, waiting for transfers between devices, hop(): lax.ppermute(value, axis, [(i, (i + distance) % size) for i in range(size)])  36.4 us
    all_to_all x2, waiting for transfers between devices, exchange(): lax.all_to_all(message.reshape(peers, MSG, LANES), 'shuf', 0, 0, tiled=True)  20.1 us
    all_to_all x2, starting transfers between devices, exchange(): lax.all_to_all(message.reshape(peers, MSG, LANES), 'shuf', 0, 0, tiled=True)  18.2 us
    ppermute x8, starting transfers between devices, hop(): lax.ppermute(value, axis, [(i, (i + distance) % size) for i in range(size)])  15.3 us
    pallas_call x2, Pallas kernels, on_device(): pl.pallas_call(lambda *refs: project_kernel(*refs, blocks=blocks, tile_ro...  10.3 us
    pallas_call x1, Pallas kernels, on_device(): pl.pallas_call(lambda *refs: stats_kernel(*refs, tiles=tiles, peers=peers...  6.26 us
    pallas_call x1, Pallas kernels, on_device(): pl.pallas_call(lambda *refs: assemble_kernel(*refs, blocks=blocks, cols=c...  2.46 us
  transfers between devices with their start and end apart: 11, of which 4 were waited for; matrix products, arithmetic and copies ran while one was open for 0% of the time, Pallas kernels for 14%

profile of v6, /device:TPU:32, one launch (start us, length us, event | category | flops | bytes accessed | tf_op | source)
XLA Modules:
  0.0 113.3 jit_solution(7877247666917592981)
XLA Ops:
  0.0 1.3 %cut.1.refs_0_ = bf16[2560,256]{1,0:T(8,128)(2,1)S(1)} custom-call(bf16[8192,256]{1,0:T(8,128)(2,1)} %refs_0_.7, bf16[256,1024]{1,0:T(8,128)(2,1)} %refs_1_.3), custom_call_target="tpu_custom_call" | custom-call | tf_op jit(solution)/shard_map/cut/pallas_call | solution.py:306
  1.3 3.1 %collective-permute-start.1 = (bf16[2560,256]{1,0:T(8,128)(2,1)S(1)}, bf16[2560,256]{1,0:T(8,128)(2,1)S(1)}, u32[]{:S(2)}, u32[]{:S(2)}) collective-permute-start(bf16[2560,256]{1,0:T(8,128)(2,1)S(1)} %cut.1.refs_0_), channel_id=1, source_target_pairs={{0,2},{1,3},{2,0},{3,1},{4,6},{5,7},{6,4},{7,5},{8,10},{9,11},{10,... | collective-permute-start | bytes 3932168 | tf_op jit(solution)/shard_map/ppermute | solution.py:269
  4.4 0.0 copy-done
  4.4 6.3 %stats.1 = (bf16[1024,128]{1,0:T(8,128)(2,1)}, bf16[1536,256]{1,0:T(8,128)(2,1)}, bf16[1024,256]{1,0:T(8,128)(2,1)}, bf16[1536,256]{1,0:T(8,128)(2,1)}, bf16[1024,256]{1,0:T(8,128)(2,1)}) custom-call(bf16[8192,256]{1,0:T(8,128)(2,1)} %refs_0_.7, bf16[256,1024]{1,0:T(8,128)(2,1)} %refs_1_.3, s32[1,64]{1,0:T(1,128)S(1)} %bitcast.10, s32[1,64]{1,0:T(1,128)S(1)} %bitcast.14), custom_call_target="tpu_custom_call" | custom-call | tf_op jit(solution)/shard_map/stats/pallas_call | solution.py:318
  10.7 0.7 collective-permute-start.6
  11.4 2.6 %collective-permute-start.7 = (bf16[1536,256]{1,0:T(8,128)(2,1)}, bf16[1536,256]{1,0:T(8,128)(2,1)S(1)}, u32[]{:S(2)}, u32[]{:S(2)}) collective-permute-start(bf16[1536,256]{1,0:T(8,128)(2,1)} %get-tuple-element.22), channel_id=1, source_target_pairs={{0,3},{1,0},{2,1},{3,2},{4,7},{5,4},{6,5},{7,6},{8,11},{9,8},{10,9... | collective-permute-start | bytes 2359304 | tf_op jit(solution)/shard_map/ppermute | solution.py:269
  14.0 36.3 %collective-permute-done.6.refs_1_ = bf16[1536,256]{1,0:T(8,128)(2,1)S(1)} collective-permute-done((bf16[1536,256]{1,0:T(8,128)(2,1)}, bf16[1536,256]{1,0:T(8,128)(2,1)S(1)}, u32[]{:S(2)}, u32[]{:S(2)}) %collective-permute-start.6) | collective-permute-done | bytes 786464 | tf_op jit(solution)/shard_map/ppermute | solution.py:269
  50.3 0.1 collective-permute-done.7.refs_3_
  50.4 0.0 collective-permute-done.1.refs_2_
  50.4 1.1 stack.1.refs_0_
  51.5 0.0 collective-permute-start.8
  51.5 11.9 %all-to-all-start = ((bf16[64,16,128]{2,1,0:T(8,128)(2,1)}), bf16[64,16,128]{2,1,0:T(8,128)(2,1)S(1)}, u32[]{:S(2)}, u32[]{:S(2)}) async-start(bf16[64,16,128]{2,1,0:T(8,128)(2,1)} %bitcast.2), calls=%async_computation | async-start | bytes 524288 | tf_op jit(solution)/shard_map/all_to_all | solution.py:341
  63.4 0.0 copy-done.1
  63.4 11.7 %all-to-all-done = bf16[64,16,128]{2,1,0:T(8,128)(2,1)S(1)} async-done(((bf16[64,16,128]{2,1,0:T(8,128)(2,1)}), bf16[64,16,128]{2,1,0:T(8,128)(2,1)S(1)}, u32[]{:S(2)}, u32[]{:S(2)}) %all-to-all-start) | async-done | bytes 262176 | tf_op jit(solution)/shard_map/all_to_all | solution.py:341
  75.1 1.4 %moments.1 = bf16[1024,128]{1,0:T(8,128)(2,1)} custom-call(bf16[1024,128]{1,0:T(8,128)(2,1)S(1)} %bitcast.9, f32[2,256]{1,0:T(2,128)S(1)} %pair.1.refs_1_), custom_call_target="tpu_custom_call" | custom-call | tf_op jit(solution)/shard_map/moments/pallas_call | solution.py:358
  76.5 6.3 %all-to-all-start.1 = ((bf16[64,16,128]{2,1,0:T(8,128)(2,1)}), bf16[64,16,128]{2,1,0:T(8,128)(2,1)S(1)}, u32[]{:S(2)}, u32[]{:S(2)}) async-start(bf16[64,16,128]{2,1,0:T(8,128)(2,1)} %bitcast.15), calls=%async_computation.1 | async-start | bytes 524288 | tf_op jit(solution)/shard_map/all_to_all | solution.py:341
  82.7 1.5 %collective-permute-start = (bf16[1024,256]{1,0:T(8,128)(2,1)}, bf16[1024,256]{1,0:T(8,128)(2,1)}, u32[]{:S(2)}, u32[]{:S(2)}) collective-permute-start(bf16[1024,256]{1,0:T(8,128)(2,1)} %get-tuple-element.14), channel_id=1, source_target_pairs={{0,1},{1,2},{2,3},{3,0},{4,5},{5,6},{6,7},{7,4},{8,9},{9,10},{10,1... | collective-permute-start | bytes 1572872 | tf_op jit(solution)/shard_map/ppermute | solution.py:269
  84.3 1.8 %collective-permute-start.2 = (bf16[1024,256]{1,0:T(8,128)(2,1)}, bf16[1024,256]{1,0:T(8,128)(2,1)}, u32[]{:S(2)}, u32[]{:S(2)}) collective-permute-start(bf16[1024,256]{1,0:T(8,128)(2,1)} %get-tuple-element.15), channel_id=1, source_target_pairs={{0,3},{1,0},{2,1},{3,2},{4,7},{5,4},{6,5},{7,6},{8,11},{9,8},{10,9... | collective-permute-start | bytes 1572872 | tf_op jit(solution)/shard_map/ppermute | solution.py:269
  86.1 8.4 %all-to-all-done.1 = bf16[64,16,128]{2,1,0:T(8,128)(2,1)S(1)} async-done(((bf16[64,16,128]{2,1,0:T(8,128)(2,1)}), bf16[64,16,128]{2,1,0:T(8,128)(2,1)S(1)}, u32[]{:S(2)}, u32[]{:S(2)}) %all-to-all-start.1) | async-done | bytes 262176 | tf_op jit(solution)/shard_map/all_to_all | solution.py:341
  94.5 0.4 pick.1
  94.9 1.5 %collective-permute-start.3 = (bf16[16,768]{1,0:T(8,128)(2,1)S(1)}, bf16[16,768]{1,0:T(8,128)(2,1)S(1)}, u32[]{:S(2)}, u32[]{:S(2)}) collective-permute-start(bf16[16,768]{1,0:T(8,128)(2,1)S(1)} %get-tuple-element.18), channel_id=1, source_target_pairs={{0,1},{1,2},{2,3},{3,0},{4,5},{5,6},{6,7},{7,4},{8,9},{9,10},{10,1... | collective-permute-start | bytes 73736 | tf_op jit(solution)/shard_map/ppermute | solution.py:269
  96.4 2.7 %collective-permute-start.4 = (bf16[16,768]{1,0:T(8,128)(2,1)S(1)}, bf16[16,768]{1,0:T(8,128)(2,1)S(1)}, u32[]{:S(2)}, u32[]{:S(2)}) collective-permute-start(bf16[16,768]{1,0:T(8,128)(2,1)S(1)} %get-tuple-element.19), channel_id=1, source_target_pairs={{0,2},{1,3},{2,0},{3,1},{4,6},{5,7},{6,4},{7,5},{8,10},{9,11},{10,... | collective-permute-start | bytes 73736 | tf_op jit(solution)/shard_map/ppermute | solution.py:269
  99.0 0.0 collective-permute-done.8.refs_1_
  99.0 1.4 %collective-permute-start.5 = (bf16[16,768]{1,0:T(8,128)(2,1)S(1)}, bf16[16,768]{1,0:T(8,128)(2,1)S(1)}, u32[]{:S(2)}, u32[]{:S(2)}) collective-permute-start(bf16[16,768]{1,0:T(8,128)(2,1)S(1)} %get-tuple-element.20), channel_id=1, source_target_pairs={{0,3},{1,0},{2,1},{3,2},{4,7},{5,4},{6,5},{7,6},{8,11},{9,8},{10,9... | collective-permute-start | bytes 73736 | tf_op jit(solution)/shard_map/ppermute | solution.py:269
  100.5 2.5 %assemble.1.refs_8_ = bf16[1024,1024]{1,0:T(8,128)(2,1)S(1)} custom-call(bf16[512,1024]{1,0:T(8,128)(2,1)} %stack.1.refs_0_, bf16[512,1024]{1,0:T(8,128)(2,1)} %collective-permute-done.8.refs_1_), custom_call_target="tpu_custom_call" | custom-call | tf_op jit(solution)/shard_map/assemble/pallas_call | solution.py:378
  102.9 0.0 collective-permute-done.3.refs_5_
  103.0 0.0 collective-permute-done.4.refs_6_
  103.0 0.0 collective-permute-done.5.refs_7_
  103.0 5.0 %shard_map.64.refs_9_ = bf16[2048,1024]{1,0:T(8,128)(2,1)} custom-call(bf16[8192,256]{1,0:T(8,128)(2,1)} %refs_0_.7, bf16[1536,256]{1,0:T(8,128)(2,1)S(1)} %collective-permute-done.6.refs_1_, bf16[2560,256]{1,0:T(8,128)(2,1)S(1)} %collective-permute-done.1.refs_2_, bf16[1536,256]{1,0:T(8,128)(2,1)S(1)} %collective-permute-done.7.refs_3_, ...), custom_call_target="tpu_custom_call" | custom-call | tf_op jit(solution)/shard_map/pallas_call | solution.py:412
  108.0 0.0 collective-permute-done.refs_1_
  108.0 0.0 collective-permute-done.2.refs_3_
  108.0 5.3 %shard_map.65 = bf16[2048,1024]{1,0:T(8,128)(2,1)} custom-call(bf16[8192,256]{1,0:T(8,128)(2,1)} %refs_0_.7, bf16[1024,256]{1,0:T(8,128)(2,1)} %collective-permute-done.refs_1_, bf16[2560,256]{1,0:T(8,128)(2,1)S(1)} %collective-permute-done.1.refs_2_, bf16[1024,256]{1,0:T(8,128)(2,1)} %collective-permute-done.2.refs_3_, ...), custom_call_target="tpu_custom_call", output_to_operand_aliasing={{}: (9, {})} | custom-call | tf_op jit(solution)/shard_map/pallas_call | solution.py:412
  (7 shorter events, 0.0 us)
Async XLA Ops:
  0.0 4.4 %copy-start = (s32[64,1]{0,1:T(1,128)S(1)}, s32[64,1]{0,1:T(1,128)}, u32[]{:S(2)}) copy-start(s32[64,1]{0,1:T(1,128)} %param.8) | copy-start | bytes 772
  0.0 4.4 %copy-start.3 = (s32[64]{0:T(128)S(1)}, s32[64]{0:T(128)}, u32[]{:S(2)}) copy-start(s32[64]{0:T(128)} %param.7) | copy-start | bytes 772
  1.3 49.1 %collective-permute-start.1 = (bf16[2560,256]{1,0:T(8,128)(2,1)S(1)}, bf16[2560,256]{1,0:T(8,128)(2,1)S(1)}, u32[]{:S(2)}, u32[]{:S(2)}) collective-permute-start(bf16[2560,256]{1,0:T(8,128)(2,1)S(1)} %cut.1.refs_0_), channel_id=1, source_target_pairs={{0,2},{1,3},{2,0},{3,1},{4,6},{5,7},{6,4},{7,5},{8,10},{9,11},{10,... | collective-permute-start | bytes 3932168 | tf_op jit(solution)/shard_map/ppermute | solution.py:269
  4.4 58.9 %copy-start.1 = (f32[256]{0:T(256)S(1)}, f32[256]{0:T(256)}, u32[]{:S(2)}) copy-start(f32[256]{0:T(256)} %param.9) | copy-start | bytes 3076
  4.4 58.9 %copy-start.2 = (f32[256]{0:T(256)S(1)}, f32[256]{0:T(256)}, u32[]{:S(2)}) copy-start(f32[256]{0:T(256)} %param.10) | copy-start | bytes 3076
  10.7 39.6 %collective-permute-start.6 = (bf16[1536,256]{1,0:T(8,128)(2,1)}, bf16[1536,256]{1,0:T(8,128)(2,1)S(1)}, u32[]{:S(2)}, u32[]{:S(2)}) collective-permute-start(bf16[1536,256]{1,0:T(8,128)(2,1)} %get-tuple-element.21), channel_id=1, source_target_pairs={{0,1},{1,2},{2,3},{3,0},{4,5},{5,6},{6,7},{7,4},{8,9},{9,10},{10,1... | collective-permute-start | bytes 2359304 | tf_op jit(solution)/shard_map/ppermute | solution.py:269
  11.4 39.0 %collective-permute-start.7 = (bf16[1536,256]{1,0:T(8,128)(2,1)}, bf16[1536,256]{1,0:T(8,128)(2,1)S(1)}, u32[]{:S(2)}, u32[]{:S(2)}) collective-permute-start(bf16[1536,256]{1,0:T(8,128)(2,1)} %get-tuple-element.22), channel_id=1, source_target_pairs={{0,3},{1,0},{2,1},{3,2},{4,7},{5,4},{6,5},{7,6},{8,11},{9,8},{10,9... | collective-permute-start | bytes 2359304 | tf_op jit(solution)/shard_map/ppermute | solution.py:269
  51.5 47.5 %collective-permute-start.8 = (bf16[512,1024]{1,0:T(8,128)(2,1)}, bf16[512,1024]{1,0:T(8,128)(2,1)}, u32[]{:S(2)}, u32[]{:S(2)}) collective-permute-start(bf16[512,1024]{1,0:T(8,128)(2,1)} %stack.1.refs_0_), channel_id=1, source_target_pairs={{0,4},{4,0},{8,12},{12,8},{16,20},{20,16},{24,28},{28,24},{32,36},... | collective-permute-start | bytes 3145736 | tf_op jit(solution)/shard_map/ppermute | solution.py:377
  51.5 23.6 %all-to-all-start = ((bf16[64,16,128]{2,1,0:T(8,128)(2,1)}), bf16[64,16,128]{2,1,0:T(8,128)(2,1)S(1)}, u32[]{:S(2)}, u32[]{:S(2)}) async-start(bf16[64,16,128]{2,1,0:T(8,128)(2,1)} %bitcast.2), calls=%async_computation | async-start | bytes 524288 | tf_op jit(solution)/shard_map/all_to_all | solution.py:341
  76.5 18.0 %all-to-all-start.1 = ((bf16[64,16,128]{2,1,0:T(8,128)(2,1)}), bf16[64,16,128]{2,1,0:T(8,128)(2,1)S(1)}, u32[]{:S(2)}, u32[]{:S(2)}) async-start(bf16[64,16,128]{2,1,0:T(8,128)(2,1)} %bitcast.15), calls=%async_computation.1 | async-start | bytes 524288 | tf_op jit(solution)/shard_map/all_to_all | solution.py:341
  82.7 25.3 %collective-permute-start = (bf16[1024,256]{1,0:T(8,128)(2,1)}, bf16[1024,256]{1,0:T(8,128)(2,1)}, u32[]{:S(2)}, u32[]{:S(2)}) collective-permute-start(bf16[1024,256]{1,0:T(8,128)(2,1)} %get-tuple-element.14), channel_id=1, source_target_pairs={{0,1},{1,2},{2,3},{3,0},{4,5},{5,6},{6,7},{7,4},{8,9},{9,10},{10,1... | collective-permute-start | bytes 1572872 | tf_op jit(solution)/shard_map/ppermute | solution.py:269
  84.3 23.7 %collective-permute-start.2 = (bf16[1024,256]{1,0:T(8,128)(2,1)}, bf16[1024,256]{1,0:T(8,128)(2,1)}, u32[]{:S(2)}, u32[]{:S(2)}) collective-permute-start(bf16[1024,256]{1,0:T(8,128)(2,1)} %get-tuple-element.15), channel_id=1, source_target_pairs={{0,3},{1,0},{2,1},{3,2},{4,7},{5,4},{6,5},{7,6},{8,11},{9,8},{10,9... | collective-permute-start | bytes 1572872 | tf_op jit(solution)/shard_map/ppermute | solution.py:269
  94.9 8.1 %collective-permute-start.3 = (bf16[16,768]{1,0:T(8,128)(2,1)S(1)}, bf16[16,768]{1,0:T(8,128)(2,1)S(1)}, u32[]{:S(2)}, u32[]{:S(2)}) collective-permute-start(bf16[16,768]{1,0:T(8,128)(2,1)S(1)} %get-tuple-element.18), channel_id=1, source_target_pairs={{0,1},{1,2},{2,3},{3,0},{4,5},{5,6},{6,7},{7,4},{8,9},{9,10},{10,1... | collective-permute-start | bytes 73736 | tf_op jit(solution)/shard_map/ppermute | solution.py:269
  96.4 6.6 %collective-permute-start.4 = (bf16[16,768]{1,0:T(8,128)(2,1)S(1)}, bf16[16,768]{1,0:T(8,128)(2,1)S(1)}, u32[]{:S(2)}, u32[]{:S(2)}) collective-permute-start(bf16[16,768]{1,0:T(8,128)(2,1)S(1)} %get-tuple-element.19), channel_id=1, source_target_pairs={{0,2},{1,3},{2,0},{3,1},{4,6},{5,7},{6,4},{7,5},{8,10},{9,11},{10,... | collective-permute-start | bytes 73736 | tf_op jit(solution)/shard_map/ppermute | solution.py:269
  99.0 3.9 %collective-permute-start.5 = (bf16[16,768]{1,0:T(8,128)(2,1)S(1)}, bf16[16,768]{1,0:T(8,128)(2,1)S(1)}, u32[]{:S(2)}, u32[]{:S(2)}) collective-permute-start(bf16[16,768]{1,0:T(8,128)(2,1)S(1)} %get-tuple-element.20), channel_id=1, source_target_pairs={{0,3},{1,0},{2,1},{3,2},{4,7},{5,4},{6,5},{7,6},{8,11},{9,8},{10,9... | collective-permute-start | bytes 73736 | tf_op jit(solution)/shard_map/ppermute | solution.py:269

commit v7 on v5

v7 whole, which is shorter than its diff:
```python
import jax
import jax.numpy as jnp
from jax import lax
from jax.experimental import pallas as pl
from jax.experimental.pallas import tpu as pltpu
from jax.sharding import PartitionSpec as P


GRP_DEV = 32
PRIOR = 256.0
LANES = 128
MSG = 16
F32 = jnp.float32
BF16 = jnp.bfloat16
MIB = 1 << 20


def iota(shape, dim):
    return lax.broadcasted_iota(jnp.int32, shape, dim)


def exact_dot(one_hot, rows):
    return jnp.dot(one_hot.astype(BF16), rows.astype(BF16), preferred_element_type=F32)


def as_column(row, size, at):
    picked = jnp.where(at == iota((size, size), 1), jnp.broadcast_to(row, (size, size)), 0.0)
    return jnp.sum(picked, axis=1, keepdims=True)


def places(owner_row):
    size = owner_row.shape[1]
    column = as_column(owner_row, size, iota((size, size), 0))
    same = column == jnp.broadcast_to(owner_row, (size, size))
    earlier = iota((size, size), 0) < iota((size, size), 1)
    return jnp.sum(jnp.where(same & earlier, 1.0, 0.0), axis=0, keepdims=True)


def put(scratch, part, peers, at):
    for n in range(part.shape[1] // LANES):
        scratch[pl.ds(at + n, peers, stride=MSG), :] = part[:, n * LANES : (n + 1) * LANES]


def take(scratch, peers, at, count):
    return jnp.concatenate([scratch[pl.ds(at + n, peers, stride=MSG), :] for n in range(count)], axis=1)


def run(copies):
    for copy in copies:
        copy.start()
    for copy in copies:
        copy.wait()


def slab_of(depth, slabs):
    index = lax.axis_index("shuf")
    return lax.rem(index // (2 * depth), slabs // 2) * 2 + lax.rem(index, 2)


def cut_kernel(values, weight, out, out_slab, sems, *, rows, blocks, depth):
    slab, cols = out_slab.shape[0], values.shape[1]
    first = pl.multiple_of(lax.rem(lax.axis_index("rep") + 2, blocks) * rows, rows)
    mine = pl.multiple_of(slab_of(depth, weight.shape[0] // slab) * slab, slab)
    copies = [
        pltpu.make_async_copy(values.at[pl.ds(first, rows), :], out.at[pl.ds(blocks * slab, rows), :], sems.at[blocks]),
        pltpu.make_async_copy(weight.at[pl.ds(mine, slab), :], out_slab, sems.at[blocks + 1]),
    ]
    for n in range(blocks):
        source = weight.at[pl.ds(mine, slab), pl.ds(n * cols, cols)]
        copies.append(pltpu.make_async_copy(source, out.at[pl.ds(n * slab, slab), :], sems.at[n]))
    run(copies)


def stack_kernel(own, one, two, three, out):
    slab, cols = own.shape[0], two.shape[1]
    for n, part in ((0, own), (1, one), (3, three)):
        out[n * slab : (n + 1) * slab, :] = part[...]
    for c in range(own.shape[1] // cols):
        out[2 * slab : 3 * slab, c * cols : (c + 1) * cols] = two[c * slab : (c + 1) * slab, :]


def assemble_kernel(mine, sibling, across, across_sibling, out, *, blocks, cols, depth):
    slab = mine.shape[0] // blocks
    slabs = cols // slab
    first = slab_of(depth, slabs)
    core = lax.rem(first, 2)
    parts = (
        (mine, first),
        (sibling, first + 1 - 2 * core),
        (across, lax.rem(first + 2, slabs)),
        (across_sibling, lax.rem(first + 2, slabs) + 1 - 2 * core),
    )
    for part, number in parts:
        for n in range(blocks):
            at = pl.multiple_of(n * cols + number * slab, slab)
            out[pl.ds(at, slab), :] = part[n * slab : (n + 1) * slab, :]


def stats_kernel(values, two, owner, sub, out, one, three, *scratches, tiles, peers):
    held_rows, first, second, scratch, sems_in, sems_out = scratches
    rows, cols = one.shape
    blocks, pieces = 4, 2
    here, size = tiles // blocks, rows // pieces
    rank = lax.axis_index("rep")
    tile_rows = rows // here
    chunk = 16
    places_of = {1: held_rows.at[0], 3: held_rows.at[1], 0: held_rows.at[2]}

    def inward(d, p):
        at = pl.multiple_of(lax.rem(rank + d, blocks) * rows + p * size, size)
        target = places_of[d].at[pl.ds(p * size, size), :]
        return pltpu.make_async_copy(values.at[pl.ds(at, size), :], target, sems_in.at[d, p])

    for d in (1, 3, 0):
        for p in range(pieces):
            inward(d, p).start()

    def moments_of(source, d, p):
        def one_tile(t, carry):
            low = high = None
            for n in range(tile_rows // chunk):
                at = pl.multiple_of(t * tile_rows + n * chunk, chunk)
                wide = source[pl.ds(at, chunk), :].astype(F32)
                low, high = (wide, wide * wide) if low is None else (low + wide, high + wide * wide)
            tile = lax.rem(rank + d, blocks) * here + p * (here // pieces) + t
            at = pl.multiple_of(tile * 8, 8)
            for n in range(cols // LANES):
                lanes = slice(n * LANES, (n + 1) * LANES)
                first[n, pl.ds(at, 8), :] = low[:8, lanes] + low[8:, lanes]
                second[n, pl.ds(at, 8), :] = high[:8, lanes] + high[8:, lanes]
            return carry

        lax.fori_loop(0, here // pieces, one_tile, 0, unroll=2)

    skipped = two.shape[0] - rows
    for p in range(pieces):
        moments_of(two.at[pl.ds(skipped + p * size, size), :], 2, p)
    outward = []
    for d in (1, 3, 0):
        for p in range(pieces):
            inward(d, p).wait()
            if d and p == pieces - 1:
                outward.append(pltpu.make_async_copy(places_of[d], one if d == 1 else three, sems_out.at[d // 2]))
                outward[-1].start()
            moments_of(places_of[d].at[pl.ds(p * size, size), :], d, p)

    def folded(ref):
        halves = []
        for n in range(cols // LANES):
            summed = [ref[n, pl.ds(r, tiles, stride=8), :] for r in range(8)]
            while len(summed) > 1:
                summed = [a + b for a, b in zip(summed[::2], summed[1::2])]
            halves.append(summed[0])
        return jnp.concatenate(halves, axis=1) * (1.0 / tile_rows)

    all_mean = folded(first)
    all_var = folded(second) - all_mean * all_mean
    dev_mean = jnp.sum(all_mean, axis=0, keepdims=True) * (1.0 / tiles)
    apart = all_mean - dev_mean
    dev_var = jnp.sum(all_var + apart * apart, axis=0, keepdims=True) * (1.0 / tiles)
    owner_row = owner[...].astype(F32)
    place = places(owner_row)
    named = jnp.broadcast_to(owner_row, (peers, tiles)) == iota((peers, tiles), 0).astype(F32)
    sub_column = as_column(sub[...].astype(F32), tiles, iota((tiles, tiles), 0))
    sub_wide = jnp.broadcast_to(sub_column + 1.0, (tiles, LANES))
    hot = jnp.concatenate([jnp.where(named & (place == float(slot)), 1.0, 0.0) for slot in range(2)], axis=0)
    sent = exact_dot(hot, jnp.concatenate([all_mean, all_var, sub_wide], axis=1))
    for slot in range(2):
        message = sent[slot * peers : (slot + 1) * peers, :]
        put(scratch, message[:, : 2 * cols], peers, 4 * slot)
        put(scratch, message[:, 2 * cols :] - 1.0, peers, 14 + slot)
    high = dev_mean.astype(BF16).astype(F32)
    put(scratch, jnp.broadcast_to(high, (peers, cols)), peers, 8)
    put(scratch, jnp.broadcast_to(dev_mean - high, (peers, cols)), peers, 10)
    put(scratch, jnp.broadcast_to(dev_var, (peers, cols)), peers, 12)
    out[...] = scratch[...].astype(BF16)
    for copy in outward:
        copy.wait()


def pair_kernel(gain, bias, out):
    out[0:1, :] = gain[...]
    out[1:2, :] = bias[...]


def owner_kernel(arrived, both, out, scratch, *, peers, tile_rows):
    scratch[...] = arrived[...].astype(F32)
    dev_mean = take(scratch, peers, 8, 2) + take(scratch, peers, 10, 2)
    mean_all = jnp.sum(dev_mean, axis=0, keepdims=True) * (1.0 / peers)
    apart = dev_mean - mean_all
    var_all = jnp.sum(take(scratch, peers, 12, 2) + apart * apart, axis=0, keepdims=True) * (1.0 / peers)
    cols = dev_mean.shape[1]
    forth, back, firsts, seconds = [], [], [], []
    for slot in range(2):
        label = take(scratch, peers, 14 + slot, 1)
        back.append(jnp.where(label[:, :GRP_DEV] == iota((peers, GRP_DEV), 1).astype(F32), 1.0, 0.0))
        on_diagonal = iota((peers, peers), 0) == iota((peers, peers), 1)
        row = jnp.sum(jnp.where(on_diagonal, label[:, :peers], 0.0), axis=0, keepdims=True)
        wide = jnp.broadcast_to(row, (GRP_DEV, peers))
        forth.append(jnp.where(wide == iota((GRP_DEV, peers), 0).astype(F32), 1.0, 0.0))
        shifted = take(scratch, peers, 4 * slot, 2) - mean_all
        firsts.append(shifted)
        seconds.append(take(scratch, peers, 4 * slot + 2, 2) + shifted * shifted)
    forth = jnp.concatenate(forth, axis=1)
    count = jnp.sum(forth, axis=1, keepdims=True) * float(tile_rows)
    data = jnp.concatenate([jnp.concatenate(firsts, axis=0), jnp.concatenate(seconds, axis=0)], axis=1)
    high = data.astype(BF16).astype(F32)
    middle = (data - high).astype(BF16).astype(F32)
    parts = exact_dot(forth, jnp.concatenate([high, middle, data - high - middle], axis=1))
    sums = (parts[:, : 2 * cols] + parts[:, 2 * cols : 4 * cols] + parts[:, 4 * cols :]) * float(tile_rows)
    portion = 1.0 / (count + PRIOR)
    center = sums[:, :cols] * portion
    second = (sums[:, cols:] + PRIOR * var_all) * portion
    inverse = lax.rsqrt(second - center * center + 1e-05)
    scale = (inverse * both[0:1, :]).astype(BF16).astype(F32)
    shift = both[1:2, :] - (center + mean_all) * scale
    shift_high = shift.astype(BF16).astype(F32)
    reply = exact_dot(
        jnp.concatenate(back, axis=0), jnp.concatenate([scale, shift_high, shift - shift_high], axis=1)
    )
    for slot in range(2):
        put(scratch, reply[slot * peers : (slot + 1) * peers, :], peers, 6 * slot)
    out[...] = scratch[...].astype(BF16)


def tile_kernel(arrived, owner, *refs, tiles, peers, blocks):
    outs, scratch = refs[:-1], refs[-1]
    scratch[...] = arrived[...].astype(F32)
    owner_row = owner[...].astype(F32)
    at = (iota((tiles, tiles), 0) + lax.axis_index("rep") * (tiles // blocks)) % tiles
    place = as_column(places(owner_row), tiles, at)
    named = as_column(owner_row, tiles, at) == iota((tiles, peers), 1).astype(F32)
    hot = jnp.concatenate([jnp.where(named & (place == float(slot)), 1.0, 0.0) for slot in range(2)], axis=1)
    rows = jnp.concatenate([take(scratch, peers, 6 * slot, 6) for slot in range(2)], axis=0)
    picked = exact_dot(hot, rows)
    each = tiles // blocks
    for n, out in enumerate(outs):
        out[...] = picked[n * each : (n + 1) * each, :].astype(BF16)


def project_kernel(*refs, blocks, tile_rows, block, skipped):
    moved, coeffs, weight, out = refs[:blocks], refs[blocks : 2 * blocks], refs[2 * blocks], refs[2 * blocks + 1]
    held_rows, result, wide, sems_in, sems_out = refs[-5:]
    _, rows, cols = held_rows.shape
    skipped = (lax.axis_index("rep") * rows, *skipped)
    tiles = block // tile_rows
    steps = rows // block

    def inward(n, j):
        source = moved[n].at[pl.ds(pl.multiple_of(skipped[n] + j * block, block), block), :]
        return pltpu.make_async_copy(source, held_rows.at[n, pl.ds(j * block, block), :], sems_in.at[n, j])

    def outward(j):
        part = pl.ds(j * block, block)
        return pltpu.make_async_copy(result.at[part, :], out.at[part, :], sems_out.at[j])

    for j in range(steps):
        for n in range(blocks):
            inward(n, j).start()
    for n in range(blocks):
        wide[n] = coeffs[n][...].astype(F32)
    for j in range(steps):
        for n in range(blocks):
            inward(n, j).wait()
        strips = []
        for t in range(tiles):
            at = j * block + t * tile_rows
            parts = []
            for n in range(blocks):
                row = wide[n, j * tiles + t : j * tiles + t + 1, :]
                value = held_rows[n, at : at + tile_rows, :]
                scored = value.astype(F32) * row[:, :cols] + (row[:, cols : 2 * cols] + row[:, 2 * cols :])
                parts.append(scored.astype(BF16))
            strips.append(jnp.concatenate(parts, axis=1))
        product = jnp.dot(jnp.concatenate(strips, axis=0), weight[...], preferred_element_type=F32)
        result[j * block : (j + 1) * block, :] = product.astype(BF16)
        outward(j).start()
    for j in range(steps):
        outward(j).wait()


def hop(value, axis, distance):
    size = lax.axis_size(axis)
    return lax.ppermute(value, axis, [(i, (i + distance) % size) for i in range(size)])


def whole(*shape):
    return pl.BlockSpec(shape, lambda *_: (0,) * len(shape))


IN_VMEM = pl.BlockSpec(memory_space=pltpu.VMEM)
IN_SMEM = pl.BlockSpec(memory_space=pltpu.SMEM)
IN_HBM = pl.BlockSpec(memory_space=pltpu.HBM)


def limit(mib):
    return pltpu.CompilerParams(vmem_limit_bytes=mib * MIB)


def held(value):
    return pltpu.with_memory_space_constraint(value, pltpu.VMEM)


def off_chip(value):
    return pltpu.with_memory_space_constraint(value, pltpu.HBM)


IN_ANY = pl.BlockSpec(memory_space=pl.ANY)


def on_device(values, subgroup, owners, col_gain, col_bias, out_weight):
    rows, cols = values.shape
    tiles = subgroup.shape[0]
    tile_rows = rows // tiles
    peers, blocks = lax.axis_size("shuf"), lax.axis_size("rep")
    own_rows = rows // blocks
    outputs = out_weight.shape[1]
    owner_row, sub_row = owners.reshape(1, tiles), subgroup.reshape(1, tiles)

    depth = max(1, peers // 8)
    slab = cols // 4
    moved = {}
    two, own_slab = pl.pallas_call(
        lambda *refs: cut_kernel(*refs, rows=own_rows, blocks=blocks, depth=depth),
        in_specs=[IN_HBM, IN_HBM],
        out_specs=[IN_VMEM] * 2,
        out_shape=[pltpu.VMEM((cols + own_rows, cols), BF16), pltpu.VMEM((slab, outputs), BF16)],
        scratch_shapes=[pltpu.SemaphoreType.DMA((blocks + 2,))],
        compiler_params=limit(2),
        name="cut",
    )(off_chip(values), off_chip(out_weight))
    moved[2] = hop(two, "rep", 2)

    outgoing, one, three = pl.pallas_call(
        lambda *refs: stats_kernel(*refs, tiles=tiles, peers=peers),
        grid=(1,),
        in_specs=[IN_HBM, IN_VMEM, whole(1, tiles), whole(1, tiles)],
        out_specs=[whole(peers * MSG, LANES), IN_HBM, IN_HBM],
        scratch_shapes=[
            pltpu.VMEM((3, own_rows, cols), BF16),
            pltpu.VMEM((cols // LANES, tiles * 8, LANES), F32),
            pltpu.VMEM((cols // LANES, tiles * 8, LANES), F32),
            pltpu.VMEM((peers * MSG, LANES), F32),
            pltpu.SemaphoreType.DMA((blocks, 2)),
            pltpu.SemaphoreType.DMA((2,)),
        ],
        out_shape=[
            pltpu.HBM((peers * MSG, LANES), BF16), pltpu.HBM((own_rows, cols), BF16), pltpu.HBM((own_rows, cols), BF16)
        ],
        compiler_params=limit(8),
        name="stats",
    )(off_chip(values), held(two), owner_row, sub_row)

    def exchange(message):
        arrived = lax.all_to_all(message.reshape(peers, MSG, LANES), "shuf", 0, 0, tiled=True)
        return held(arrived.reshape(peers * MSG, LANES))

    arrived = exchange(outgoing)

    slabs = {0: own_slab}
    for d in (1, 3):
        slabs[d] = hop(own_slab, "rep", d)
    for d, sent in ((1, one), (3, three)):
        moved[d] = hop(sent, "rep", d)

    both = pl.pallas_call(
        pair_kernel,
        out_shape=jax.ShapeDtypeStruct((2, cols), F32),
        compiler_params=limit(1),
        name="pair",
    )(col_gain.reshape(1, cols), col_bias.reshape(1, cols))
    answer = pl.pallas_call(
        lambda *refs: owner_kernel(*refs, peers=peers, tile_rows=tile_rows),
        in_specs=[IN_VMEM, whole(2, cols)],
        out_shape=pltpu.HBM((peers * MSG, LANES), BF16),
        scratch_shapes=[pltpu.VMEM((peers * MSG, LANES), F32)],
        compiler_params=limit(6),
        name="moments",
    )(arrived, both)
    returned = exchange(answer)

    def trade(value, distance):
        return lax.ppermute(value, "shuf", [(i, i ^ distance) for i in range(peers)])

    mine = pl.pallas_call(
        stack_kernel,
        grid=(1,),
        in_specs=[whole(slab, outputs), whole(slab, outputs), whole(cols, cols), whole(slab, outputs)],
        out_specs=whole(cols, outputs),
        out_shape=pltpu.HBM((cols, outputs), BF16),
        compiler_params=limit(8),
        name="stack",
    )(slabs[0], slabs[1], moved[2], slabs[3])
    across = trade(mine, 2 * depth)
    sibling = trade(mine, 1)
    across_sibling = trade(across, 1)
    weight = pl.pallas_call(
        lambda *refs: assemble_kernel(*refs, blocks=blocks, cols=cols, depth=depth),
        grid=(1,),
        in_specs=[whole(cols, outputs)] * 3 + [IN_VMEM],
        out_specs=IN_VMEM,
        out_shape=pltpu.VMEM((blocks * cols, outputs), BF16),
        compiler_params=limit(8),
        name="assemble",
    )(mine, sibling, across, held(across_sibling))

    each = tiles // blocks
    coeffs = pl.pallas_call(
        lambda *refs: tile_kernel(*refs, tiles=tiles, peers=peers, blocks=blocks),
        in_specs=[IN_VMEM, whole(1, tiles)],
        out_specs=[IN_VMEM] * blocks,
        out_shape=[pltpu.VMEM((each, 3 * cols), BF16)] * blocks,
        scratch_shapes=[pltpu.VMEM((peers * MSG, LANES), F32)],
        compiler_params=limit(4),
        name="pick",
    )(returned, owner_row)
    known = {0: coeffs[0]}
    for d in (2, 1, 3):
        known[d] = hop(coeffs[d], "rep", d)

    block = min(256, own_rows)
    return pl.pallas_call(
        lambda *refs: project_kernel(
            *refs, blocks=blocks, tile_rows=tile_rows, block=block, skipped=(0, two.shape[0] - own_rows, 0)
        ),
        in_specs=[IN_HBM] * blocks + [IN_VMEM] * (blocks + 1),
        out_specs=IN_HBM,
        out_shape=pltpu.HBM((own_rows, outputs), BF16),
        scratch_shapes=[
            pltpu.VMEM((blocks, own_rows, cols), BF16),
            pltpu.VMEM((own_rows, outputs), BF16),
            pltpu.VMEM((blocks, each, 3 * cols), F32),
            pltpu.SemaphoreType.DMA((blocks, own_rows // block)),
            pltpu.SemaphoreType.DMA((own_rows // block,)),
        ],
        compiler_params=limit(24),
        name="project",
    )(
        off_chip(values),
        *[off_chip(moved[d]) for d in range(1, blocks)],
        *[held(known[d]) for d in range(blocks)],
        held(weight),
    )


def solution(mesh):
    return jax.shard_map(
        on_device,
        mesh=mesh,
        in_specs=(P("shuf", "rep"), P("shuf"), P("shuf", None), P("rep"), P("rep"), P("rep", None)),
        out_specs=P(("shuf", "rep"), None),
        check_vma=False,
    )
```

time: 107 us -> 99.4 us (0.929)
  Pallas kernels: 20.9 us -> 15.5 us
  waiting for transfers between devices: 40.1 us -> 37.2 us
    pallas_call x1, Pallas kernels: 6.45 us -> 3.37 us  [on_device(): pl.pallas_call(lambda *refs: stats_kernel(*refs, tiles=tiles, peers=peers...]
    ppermute x9 -> x8, waiting for transfers between devices: 32.2 us -> 29.3 us  [hop(): lax.ppermute(value, axis, [(i, (i + distance) % size) for i in range(size)])]
    ppermute x1 -> x3, starting transfers between devices: 0.01 us -> 2.08 us  [trade(): lax.ppermute(value, 'shuf', [(i, i ^ distance) for i in range(peers)])]
    pallas_call x1, Pallas kernels: 1.77 us -> 0.18 us  [on_device(): pl.pallas_call(lambda *refs: assemble_kernel(*refs, blocks=blocks, cols=c...]
    ppermute x9 -> x8, starting transfers between devices: 15.4 us -> 14 us  [hop(): lax.ppermute(value, axis, [(i, (i + distance) % size) for i in range(size)])]
  transfers between devices with their start and end apart: 11 -> 12, of which waited for: 4 -> 4; matrix products, arithmetic and copies ran while one was open for 0% -> 0% of each run, Pallas kernels for 10% -> 5%
where the time goes in v7:
time: 99.4 us; the launch traced here: 98.6 us
  waiting for transfers between devices  37.2 us (37%)
  starting transfers between devices  27.6 us (28%)
  blocking collectives  18 us (18%)
  Pallas kernels  15.5 us (16%)
    ppermute x8, waiting for transfers between devices, hop(): lax.ppermute(value, axis, [(i, (i + distance) % size) for i in range(size)])  29.3 us
    all_to_all x1, blocking collectives, exchange(): lax.all_to_all(message.reshape(peers, MSG, LANES), 'shuf', 0, 0, tiled=True)  18 us
    ppermute x8, starting transfers between devices, hop(): lax.ppermute(value, axis, [(i, (i + distance) % size) for i in range(size)])  14 us
    all_to_all x1, starting transfers between devices, exchange(): lax.all_to_all(message.reshape(peers, MSG, LANES), 'shuf', 0, 0, tiled=True)  11.5 us
    pallas_call x1, Pallas kernels, on_device(): pl.pallas_call(lambda *refs: project_kernel(*refs, blocks=blocks, tile_ro...  8.07 us
    all_to_all x1, waiting for transfers between devices, exchange(): lax.all_to_all(message.reshape(peers, MSG, LANES), 'shuf', 0, 0, tiled=True)  7.87 us
    pallas_call x1, Pallas kernels, on_device(): pl.pallas_call(lambda *refs: stats_kernel(*refs, tiles=tiles, peers=peers...  3.37 us
    ppermute x3, starting transfers between devices, trade(): lax.ppermute(value, 'shuf', [(i, i ^ distance) for i in range(peers)])  2.08 us
  transfers between devices with their start and end apart: 12, of which 4 were waited for; matrix products, arithmetic and copies ran while one was open for 0% of the time, Pallas kernels for 5%

profile of v7, /device:TPU:32, one launch (start us, length us, event | category | flops | bytes accessed | tf_op | source)
XLA Modules:
  0.0 98.6 jit_solution(1759854180375640341)
XLA Ops:
  0.0 1.3 %cut.1 = (bf16[2304,256]{1,0:T(8,128)(2,1)S(1)}, bf16[64,1024]{1,0:T(8,128)(2,1)S(1)}) custom-call(bf16[8192,256]{1,0:T(8,128)(2,1)} %refs_0_.5, bf16[256,1024]{1,0:T(8,128)(2,1)} %refs_1_.1), custom_call_target="tpu_custom_call" | custom-call | tf_op jit(solution)/shard_map/cut/pallas_call | solution.py:323
  1.3 0.0 copy-start.2
  1.3 0.0 copy-start.5
  1.3 3.1 %collective-permute-start.1 = (bf16[2304,256]{1,0:T(8,128)(2,1)S(1)}, bf16[2304,256]{1,0:T(8,128)(2,1)S(1)}, u32[]{:S(2)}, u32[]{:S(2)}) collective-permute-start(bf16[2304,256]{1,0:T(8,128)(2,1)S(1)} %get-tuple-element.14.refs_1_), channel_id=1, source_target_pairs={{0,2},{1,3},{2,0},{3,1},{4,6},{5,7},{6,4},{7,5},{8,10},{9,11},{10,... | collective-permute-start | bytes 3538952 | tf_op jit(solution)/shard_map/ppermute | solution.py:284
  4.4 1.1 %collective-permute-start.7 = (bf16[64,1024]{1,0:T(8,128)(2,1)S(1)}, bf16[64,1024]{1,0:T(8,128)(2,1)S(1)}, u32[]{:S(2)}, u32[]{:S(2)}) collective-permute-start(bf16[64,1024]{1,0:T(8,128)(2,1)S(1)} %get-tuple-element.22.own), channel_id=1, source_target_pairs={{0,3},{1,0},{2,1},{3,2},{4,7},{5,4},{6,5},{7,6},{8,11},{9,8},{10,9... | collective-permute-start | bytes 393224 | tf_op jit(solution)/shard_map/ppermute | solution.py:284
  5.6 0.9 collective-permute-start.6
  6.5 27.1 %collective-permute-done.7.three = bf16[64,1024]{1,0:T(8,128)(2,1)S(1)} collective-permute-done((bf16[64,1024]{1,0:T(8,128)(2,1)S(1)}, bf16[64,1024]{1,0:T(8,128)(2,1)S(1)}, u32[]{:S(2)}, u32[]{:S(2)}) %collective-permute-start.7) | collective-permute-done | bytes 131104 | tf_op jit(solution)/shard_map/ppermute | solution.py:284
  33.6 0.0 collective-permute-done.6.one
  33.6 0.9 stack.1.refs_0_
  34.5 1.6 %collective-permute-start.9 = (bf16[256,1024]{1,0:T(8,128)(2,1)}, bf16[256,1024]{1,0:T(8,128)(2,1)S(1)}, u32[]{:S(2)}, u32[]{:S(2)}) collective-permute-start(bf16[256,1024]{1,0:T(8,128)(2,1)} %stack.1.refs_0_), channel_id=1, source_target_pairs={{0,64},{4,68},{8,72},{12,76},{16,80},{20,84},{24,88},{28,92},{32,9... | collective-permute-start | bytes 1572872 | tf_op jit(solution)/shard_map/ppermute | solution.py:383
  36.0 0.0 copy-start.4
  36.1 3.4 %stats.1 = (bf16[1024,128]{1,0:T(8,128)(2,1)}, bf16[2048,256]{1,0:T(8,128)(2,1)}, bf16[2048,256]{1,0:T(8,128)(2,1)}) custom-call(bf16[8192,256]{1,0:T(8,128)(2,1)} %refs_0_.5, bf16[2304,256]{1,0:T(8,128)(2,1)S(1)} %get-tuple-element.14.refs_1_, s32[1,64]{1,0:T(1,128)S(1)} %bitcast.10, s32[1,64]{1,0:T(1,128)S(1)} %bitcast.14), custom_call_target="tpu_custom_call" | custom-call | tf_op jit(solution)/shard_map/stats/pallas_call | solution.py:334
  39.4 11.5 %all-to-all-start = ((bf16[64,16,128]{2,1,0:T(8,128)(2,1)}), bf16[64,16,128]{2,1,0:T(8,128)(2,1)S(1)}, u32[]{:S(2)}, u32[]{:S(2)}) async-start(bf16[64,16,128]{2,1,0:T(8,128)(2,1)} %bitcast.16), calls=%async_computation | async-start | bytes 524288 | tf_op jit(solution)/shard_map/all_to_all | solution.py:355
  50.9 1.5 %collective-permute-start = (bf16[2048,256]{1,0:T(8,128)(2,1)}, bf16[2048,256]{1,0:T(8,128)(2,1)S(1)}, u32[]{:S(2)}, u32[]{:S(2)}) collective-permute-start(bf16[2048,256]{1,0:T(8,128)(2,1)} %get-tuple-element.15), channel_id=1, source_target_pairs={{0,1},{1,2},{2,3},{3,0},{4,5},{5,6},{6,7},{7,4},{8,9},{9,10},{10,1... | collective-permute-start | bytes 3145736 | tf_op jit(solution)/shard_map/ppermute | solution.py:284
  52.4 1.8 %collective-permute-start.2 = (bf16[2048,256]{1,0:T(8,128)(2,1)}, bf16[2048,256]{1,0:T(8,128)(2,1)}, u32[]{:S(2)}, u32[]{:S(2)}) collective-permute-start(bf16[2048,256]{1,0:T(8,128)(2,1)} %get-tuple-element.16), channel_id=1, source_target_pairs={{0,3},{1,0},{2,1},{3,2},{4,7},{5,4},{6,5},{7,6},{8,11},{9,8},{10,9... | collective-permute-start | bytes 3145736 | tf_op jit(solution)/shard_map/ppermute | solution.py:284
  54.2 0.0 collective-permute-start.8
  54.3 0.0 collective-permute-done.9.refs_2_
  54.3 0.5 collective-permute-start.10
  54.8 7.9 %all-to-all-done = bf16[64,16,128]{2,1,0:T(8,128)(2,1)S(1)} async-done(((bf16[64,16,128]{2,1,0:T(8,128)(2,1)}), bf16[64,16,128]{2,1,0:T(8,128)(2,1)S(1)}, u32[]{:S(2)}, u32[]{:S(2)}) %all-to-all-start) | async-done | bytes 262176 | tf_op jit(solution)/shard_map/all_to_all | solution.py:355
  62.6 1.4 %moments.1 = bf16[1024,128]{1,0:T(8,128)(2,1)} custom-call(bf16[1024,128]{1,0:T(8,128)(2,1)S(1)} %bitcast.8, f32[2,256]{1,0:T(2,128)S(1)} %pair.1.refs_1_), custom_call_target="tpu_custom_call" | custom-call | tf_op jit(solution)/shard_map/moments/pallas_call | solution.py:372
  64.0 18.0 %all_to_all.10 = bf16[64,16,128]{2,1,0:T(8,128)(2,1)S(1)} all-to-all(bf16[64,16,128]{2,1,0:T(8,128)(2,1)} %bitcast.15), channel_id=1, replica_groups=mesh['shuf'=64,'rep'=4] {'shuf'}, dimensions={0} | all-to-all | bytes 524288 | tf_op jit(solution)/shard_map/all_to_all | solution.py:355
  82.0 0.4 pick.1
  82.4 1.5 %collective-permute-start.3 = (bf16[16,768]{1,0:T(8,128)(2,1)S(1)}, bf16[16,768]{1,0:T(8,128)(2,1)S(1)}, u32[]{:S(2)}, u32[]{:S(2)}) collective-permute-start(bf16[16,768]{1,0:T(8,128)(2,1)S(1)} %get-tuple-element.19), channel_id=1, source_target_pairs={{0,1},{1,2},{2,3},{3,0},{4,5},{5,6},{6,7},{7,4},{8,9},{9,10},{10,1... | collective-permute-start | bytes 73736 | tf_op jit(solution)/shard_map/ppermute | solution.py:284
  83.9 0.0 collective-permute-done.8.refs_1_
  83.9 2.7 %collective-permute-start.4 = (bf16[16,768]{1,0:T(8,128)(2,1)S(1)}, bf16[16,768]{1,0:T(8,128)(2,1)S(1)}, u32[]{:S(2)}, u32[]{:S(2)}) collective-permute-start(bf16[16,768]{1,0:T(8,128)(2,1)S(1)} %get-tuple-element.20), channel_id=1, source_target_pairs={{0,2},{1,3},{2,0},{3,1},{4,6},{5,7},{6,4},{7,5},{8,10},{9,11},{10,... | collective-permute-start | bytes 73736 | tf_op jit(solution)/shard_map/ppermute | solution.py:284
  86.6 0.0 collective-permute-done.10.refs_3_
  86.6 1.4 %collective-permute-start.5 = (bf16[16,768]{1,0:T(8,128)(2,1)S(1)}, bf16[16,768]{1,0:T(8,128)(2,1)S(1)}, u32[]{:S(2)}, u32[]{:S(2)}) collective-permute-start(bf16[16,768]{1,0:T(8,128)(2,1)S(1)} %get-tuple-element.21), channel_id=1, source_target_pairs={{0,3},{1,0},{2,1},{3,2},{4,7},{5,4},{6,5},{7,6},{8,11},{9,8},{10,9... | collective-permute-start | bytes 73736 | tf_op jit(solution)/shard_map/ppermute | solution.py:284
  88.0 0.2 assemble.1.refs_8_
  88.2 0.0 collective-permute-done.3.refs_5_
  88.2 1.0 %collective-permute-done.4.refs_6_ = bf16[16,768]{1,0:T(8,128)(2,1)S(1)} collective-permute-done((bf16[16,768]{1,0:T(8,128)(2,1)S(1)}, bf16[16,768]{1,0:T(8,128)(2,1)S(1)}, u32[]{:S(2)}, u32[]{:S(2)}) %collective-permute-start.4) | collective-permute-done | bytes 24608 | tf_op jit(solution)/shard_map/ppermute | solution.py:284
  89.2 1.2 %collective-permute-done.5.refs_7_ = bf16[16,768]{1,0:T(8,128)(2,1)S(1)} collective-permute-done((bf16[16,768]{1,0:T(8,128)(2,1)S(1)}, bf16[16,768]{1,0:T(8,128)(2,1)S(1)}, u32[]{:S(2)}, u32[]{:S(2)}) %collective-permute-start.5) | collective-permute-done | bytes 24608 | tf_op jit(solution)/shard_map/ppermute | solution.py:284
  90.4 8.1 %project.1 = bf16[2048,1024]{1,0:T(8,128)(2,1)} custom-call(bf16[8192,256]{1,0:T(8,128)(2,1)} %refs_0_.5, bf16[2048,256]{1,0:T(8,128)(2,1)} %copy-done.6, bf16[2304,256]{1,0:T(8,128)(2,1)} %copy-done, bf16[2048,256]{1,0:T(8,128)(2,1)} %collective-permute-done.2.refs_3_, bf16[16,768]{1,0:T(8,128)(2,1)S(1)} %get-tuple-element.18.refs_4_, ...), custom_call_target="tpu_custom_call" | custom-call | tf_op jit(solution)/shard_map/project/pallas_call | solution.py:422
  (15 shorter events, 0.0 us)
Async XLA Ops:
  1.3 34.7 %copy-start.2 = (s32[64,1]{0,1:T(1,128)S(1)}, s32[64,1]{0,1:T(1,128)}, u32[]{:S(2)}) copy-start(s32[64,1]{0,1:T(1,128)} %param.8) | copy-start | bytes 772
  1.3 34.7 %copy-start.5 = (s32[64]{0:T(128)S(1)}, s32[64]{0:T(128)}, u32[]{:S(2)}) copy-start(s32[64]{0:T(128)} %param.7) | copy-start | bytes 772
  1.3 32.2 %collective-permute-start.1 = (bf16[2304,256]{1,0:T(8,128)(2,1)S(1)}, bf16[2304,256]{1,0:T(8,128)(2,1)S(1)}, u32[]{:S(2)}, u32[]{:S(2)}) collective-permute-start(bf16[2304,256]{1,0:T(8,128)(2,1)S(1)} %get-tuple-element.14.refs_1_), channel_id=1, source_target_pairs={{0,2},{1,3},{2,0},{3,1},{4,6},{5,7},{6,4},{7,5},{8,10},{9,11},{10,... | collective-permute-start | bytes 3538952 | tf_op jit(solution)/shard_map/ppermute | solution.py:284
  4.4 29.1 %collective-permute-start.7 = (bf16[64,1024]{1,0:T(8,128)(2,1)S(1)}, bf16[64,1024]{1,0:T(8,128)(2,1)S(1)}, u32[]{:S(2)}, u32[]{:S(2)}) collective-permute-start(bf16[64,1024]{1,0:T(8,128)(2,1)S(1)} %get-tuple-element.22.own), channel_id=1, source_target_pairs={{0,3},{1,0},{2,1},{3,2},{4,7},{5,4},{6,5},{7,6},{8,11},{9,8},{10,9... | collective-permute-start | bytes 393224 | tf_op jit(solution)/shard_map/ppermute | solution.py:284
  5.6 28.0 %collective-permute-start.6 = (bf16[64,1024]{1,0:T(8,128)(2,1)S(1)}, bf16[64,1024]{1,0:T(8,128)(2,1)S(1)}, u32[]{:S(2)}, u32[]{:S(2)}) collective-permute-start(bf16[64,1024]{1,0:T(8,128)(2,1)S(1)} %get-tuple-element.22.own), channel_id=1, source_target_pairs={{0,1},{1,2},{2,3},{3,0},{4,5},{5,6},{6,7},{7,4},{8,9},{9,10},{10,1... | collective-permute-start | bytes 393224 | tf_op jit(solution)/shard_map/ppermute | solution.py:284
  33.6 5.9 %copy-start = (bf16[2304,256]{1,0:T(8,128)(2,1)}, bf16[2304,256]{1,0:T(8,128)(2,1)S(1)}, u32[]{:S(2)}) copy-start(bf16[2304,256]{1,0:T(8,128)(2,1)S(1)} %collective-permute-done.1.two.refs_2_) | copy-start | bytes 3538948
  34.5 19.8 %collective-permute-start.9 = (bf16[256,1024]{1,0:T(8,128)(2,1)}, bf16[256,1024]{1,0:T(8,128)(2,1)S(1)}, u32[]{:S(2)}, u32[]{:S(2)}) collective-permute-start(bf16[256,1024]{1,0:T(8,128)(2,1)} %stack.1.refs_0_), channel_id=1, source_target_pairs={{0,64},{4,68},{8,72},{12,76},{16,80},{20,84},{24,88},{28,92},{32,9... | collective-permute-start | bytes 1572872 | tf_op jit(solution)/shard_map/ppermute | solution.py:383
  36.0 18.2 %copy-start.1 = (bf16[256,1024]{1,0:T(8,128)(2,1)S(1)}, bf16[256,1024]{1,0:T(8,128)(2,1)}, u32[]{:S(2)}) copy-start(bf16[256,1024]{1,0:T(8,128)(2,1)} %stack.1.refs_0_) | copy-start | bytes 1572868
  36.0 18.7 %copy-start.3 = (f32[256]{0:T(256)S(1)}, f32[256]{0:T(256)}, u32[]{:S(2)}) copy-start(f32[256]{0:T(256)} %param.9) | copy-start | bytes 3076
  36.0 18.7 %copy-start.4 = (f32[256]{0:T(256)S(1)}, f32[256]{0:T(256)}, u32[]{:S(2)}) copy-start(f32[256]{0:T(256)} %param.10) | copy-start | bytes 3076
  39.4 23.2 %all-to-all-start = ((bf16[64,16,128]{2,1,0:T(8,128)(2,1)}), bf16[64,16,128]{2,1,0:T(8,128)(2,1)S(1)}, u32[]{:S(2)}, u32[]{:S(2)}) async-start(bf16[64,16,128]{2,1,0:T(8,128)(2,1)} %bitcast.16), calls=%async_computation | async-start | bytes 524288 | tf_op jit(solution)/shard_map/all_to_all | solution.py:355
  50.9 37.3 %collective-permute-start = (bf16[2048,256]{1,0:T(8,128)(2,1)}, bf16[2048,256]{1,0:T(8,128)(2,1)S(1)}, u32[]{:S(2)}, u32[]{:S(2)}) collective-permute-start(bf16[2048,256]{1,0:T(8,128)(2,1)} %get-tuple-element.15), channel_id=1, source_target_pairs={{0,1},{1,2},{2,3},{3,0},{4,5},{5,6},{6,7},{7,4},{8,9},{9,10},{10,1... | collective-permute-start | bytes 3145736 | tf_op jit(solution)/shard_map/ppermute | solution.py:284
  52.4 35.8 %collective-permute-start.2 = (bf16[2048,256]{1,0:T(8,128)(2,1)}, bf16[2048,256]{1,0:T(8,128)(2,1)}, u32[]{:S(2)}, u32[]{:S(2)}) collective-permute-start(bf16[2048,256]{1,0:T(8,128)(2,1)} %get-tuple-element.16), channel_id=1, source_target_pairs={{0,3},{1,0},{2,1},{3,2},{4,7},{5,4},{6,5},{7,6},{8,11},{9,8},{10,9... | collective-permute-start | bytes 3145736 | tf_op jit(solution)/shard_map/ppermute | solution.py:284
  54.2 29.7 %collective-permute-start.8 = (bf16[256,1024]{1,0:T(8,128)(2,1)S(1)}, bf16[256,1024]{1,0:T(8,128)(2,1)S(1)}, u32[]{:S(2)}, u32[]{:S(2)}) collective-permute-start(bf16[256,1024]{1,0:T(8,128)(2,1)S(1)} %copy-done.1), channel_id=1, source_target_pairs={{0,4},{4,0},{8,12},{12,8},{16,20},{20,16},{24,28},{28,24},{32,36},... | collective-permute-start | bytes 1572872 | tf_op jit(solution)/shard_map/ppermute | solution.py:383
  54.3 32.3 %collective-permute-start.10 = (bf16[256,1024]{1,0:T(8,128)(2,1)S(1)}, bf16[256,1024]{1,0:T(8,128)(2,1)S(1)}, u32[]{:S(2)}, u32[]{:S(2)}) collective-permute-start(bf16[256,1024]{1,0:T(8,128)(2,1)S(1)} %collective-permute-done.9.refs_2_), channel_id=1, source_target_pairs={{0,4},{4,0},{8,12},{12,8},{16,20},{20,16},{24,28},{28,24},{32,36},... | collective-permute-start | bytes 1572872 | tf_op jit(solution)/shard_map/ppermute | solution.py:383
  82.4 5.8 %collective-permute-start.3 = (bf16[16,768]{1,0:T(8,128)(2,1)S(1)}, bf16[16,768]{1,0:T(8,128)(2,1)S(1)}, u32[]{:S(2)}, u32[]{:S(2)}) collective-permute-start(bf16[16,768]{1,0:T(8,128)(2,1)S(1)} %get-tuple-element.19), channel_id=1, source_target_pairs={{0,1},{1,2},{2,3},{3,0},{4,5},{5,6},{6,7},{7,4},{8,9},{9,10},{10,1... | collective-permute-start | bytes 73736 | tf_op jit(solution)/shard_map/ppermute | solution.py:284
  83.9 5.3 %collective-permute-start.4 = (bf16[16,768]{1,0:T(8,128)(2,1)S(1)}, bf16[16,768]{1,0:T(8,128)(2,1)S(1)}, u32[]{:S(2)}, u32[]{:S(2)}) collective-permute-start(bf16[16,768]{1,0:T(8,128)(2,1)S(1)} %get-tuple-element.20), channel_id=1, source_target_pairs={{0,2},{1,3},{2,0},{3,1},{4,6},{5,7},{6,4},{7,5},{8,10},{9,11},{10,... | collective-permute-start | bytes 73736 | tf_op jit(solution)/shard_map/ppermute | solution.py:284
  86.6 3.8 %collective-permute-start.5 = (bf16[16,768]{1,0:T(8,128)(2,1)S(1)}, bf16[16,768]{1,0:T(8,128)(2,1)S(1)}, u32[]{:S(2)}, u32[]{:S(2)}) collective-permute-start(bf16[16,768]{1,0:T(8,128)(2,1)S(1)} %get-tuple-element.21), channel_id=1, source_target_pairs={{0,3},{1,0},{2,1},{3,2},{4,7},{5,4},{6,5},{7,6},{8,11},{9,8},{10,9... | collective-permute-start | bytes 73736 | tf_op jit(solution)/shard_map/ppermute | solution.py:284
  88.2 2.2 %copy-start.6 = (bf16[2048,256]{1,0:T(8,128)(2,1)}, bf16[2048,256]{1,0:T(8,128)(2,1)S(1)}, u32[]{:S(2)}) copy-start(bf16[2048,256]{1,0:T(8,128)(2,1)S(1)} %collective-permute-done.refs_1_) | copy-start | bytes 3145732

commit v8 on v7

--- a/solution.py
+++ b/solution.py
@@ -243,35 +243,38 @@
     held_rows, result, wide, sems_in, sems_out = refs[-5:]
     _, rows, cols = held_rows.shape
     skipped = (lax.axis_index("rep") * rows, *skipped)
+    parts = ((0, block), (block, rows - block)) if rows > block else ((0, rows),)
     tiles = block // tile_rows
     steps = rows // block
 
-    def inward(n, j):
-        source = moved[n].at[pl.ds(pl.multiple_of(skipped[n] + j * block, block), block), :]
-        return pltpu.make_async_copy(source, held_rows.at[n, pl.ds(j * block, block), :], sems_in.at[n, j])
+    def inward(n, p):
+        at, size = parts[p]
+        source = moved[n].at[pl.ds(pl.multiple_of(skipped[n] + at, tile_rows), size), :]
+        return pltpu.make_async_copy(source, held_rows.at[n, pl.ds(at, size), :], sems_in.at[n, p])
 
     def outward(j):
         part = pl.ds(j * block, block)
         return pltpu.make_async_copy(result.at[part, :], out.at[part, :], sems_out.at[j])
 
-    for j in range(steps):
+    for p in range(len(parts)):
         for n in range(blocks):
-            inward(n, j).start()
+            inward(n, p).start()
     for n in range(blocks):
         wide[n] = coeffs[n][...].astype(F32)
     for j in range(steps):
-        for n in range(blocks):
-            inward(n, j).wait()
+        if j < len(parts):
+            for n in range(blocks):
+                inward(n, j).wait()
         strips = []
         for t in range(tiles):
             at = j * block + t * tile_rows
-            parts = []
+            scores = []
             for n in range(blocks):
                 row = wide[n, j * tiles + t : j * tiles + t + 1, :]
                 value = held_rows[n, at : at + tile_rows, :]
                 scored = value.astype(F32) * row[:, :cols] + (row[:, cols : 2 * cols] + row[:, 2 * cols :])
-                parts.append(scored.astype(BF16))
-            strips.append(jnp.concatenate(parts, axis=1))
+                scores.append(scored.astype(BF16))
+            strips.append(jnp.concatenate(scores, axis=1))
         product = jnp.dot(jnp.concatenate(strips, axis=0), weight[...], preferred_element_type=F32)
         result[j * block : (j + 1) * block, :] = product.astype(BF16)
         outward(j).start()
@@ -397,12 +400,12 @@
     weight = pl.pallas_call(
         lambda *refs: assemble_kernel(*refs, blocks=blocks, cols=cols, depth=depth),
         grid=(1,),
-        in_specs=[whole(cols, outputs)] * 3 + [IN_VMEM],
+        in_specs=[whole(cols, outputs)] + [IN_VMEM] * 3,
         out_specs=IN_VMEM,
         out_shape=pltpu.VMEM((blocks * cols, outputs), BF16),
         compiler_params=limit(8),
         name="assemble",
-    )(mine, sibling, across, held(across_sibling))
+    )(off_chip(mine), held(sibling), held(across), held(across_sibling))
 
     each = tiles // blocks
     coeffs = pl.pallas_call(
@@ -418,7 +421,7 @@
     for d in (2, 1, 3):
         known[d] = hop(coeffs[d], "rep", d)
 
-    block = min(256, own_rows)
+    block = min(512, own_rows)
     return pl.pallas_call(
         lambda *refs: project_kernel(
             *refs, blocks=blocks, tile_rows=tile_rows, block=block, skipped=(0, two.shape[0] - own_rows, 0)
@@ -430,7 +433,7 @@
             pltpu.VMEM((blocks, own_rows, cols), BF16),
             pltpu.VMEM((own_rows, outputs), BF16),
             pltpu.VMEM((blocks, each, 3 * cols), F32),
-            pltpu.SemaphoreType.DMA((blocks, own_rows // block)),
+            pltpu.SemaphoreType.DMA((blocks, 2)),
             pltpu.SemaphoreType.DMA((own_rows // block,)),
         ],
         compiler_params=limit(24),

time: 99.4 us -> 98.4 us (0.990)
  waiting for transfers between devices: 37.2 us -> 36.1 us
    pallas_call x1, Pallas kernels: 8.07 us -> 6.99 us  [on_device(): pl.pallas_call(lambda *refs: project_kernel(*refs, blocks=blocks, tile_ro...]
    ppermute x8, waiting for transfers between devices: 29.3 us -> 28.2 us  [hop(): lax.ppermute(value, axis, [(i, (i + distance) % size) for i in range(size)])]
    pallas_call x1, Pallas kernels: 0.18 us -> 1.22 us  [on_device(): pl.pallas_call(lambda *refs: assemble_kernel(*refs, blocks=blocks, cols=c...]
  transfers between devices with their start and end apart: 12 -> 12, of which waited for: 4 -> 3; matrix products, arithmetic and copies ran while one was open for 0% -> 0% of each run, Pallas kernels for 5% -> 6%
where the time goes in v8:
time: 98.4 us; the launch traced here: 97.5 us
  waiting for transfers between devices  36.1 us (37%)
  starting transfers between devices  27.6 us (28%)
  blocking collectives  18 us (18%)
  Pallas kernels  15.5 us (16%)
    ppermute x8, waiting for transfers between devices, hop(): lax.ppermute(value, axis, [(i, (i + distance) % size) for i in range(size)])  28.2 us
    all_to_all x1, blocking collectives, exchange(): lax.all_to_all(message.reshape(peers, MSG, LANES), 'shuf', 0, 0, tiled=True)  18 us
    ppermute x8, starting transfers between devices, hop(): lax.ppermute(value, axis, [(i, (i + distance) % size) for i in range(size)])  14 us
    all_to_all x1, starting transfers between devices, exchange(): lax.all_to_all(message.reshape(peers, MSG, LANES), 'shuf', 0, 0, tiled=True)  11.5 us
    all_to_all x1, waiting for transfers between devices, exchange(): lax.all_to_all(message.reshape(peers, MSG, LANES), 'shuf', 0, 0, tiled=True)  7.87 us
    pallas_call x1, Pallas kernels, on_device(): pl.pallas_call(lambda *refs: project_kernel(*refs, blocks=blocks, tile_ro...  6.99 us
    pallas_call x1, Pallas kernels, on_device(): pl.pallas_call(lambda *refs: stats_kernel(*refs, tiles=tiles, peers=peers...  3.37 us
    ppermute x3, starting transfers between devices, trade(): lax.ppermute(value, 'shuf', [(i, i ^ distance) for i in range(peers)])  2.08 us
  transfers between devices with their start and end apart: 12, of which 3 were waited for; matrix products, arithmetic and copies ran while one was open for 0% of the time, Pallas kernels for 6%

profile of v8, /device:TPU:32, one launch (start us, length us, event | category | flops | bytes accessed | tf_op | source)
XLA Modules:
  0.0 97.5 jit_solution(12263114263059370362)
XLA Ops:
  0.0 1.3 %cut.1 = (bf16[2304,256]{1,0:T(8,128)(2,1)S(1)}, bf16[64,1024]{1,0:T(8,128)(2,1)S(1)}) custom-call(bf16[8192,256]{1,0:T(8,128)(2,1)} %refs_0_.5, bf16[256,1024]{1,0:T(8,128)(2,1)} %refs_1_.1), custom_call_target="tpu_custom_call" | custom-call | tf_op jit(solution)/shard_map/cut/pallas_call | solution.py:326
  1.3 0.0 copy-start.1
  1.3 0.0 copy-start.4
  1.3 3.1 %collective-permute-start.1 = (bf16[2304,256]{1,0:T(8,128)(2,1)S(1)}, bf16[2304,256]{1,0:T(8,128)(2,1)S(1)}, u32[]{:S(2)}, u32[]{:S(2)}) collective-permute-start(bf16[2304,256]{1,0:T(8,128)(2,1)S(1)} %get-tuple-element.14.refs_1_), channel_id=1, source_target_pairs={{0,2},{1,3},{2,0},{3,1},{4,6},{5,7},{6,4},{7,5},{8,10},{9,11},{10,... | collective-permute-start | bytes 3538952 | tf_op jit(solution)/shard_map/ppermute | solution.py:287
  4.4 1.1 %collective-permute-start.7 = (bf16[64,1024]{1,0:T(8,128)(2,1)S(1)}, bf16[64,1024]{1,0:T(8,128)(2,1)S(1)}, u32[]{:S(2)}, u32[]{:S(2)}) collective-permute-start(bf16[64,1024]{1,0:T(8,128)(2,1)S(1)} %get-tuple-element.22.own), channel_id=1, source_target_pairs={{0,3},{1,0},{2,1},{3,2},{4,7},{5,4},{6,5},{7,6},{8,11},{9,8},{10,9... | collective-permute-start | bytes 393224 | tf_op jit(solution)/shard_map/ppermute | solution.py:287
  5.6 0.9 collective-permute-start.6
  6.5 27.1 %collective-permute-done.7.three = bf16[64,1024]{1,0:T(8,128)(2,1)S(1)} collective-permute-done((bf16[64,1024]{1,0:T(8,128)(2,1)S(1)}, bf16[64,1024]{1,0:T(8,128)(2,1)S(1)}, u32[]{:S(2)}, u32[]{:S(2)}) %collective-permute-start.7) | collective-permute-done | bytes 131104 | tf_op jit(solution)/shard_map/ppermute | solution.py:287
  33.6 0.0 collective-permute-done.6.one
  33.6 0.9 stack.1.refs_0_
  34.5 1.6 %collective-permute-start.9 = (bf16[256,1024]{1,0:T(8,128)(2,1)}, bf16[256,1024]{1,0:T(8,128)(2,1)S(1)}, u32[]{:S(2)}, u32[]{:S(2)}) collective-permute-start(bf16[256,1024]{1,0:T(8,128)(2,1)} %stack.1.refs_0_), channel_id=1, source_target_pairs={{0,64},{4,68},{8,72},{12,76},{16,80},{20,84},{24,88},{28,92},{32,9... | collective-permute-start | bytes 1572872 | tf_op jit(solution)/shard_map/ppermute | solution.py:386
  36.0 0.0 copy-start.3
  36.1 3.4 %stats.1 = (bf16[1024,128]{1,0:T(8,128)(2,1)}, bf16[2048,256]{1,0:T(8,128)(2,1)}, bf16[2048,256]{1,0:T(8,128)(2,1)}) custom-call(bf16[8192,256]{1,0:T(8,128)(2,1)} %refs_0_.5, bf16[2304,256]{1,0:T(8,128)(2,1)S(1)} %get-tuple-element.14.refs_1_, s32[1,64]{1,0:T(1,128)S(1)} %bitcast.10, s32[1,64]{1,0:T(1,128)S(1)} %bitcast.14), custom_call_target="tpu_custom_call" | custom-call | tf_op jit(solution)/shard_map/stats/pallas_call | solution.py:337
  39.4 11.5 %all-to-all-start = ((bf16[64,16,128]{2,1,0:T(8,128)(2,1)}), bf16[64,16,128]{2,1,0:T(8,128)(2,1)S(1)}, u32[]{:S(2)}, u32[]{:S(2)}) async-start(bf16[64,16,128]{2,1,0:T(8,128)(2,1)} %bitcast.16), calls=%async_computation | async-start | bytes 524288 | tf_op jit(solution)/shard_map/all_to_all | solution.py:358
  50.9 1.5 %collective-permute-start = (bf16[2048,256]{1,0:T(8,128)(2,1)}, bf16[2048,256]{1,0:T(8,128)(2,1)S(1)}, u32[]{:S(2)}, u32[]{:S(2)}) collective-permute-start(bf16[2048,256]{1,0:T(8,128)(2,1)} %get-tuple-element.15), channel_id=1, source_target_pairs={{0,1},{1,2},{2,3},{3,0},{4,5},{5,6},{6,7},{7,4},{8,9},{9,10},{10,1... | collective-permute-start | bytes 3145736 | tf_op jit(solution)/shard_map/ppermute | solution.py:287
  52.4 1.8 %collective-permute-start.2 = (bf16[2048,256]{1,0:T(8,128)(2,1)}, bf16[2048,256]{1,0:T(8,128)(2,1)}, u32[]{:S(2)}, u32[]{:S(2)}) collective-permute-start(bf16[2048,256]{1,0:T(8,128)(2,1)} %get-tuple-element.16), channel_id=1, source_target_pairs={{0,3},{1,0},{2,1},{3,2},{4,7},{5,4},{6,5},{7,6},{8,11},{9,8},{10,9... | collective-permute-start | bytes 3145736 | tf_op jit(solution)/shard_map/ppermute | solution.py:287
  54.2 0.0 collective-permute-start.8
  54.3 0.0 collective-permute-done.9.refs_2_
  54.3 0.5 collective-permute-start.10
  54.8 7.9 %all-to-all-done = bf16[64,16,128]{2,1,0:T(8,128)(2,1)S(1)} async-done(((bf16[64,16,128]{2,1,0:T(8,128)(2,1)}), bf16[64,16,128]{2,1,0:T(8,128)(2,1)S(1)}, u32[]{:S(2)}, u32[]{:S(2)}) %all-to-all-start) | async-done | bytes 262176 | tf_op jit(solution)/shard_map/all_to_all | solution.py:358
  62.6 1.3 %moments.1 = bf16[1024,128]{1,0:T(8,128)(2,1)} custom-call(bf16[1024,128]{1,0:T(8,128)(2,1)S(1)} %bitcast.8, f32[2,256]{1,0:T(2,128)S(1)} %pair.1.refs_1_), custom_call_target="tpu_custom_call" | custom-call | tf_op jit(solution)/shard_map/moments/pallas_call | solution.py:375
  64.0 18.0 %all_to_all.10 = bf16[64,16,128]{2,1,0:T(8,128)(2,1)S(1)} all-to-all(bf16[64,16,128]{2,1,0:T(8,128)(2,1)} %bitcast.15), channel_id=1, replica_groups=mesh['shuf'=64,'rep'=4] {'shuf'}, dimensions={0} | all-to-all | bytes 524288 | tf_op jit(solution)/shard_map/all_to_all | solution.py:358
  82.0 0.4 pick.1
  82.4 1.5 %collective-permute-start.3 = (bf16[16,768]{1,0:T(8,128)(2,1)S(1)}, bf16[16,768]{1,0:T(8,128)(2,1)S(1)}, u32[]{:S(2)}, u32[]{:S(2)}) collective-permute-start(bf16[16,768]{1,0:T(8,128)(2,1)S(1)} %get-tuple-element.19), channel_id=1, source_target_pairs={{0,1},{1,2},{2,3},{3,0},{4,5},{5,6},{6,7},{7,4},{8,9},{9,10},{10,1... | collective-permute-start | bytes 73736 | tf_op jit(solution)/shard_map/ppermute | solution.py:287
  83.9 0.0 collective-permute-done.8.refs_1_
  83.9 2.7 %collective-permute-start.4 = (bf16[16,768]{1,0:T(8,128)(2,1)S(1)}, bf16[16,768]{1,0:T(8,128)(2,1)S(1)}, u32[]{:S(2)}, u32[]{:S(2)}) collective-permute-start(bf16[16,768]{1,0:T(8,128)(2,1)S(1)} %get-tuple-element.20), channel_id=1, source_target_pairs={{0,2},{1,3},{2,0},{3,1},{4,6},{5,7},{6,4},{7,5},{8,10},{9,11},{10,... | collective-permute-start | bytes 73736 | tf_op jit(solution)/shard_map/ppermute | solution.py:287
  86.6 0.0 collective-permute-done.10.refs_3_
  86.6 1.4 %collective-permute-start.5 = (bf16[16,768]{1,0:T(8,128)(2,1)S(1)}, bf16[16,768]{1,0:T(8,128)(2,1)S(1)}, u32[]{:S(2)}, u32[]{:S(2)}) collective-permute-start(bf16[16,768]{1,0:T(8,128)(2,1)S(1)} %get-tuple-element.21), channel_id=1, source_target_pairs={{0,3},{1,0},{2,1},{3,2},{4,7},{5,4},{6,5},{7,6},{8,11},{9,8},{10,9... | collective-permute-start | bytes 73736 | tf_op jit(solution)/shard_map/ppermute | solution.py:287
  88.0 1.2 %assemble.1.refs_8_ = bf16[1024,1024]{1,0:T(8,128)(2,1)S(1)} custom-call(bf16[256,1024]{1,0:T(8,128)(2,1)} %stack.1.refs_0_, bf16[256,1024]{1,0:T(8,128)(2,1)S(1)} %collective-permute-done.8.refs_1_, bf16[256,1024]{1,0:T(8,128)(2,1)S(1)} %collective-permute-done.9.refs_2_, bf16[256,1024]{1,0:T(8,128)(2,1)S(1)} %collective-permute-done.10.refs_3_), custom_call_target="tpu_custom_call" | custom-call | tf_op jit(solution)/shard_map/assemble/pallas_call | solution.py:400
  89.2 0.0 collective-permute-done.refs_1_
  89.2 0.0 collective-permute-done.2.refs_3_
  89.3 1.1 %collective-permute-done.5.refs_7_ = bf16[16,768]{1,0:T(8,128)(2,1)S(1)} collective-permute-done((bf16[16,768]{1,0:T(8,128)(2,1)S(1)}, bf16[16,768]{1,0:T(8,128)(2,1)S(1)}, u32[]{:S(2)}, u32[]{:S(2)}) %collective-permute-start.5) | collective-permute-done | bytes 24608 | tf_op jit(solution)/shard_map/ppermute | solution.py:287
  90.4 7.0 %project.1 = bf16[2048,1024]{1,0:T(8,128)(2,1)} custom-call(bf16[8192,256]{1,0:T(8,128)(2,1)} %refs_0_.5, bf16[2048,256]{1,0:T(8,128)(2,1)} %copy-done.6, bf16[2304,256]{1,0:T(8,128)(2,1)} %copy-done, bf16[2048,256]{1,0:T(8,128)(2,1)} %collective-permute-done.2.refs_3_, bf16[16,768]{1,0:T(8,128)(2,1)S(1)} %get-tuple-element.18.refs_4_, ...), custom_call_target="tpu_custom_call" | custom-call | tf_op jit(solution)/shard_map/project/pallas_call | solution.py:425
  (15 shorter events, 0.0 us)
Async XLA Ops:
  1.3 34.7 %copy-start.1 = (s32[64,1]{0,1:T(1,128)S(1)}, s32[64,1]{0,1:T(1,128)}, u32[]{:S(2)}) copy-start(s32[64,1]{0,1:T(1,128)} %param.8) | copy-start | bytes 772
  1.3 34.7 %copy-start.4 = (s32[64]{0:T(128)S(1)}, s32[64]{0:T(128)}, u32[]{:S(2)}) copy-start(s32[64]{0:T(128)} %param.7) | copy-start | bytes 772
  1.3 32.2 %collective-permute-start.1 = (bf16[2304,256]{1,0:T(8,128)(2,1)S(1)}, bf16[2304,256]{1,0:T(8,128)(2,1)S(1)}, u32[]{:S(2)}, u32[]{:S(2)}) collective-permute-start(bf16[2304,256]{1,0:T(8,128)(2,1)S(1)} %get-tuple-element.14.refs_1_), channel_id=1, source_target_pairs={{0,2},{1,3},{2,0},{3,1},{4,6},{5,7},{6,4},{7,5},{8,10},{9,11},{10,... | collective-permute-start | bytes 3538952 | tf_op jit(solution)/shard_map/ppermute | solution.py:287
  4.4 29.1 %collective-permute-start.7 = (bf16[64,1024]{1,0:T(8,128)(2,1)S(1)}, bf16[64,1024]{1,0:T(8,128)(2,1)S(1)}, u32[]{:S(2)}, u32[]{:S(2)}) collective-permute-start(bf16[64,1024]{1,0:T(8,128)(2,1)S(1)} %get-tuple-element.22.own), channel_id=1, source_target_pairs={{0,3},{1,0},{2,1},{3,2},{4,7},{5,4},{6,5},{7,6},{8,11},{9,8},{10,9... | collective-permute-start | bytes 393224 | tf_op jit(solution)/shard_map/ppermute | solution.py:287
  5.6 28.0 %collective-permute-start.6 = (bf16[64,1024]{1,0:T(8,128)(2,1)S(1)}, bf16[64,1024]{1,0:T(8,128)(2,1)S(1)}, u32[]{:S(2)}, u32[]{:S(2)}) collective-permute-start(bf16[64,1024]{1,0:T(8,128)(2,1)S(1)} %get-tuple-element.22.own), channel_id=1, source_target_pairs={{0,1},{1,2},{2,3},{3,0},{4,5},{5,6},{6,7},{7,4},{8,9},{9,10},{10,1... | collective-permute-start | bytes 393224 | tf_op jit(solution)/shard_map/ppermute | solution.py:287
  33.6 5.9 %copy-start = (bf16[2304,256]{1,0:T(8,128)(2,1)}, bf16[2304,256]{1,0:T(8,128)(2,1)S(1)}, u32[]{:S(2)}) copy-start(bf16[2304,256]{1,0:T(8,128)(2,1)S(1)} %collective-permute-done.1.two.refs_2_) | copy-start | bytes 3538948
  34.5 19.8 %collective-permute-start.9 = (bf16[256,1024]{1,0:T(8,128)(2,1)}, bf16[256,1024]{1,0:T(8,128)(2,1)S(1)}, u32[]{:S(2)}, u32[]{:S(2)}) collective-permute-start(bf16[256,1024]{1,0:T(8,128)(2,1)} %stack.1.refs_0_), channel_id=1, source_target_pairs={{0,64},{4,68},{8,72},{12,76},{16,80},{20,84},{24,88},{28,92},{32,9... | collective-permute-start | bytes 1572872 | tf_op jit(solution)/shard_map/ppermute | solution.py:386
  36.0 18.2 %copy-start.5 = (bf16[256,1024]{1,0:T(8,128)(2,1)S(1)}, bf16[256,1024]{1,0:T(8,128)(2,1)}, u32[]{:S(2)}) copy-start(bf16[256,1024]{1,0:T(8,128)(2,1)} %stack.1.refs_0_) | copy-start | bytes 1572868
  36.0 18.7 %copy-start.2 = (f32[256]{0:T(256)S(1)}, f32[256]{0:T(256)}, u32[]{:S(2)}) copy-start(f32[256]{0:T(256)} %param.9) | copy-start | bytes 3076
  36.0 18.7 %copy-start.3 = (f32[256]{0:T(256)S(1)}, f32[256]{0:T(256)}, u32[]{:S(2)}) copy-start(f32[256]{0:T(256)} %param.10) | copy-start | bytes 3076
  39.4 23.2 %all-to-all-start = ((bf16[64,16,128]{2,1,0:T(8,128)(2,1)}), bf16[64,16,128]{2,1,0:T(8,128)(2,1)S(1)}, u32[]{:S(2)}, u32[]{:S(2)}) async-start(bf16[64,16,128]{2,1,0:T(8,128)(2,1)} %bitcast.16), calls=%async_computation | async-start | bytes 524288 | tf_op jit(solution)/shard_map/all_to_all | solution.py:358
  50.9 38.3 %collective-permute-start = (bf16[2048,256]{1,0:T(8,128)(2,1)}, bf16[2048,256]{1,0:T(8,128)(2,1)S(1)}, u32[]{:S(2)}, u32[]{:S(2)}) collective-permute-start(bf16[2048,256]{1,0:T(8,128)(2,1)} %get-tuple-element.15), channel_id=1, source_target_pairs={{0,1},{1,2},{2,3},{3,0},{4,5},{5,6},{6,7},{7,4},{8,9},{9,10},{10,1... | collective-permute-start | bytes 3145736 | tf_op jit(solution)/shard_map/ppermute | solution.py:287
  52.4 36.8 %collective-permute-start.2 = (bf16[2048,256]{1,0:T(8,128)(2,1)}, bf16[2048,256]{1,0:T(8,128)(2,1)}, u32[]{:S(2)}, u32[]{:S(2)}) collective-permute-start(bf16[2048,256]{1,0:T(8,128)(2,1)} %get-tuple-element.16), channel_id=1, source_target_pairs={{0,3},{1,0},{2,1},{3,2},{4,7},{5,4},{6,5},{7,6},{8,11},{9,8},{10,9... | collective-permute-start | bytes 3145736 | tf_op jit(solution)/shard_map/ppermute | solution.py:287
  54.2 29.6 %collective-permute-start.8 = (bf16[256,1024]{1,0:T(8,128)(2,1)S(1)}, bf16[256,1024]{1,0:T(8,128)(2,1)S(1)}, u32[]{:S(2)}, u32[]{:S(2)}) collective-permute-start(bf16[256,1024]{1,0:T(8,128)(2,1)S(1)} %copy-done.5), channel_id=1, source_target_pairs={{0,4},{4,0},{8,12},{12,8},{16,20},{20,16},{24,28},{28,24},{32,36},... | collective-permute-start | bytes 1572872 | tf_op jit(solution)/shard_map/ppermute | solution.py:386
  54.3 32.3 %collective-permute-start.10 = (bf16[256,1024]{1,0:T(8,128)(2,1)S(1)}, bf16[256,1024]{1,0:T(8,128)(2,1)S(1)}, u32[]{:S(2)}, u32[]{:S(2)}) collective-permute-start(bf16[256,1024]{1,0:T(8,128)(2,1)S(1)} %collective-permute-done.9.refs_2_), channel_id=1, source_target_pairs={{0,4},{4,0},{8,12},{12,8},{16,20},{20,16},{24,28},{28,24},{32,36},... | collective-permute-start | bytes 1572872 | tf_op jit(solution)/shard_map/ppermute | solution.py:386
  82.4 6.9 %collective-permute-start.3 = (bf16[16,768]{1,0:T(8,128)(2,1)S(1)}, bf16[16,768]{1,0:T(8,128)(2,1)S(1)}, u32[]{:S(2)}, u32[]{:S(2)}) collective-permute-start(bf16[16,768]{1,0:T(8,128)(2,1)S(1)} %get-tuple-element.19), channel_id=1, source_target_pairs={{0,1},{1,2},{2,3},{3,0},{4,5},{5,6},{6,7},{7,4},{8,9},{9,10},{10,1... | collective-permute-start | bytes 73736 | tf_op jit(solution)/shard_map/ppermute | solution.py:287
  83.9 5.4 %collective-permute-start.4 = (bf16[16,768]{1,0:T(8,128)(2,1)S(1)}, bf16[16,768]{1,0:T(8,128)(2,1)S(1)}, u32[]{:S(2)}, u32[]{:S(2)}) collective-permute-start(bf16[16,768]{1,0:T(8,128)(2,1)S(1)} %get-tuple-element.20), channel_id=1, source_target_pairs={{0,2},{1,3},{2,0},{3,1},{4,6},{5,7},{6,4},{7,5},{8,10},{9,11},{10,... | collective-permute-start | bytes 73736 | tf_op jit(solution)/shard_map/ppermute | solution.py:287
  86.6 3.8 %collective-permute-start.5 = (bf16[16,768]{1,0:T(8,128)(2,1)S(1)}, bf16[16,768]{1,0:T(8,128)(2,1)S(1)}, u32[]{:S(2)}, u32[]{:S(2)}) collective-permute-start(bf16[16,768]{1,0:T(8,128)(2,1)S(1)} %get-tuple-element.21), channel_id=1, source_target_pairs={{0,3},{1,0},{2,1},{3,2},{4,7},{5,4},{6,5},{7,6},{8,11},{9,8},{10,9... | collective-permute-start | bytes 73736 | tf_op jit(solution)/shard_map/ppermute | solution.py:287
  89.2 1.2 %copy-start.6 = (bf16[2048,256]{1,0:T(8,128)(2,1)}, bf16[2048,256]{1,0:T(8,128)(2,1)S(1)}, u32[]{:S(2)}) copy-start(bf16[2048,256]{1,0:T(8,128)(2,1)S(1)} %collective-permute-done.refs_1_) | copy-start | bytes 3145732

commit v9 on v8

--- a/solution.py
+++ b/solution.py
@@ -77,23 +77,6 @@
         out[n * slab : (n + 1) * slab, :] = part[...]
     for c in range(own.shape[1] // cols):
         out[2 * slab : 3 * slab, c * cols : (c + 1) * cols] = two[c * slab : (c + 1) * slab, :]
-
-
-def assemble_kernel(mine, sibling, across, across_sibling, out, *, blocks, cols, depth):
-    slab = mine.shape[0] // blocks
-    slabs = cols // slab
-    first = slab_of(depth, slabs)
-    core = lax.rem(first, 2)
-    parts = (
-        (mine, first),
-        (sibling, first + 1 - 2 * core),
-        (across, lax.rem(first + 2, slabs)),
-        (across_sibling, lax.rem(first + 2, slabs) + 1 - 2 * core),
-    )
-    for part, number in parts:
-        for n in range(blocks):
-            at = pl.multiple_of(n * cols + number * slab, slab)
-            out[pl.ds(at, slab), :] = part[n * slab : (n + 1) * slab, :]
 
 
 def stats_kernel(values, two, owner, sub, out, one, three, *scratches, tiles, peers):
@@ -238,48 +221,72 @@
         out[...] = picked[n * each : (n + 1) * each, :].astype(BF16)
 
 
-def project_kernel(*refs, blocks, tile_rows, block, skipped):
-    moved, coeffs, weight, out = refs[:blocks], refs[blocks : 2 * blocks], refs[2 * blocks], refs[2 * blocks + 1]
-    held_rows, result, wide, sems_in, sems_out = refs[-5:]
+def project_kernel(*refs, blocks, tile_rows, sizes, skipped, depth):
+    moved, coeffs, (mine, *others), out = refs[:blocks], refs[blocks : 2 * blocks], refs[2 * blocks : -7], refs[-7]
+    held_rows, weight, result, wide, sems_in, sems_weight = refs[-6:]
     _, rows, cols = held_rows.shape
     skipped = (lax.axis_index("rep") * rows, *skipped)
-    parts = ((0, block), (block, rows - block)) if rows > block else ((0, rows),)
-    tiles = block // tile_rows
-    steps = rows // block
+    parts = ((0, sizes[0]), (sizes[0], rows - sizes[0])) if rows > sizes[0] else ((0, rows),)
 
     def inward(n, p):
         at, size = parts[p]
         source = moved[n].at[pl.ds(pl.multiple_of(skipped[n] + at, tile_rows), size), :]
         return pltpu.make_async_copy(source, held_rows.at[n, pl.ds(at, size), :], sems_in.at[n, p])
 
-    def outward(j):
-        part = pl.ds(j * block, block)
-        return pltpu.make_async_copy(result.at[part, :], out.at[part, :], sems_out.at[j])
-
-    for p in range(len(parts)):
+    slab = mine.shape[0] // blocks
+    slabs = cols // slab
+    own = slab_of(depth, slabs)
+    core = lax.rem(own, 2)
+    beyond = lax.rem(own + 2, slabs)
+    numbers = (own + 1 - 2 * core, beyond, beyond + 1 - 2 * core)
+
+    def rows_of(n, number):
+        return weight.at[pl.ds(pl.multiple_of(n * cols + number * slab, slab), slab), :]
+
+    own_slabs = [
+        pltpu.make_async_copy(mine.at[pl.ds(n * slab, slab), :], rows_of(n, own), sems_weight.at[n])
+        for n in range(blocks)
+    ]
+    for n in range(blocks):
+        inward(n, 0).start()
+    for copy in own_slabs:
+        copy.start()
+    for n in range(blocks):
+        if len(parts) > 1:
+            inward(n, 1).start()
+    for part, number in zip(others, numbers):
         for n in range(blocks):
-            inward(n, p).start()
+            rows_of(n, number)[...] = part[n * slab : (n + 1) * slab, :]
     for n in range(blocks):
         wide[n] = coeffs[n][...].astype(F32)
-    for j in range(steps):
+    for copy in own_slabs:
+        copy.wait()
+
+    def outward(at, size, j):
+        return pltpu.make_async_copy(result.at[pl.ds(at, size), :], out.at[pl.ds(at, size), :], sems_in.at[j % blocks, 2 + j // blocks])
+
+    first, ended = 0, []
+    for j, size in enumerate(sizes):
         if j < len(parts):
             for n in range(blocks):
                 inward(n, j).wait()
         strips = []
-        for t in range(tiles):
-            at = j * block + t * tile_rows
+        for t in range(size // tile_rows):
+            at = first + t * tile_rows
             scores = []
             for n in range(blocks):
-                row = wide[n, j * tiles + t : j * tiles + t + 1, :]
+                row = wide[n, at // tile_rows : at // tile_rows + 1, :]
                 value = held_rows[n, at : at + tile_rows, :]
                 scored = value.astype(F32) * row[:, :cols] + (row[:, cols : 2 * cols] + row[:, 2 * cols :])
                 scores.append(scored.astype(BF16))
             strips.append(jnp.concatenate(scores, axis=1))
         product = jnp.dot(jnp.concatenate(strips, axis=0), weight[...], preferred_element_type=F32)
-        result[j * block : (j + 1) * block, :] = product.astype(BF16)
-        outward(j).start()
-    for j in range(steps):
-        outward(j).wait()
+        result[first : first + size, :] = product.astype(BF16)
+        ended.append(outward(first, size, j))
+        ended[-1].start()
+        first += size
+    for copy in ended:
+        copy.wait()
 
 
 def hop(value, axis, distance):
@@ -397,16 +404,6 @@
     across = trade(mine, 2 * depth)
     sibling = trade(mine, 1)
     across_sibling = trade(across, 1)
-    weight = pl.pallas_call(
-        lambda *refs: assemble_kernel(*refs, blocks=blocks, cols=cols, depth=depth),
-        grid=(1,),
-        in_specs=[whole(cols, outputs)] + [IN_VMEM] * 3,
-        out_specs=IN_VMEM,
-        out_shape=pltpu.VMEM((blocks * cols, outputs), BF16),
-        compiler_params=limit(8),
-        name="assemble",
-    )(off_chip(mine), held(sibling), held(across), held(across_sibling))
-
     each = tiles // blocks
     coeffs = pl.pallas_call(
         lambda *refs: tile_kernel(*refs, tiles=tiles, peers=peers, blocks=blocks),
@@ -421,28 +418,38 @@
     for d in (2, 1, 3):
         known[d] = hop(coeffs[d], "rep", d)
 
-    block = min(512, own_rows)
+    middle = own_rows // 4
+    sizes = (middle // 2, middle, middle, middle, middle // 2)
     return pl.pallas_call(
         lambda *refs: project_kernel(
-            *refs, blocks=blocks, tile_rows=tile_rows, block=block, skipped=(0, two.shape[0] - own_rows, 0)
+            *refs,
+            blocks=blocks,
+            tile_rows=tile_rows,
+            sizes=sizes,
+            skipped=(0, two.shape[0] - own_rows, 0),
+            depth=depth,
         ),
-        in_specs=[IN_HBM] * blocks + [IN_VMEM] * (blocks + 1),
+        in_specs=[IN_HBM] * blocks + [IN_VMEM] * blocks + [IN_HBM] + [IN_VMEM] * 3,
         out_specs=IN_HBM,
         out_shape=pltpu.HBM((own_rows, outputs), BF16),
         scratch_shapes=[
             pltpu.VMEM((blocks, own_rows, cols), BF16),
+            pltpu.VMEM((blocks * cols, outputs), BF16),
             pltpu.VMEM((own_rows, outputs), BF16),
             pltpu.VMEM((blocks, each, 3 * cols), F32),
-            pltpu.SemaphoreType.DMA((blocks, 2)),
-            pltpu.SemaphoreType.DMA((own_rows // block,)),
+            pltpu.SemaphoreType.DMA((blocks, 4)),
+            pltpu.SemaphoreType.DMA((blocks,)),
         ],
-        compiler_params=limit(24),
+        compiler_params=limit(28),
         name="project",
     )(
         off_chip(values),
         *[off_chip(moved[d]) for d in range(1, blocks)],
         *[held(known[d]) for d in range(blocks)],
-        held(weight),
+        off_chip(mine),
+        held(sibling),
+        held(across),
+        held(across_sibling),
     )
 
 

time: 98.4 us -> 77.6 us (0.79)
  blocking collectives: 18 us -> 0 us
  waiting for transfers between devices: 36.1 us -> 23.2 us
  starting transfers between devices: 27.6 us -> 38.6 us
    all_to_all x1 -> x0, blocking collectives: 18 us -> none  [exchange(): lax.all_to_all(message.reshape(peers, MSG, LANES), 'shuf', 0, 0, tiled=True)]
    ppermute x8, waiting for transfers between devices: 28.2 us -> 12.1 us  [hop(): lax.ppermute(value, axis, [(i, (i + distance) % size) for i in range(size)])]
    all_to_all x1 -> x2, starting transfers between devices: 11.5 us -> 23.2 us  [exchange(): lax.all_to_all(message.reshape(peers, MSG, LANES), 'shuf', 0, 0, tiled=True)]
    all_to_all x1 -> x2, waiting for transfers between devices: 7.87 us -> 11.1 us  [exchange(): lax.all_to_all(message.reshape(peers, MSG, LANES), 'shuf', 0, 0, tiled=True)]
    pallas_call x1 -> x0, Pallas kernels: 1.22 us -> none  [on_device(): pl.pallas_call(lambda *refs: assemble_kernel(*refs, blocks=blocks, cols=c...]
  transfers between devices with their start and end apart: 12 -> 13, of which waited for: 3 -> 5; matrix products, arithmetic and copies ran while one was open for 0% -> 0% of each run, Pallas kernels for 6% -> 8%
where the time goes in v9:
time: 77.6 us; the launch traced here: 76.7 us
  starting transfers between devices  38.6 us (50%)
  waiting for transfers between devices  23.2 us (30%)
  Pallas kernels  14.7 us (19%)
    all_to_all x2, starting transfers between devices, exchange(): lax.all_to_all(message.reshape(peers, MSG, LANES), 'shuf', 0, 0, tiled=True)  23.2 us
    ppermute x8, starting transfers between devices, hop(): lax.ppermute(value, axis, [(i, (i + distance) % size) for i in range(size)])  13.2 us
    ppermute x8, waiting for transfers between devices, hop(): lax.ppermute(value, axis, [(i, (i + distance) % size) for i in range(size)])  12.1 us
    all_to_all x2, waiting for transfers between devices, exchange(): lax.all_to_all(message.reshape(peers, MSG, LANES), 'shuf', 0, 0, tiled=True)  11.1 us
    pallas_call x1, Pallas kernels, on_device(): pl.pallas_call(lambda *refs: project_kernel(*refs, blocks=blocks, tile_ro...  7.41 us
    pallas_call x1, Pallas kernels, on_device(): pl.pallas_call(lambda *refs: stats_kernel(*refs, tiles=tiles, peers=peers...  3.31 us
    ppermute x3, starting transfers between devices, trade(): lax.ppermute(value, 'shuf', [(i, i ^ distance) for i in range(peers)])  2.17 us
  transfers between devices with their start and end apart: 13, of which 5 were waited for; matrix products, arithmetic and copies ran while one was open for 0% of the time, Pallas kernels for 8%

profile of v9, /device:TPU:32, one launch (start us, length us, event | category | flops | bytes accessed | tf_op | source)
XLA Modules:
  0.0 76.7 jit_solution(17212313930785581268)
XLA Ops:
  0.0 1.3 %cut.1 = (bf16[2304,256]{1,0:T(8,128)(2,1)S(1)}, bf16[64,1024]{1,0:T(8,128)(2,1)S(1)}) custom-call(bf16[8192,256]{1,0:T(8,128)(2,1)} %refs_0_.5, bf16[256,1024]{1,0:T(8,128)(2,1)} %refs_1_.1), custom_call_target="tpu_custom_call" | custom-call | tf_op jit(solution)/shard_map/cut/pallas_call | solution.py:333
  1.3 0.0 copy-start.2
  1.3 0.0 copy-start.3
  1.3 3.1 %collective-permute-start.1 = (bf16[2304,256]{1,0:T(8,128)(2,1)S(1)}, bf16[2304,256]{1,0:T(8,128)(2,1)S(1)}, u32[]{:S(2)}, u32[]{:S(2)}) collective-permute-start(bf16[2304,256]{1,0:T(8,128)(2,1)S(1)} %get-tuple-element.14.refs_1_), channel_id=1, source_target_pairs={{0,2},{1,3},{2,0},{3,1},{4,6},{5,7},{6,4},{7,5},{8,10},{9,11},{10,... | collective-permute-start | bytes 3538952 | tf_op jit(solution)/shard_map/ppermute | solution.py:294
  4.5 1.1 %collective-permute-start.7 = (bf16[64,1024]{1,0:T(8,128)(2,1)S(1)}, bf16[64,1024]{1,0:T(8,128)(2,1)S(1)}, u32[]{:S(2)}, u32[]{:S(2)}) collective-permute-start(bf16[64,1024]{1,0:T(8,128)(2,1)S(1)} %get-tuple-element.22.own), channel_id=1, source_target_pairs={{0,3},{1,0},{2,1},{3,2},{4,7},{5,4},{6,5},{7,6},{8,11},{9,8},{10,9... | collective-permute-start | bytes 393224 | tf_op jit(solution)/shard_map/ppermute | solution.py:294
  5.6 0.9 %collective-permute-start.6 = (bf16[64,1024]{1,0:T(8,128)(2,1)S(1)}, bf16[64,1024]{1,0:T(8,128)(2,1)S(1)}, u32[]{:S(2)}, u32[]{:S(2)}) collective-permute-start(bf16[64,1024]{1,0:T(8,128)(2,1)S(1)} %get-tuple-element.22.own), channel_id=1, source_target_pairs={{0,1},{1,2},{2,3},{3,0},{4,5},{5,6},{6,7},{7,4},{8,9},{9,10},{10,1... | collective-permute-start | bytes 393224 | tf_op jit(solution)/shard_map/ppermute | solution.py:294
  6.5 3.3 %stats.1 = (bf16[1024,128]{1,0:T(8,128)(2,1)}, bf16[2048,256]{1,0:T(8,128)(2,1)}, bf16[2048,256]{1,0:T(8,128)(2,1)}) custom-call(bf16[8192,256]{1,0:T(8,128)(2,1)} %refs_0_.5, bf16[2304,256]{1,0:T(8,128)(2,1)S(1)} %get-tuple-element.14.refs_1_, s32[1,64]{1,0:T(1,128)S(1)} %bitcast.10, s32[1,64]{1,0:T(1,128)S(1)} %bitcast.14), custom_call_target="tpu_custom_call" | custom-call | tf_op jit(solution)/shard_map/stats/pallas_call | solution.py:344
  9.8 0.7 collective-permute-start
  10.5 2.6 %collective-permute-start.2 = (bf16[2048,256]{1,0:T(8,128)(2,1)}, bf16[2048,256]{1,0:T(8,128)(2,1)}, u32[]{:S(2)}, u32[]{:S(2)}) collective-permute-start(bf16[2048,256]{1,0:T(8,128)(2,1)} %get-tuple-element.16), channel_id=1, source_target_pairs={{0,3},{1,0},{2,1},{3,2},{4,7},{5,4},{6,5},{7,6},{8,11},{9,8},{10,9... | collective-permute-start | bytes 3145736 | tf_op jit(solution)/shard_map/ppermute | solution.py:294
  13.1 11.8 %all-to-all-start = ((bf16[64,16,128]{2,1,0:T(8,128)(2,1)}), bf16[64,16,128]{2,1,0:T(8,128)(2,1)S(1)}, u32[]{:S(2)}, u32[]{:S(2)}) async-start(bf16[64,16,128]{2,1,0:T(8,128)(2,1)} %bitcast.16), calls=%async_computation | async-start | bytes 524288 | tf_op jit(solution)/shard_map/all_to_all | solution.py:365
  24.9 9.8 %collective-permute-done.7.three = bf16[64,1024]{1,0:T(8,128)(2,1)S(1)} collective-permute-done((bf16[64,1024]{1,0:T(8,128)(2,1)S(1)}, bf16[64,1024]{1,0:T(8,128)(2,1)S(1)}, u32[]{:S(2)}, u32[]{:S(2)}) %collective-permute-start.7) | collective-permute-done | bytes 131104 | tf_op jit(solution)/shard_map/ppermute | solution.py:294
  34.7 0.0 collective-permute-done.6.one
  34.7 0.0 collective-permute-done.1.two.refs_2_
  34.7 0.9 %stack.1.refs_8_ = bf16[256,1024]{1,0:T(8,128)(2,1)} custom-call(bf16[64,1024]{1,0:T(8,128)(2,1)S(1)} %get-tuple-element.22.own, bf16[64,1024]{1,0:T(8,128)(2,1)S(1)} %collective-permute-done.6.one, bf16[2304,256]{1,0:T(8,128)(2,1)S(1)} %collective-permute-done.1.two.refs_2_, bf16[64,1024]{1,0:T(8,128)(2,1)S(1)} %collective-permute-done.7.three), custom_call_target="tpu_custom_call" | custom-call | tf_op jit(solution)/shard_map/stack/pallas_call | solution.py:395
  35.6 1.6 %collective-permute-start.9 = (bf16[256,1024]{1,0:T(8,128)(2,1)}, bf16[256,1024]{1,0:T(8,128)(2,1)S(1)}, u32[]{:S(2)}, u32[]{:S(2)}) collective-permute-start(bf16[256,1024]{1,0:T(8,128)(2,1)} %stack.1.refs_8_), channel_id=1, source_target_pairs={{0,64},{4,68},{8,72},{12,76},{16,80},{20,84},{24,88},{28,92},{32,9... | collective-permute-start | bytes 1572872 | tf_op jit(solution)/shard_map/ppermute | solution.py:393
  37.2 0.0 all-to-all-done
  37.2 1.4 %moments.1 = bf16[1024,128]{1,0:T(8,128)(2,1)} custom-call(bf16[1024,128]{1,0:T(8,128)(2,1)S(1)} %bitcast.8, f32[2,256]{1,0:T(2,128)S(1)} %pair.1.refs_1_), custom_call_target="tpu_custom_call" | custom-call | tf_op jit(solution)/shard_map/moments/pallas_call | solution.py:382
  38.6 11.5 %all-to-all-start.1 = ((bf16[64,16,128]{2,1,0:T(8,128)(2,1)}), bf16[64,16,128]{2,1,0:T(8,128)(2,1)S(1)}, u32[]{:S(2)}, u32[]{:S(2)}) async-start(bf16[64,16,128]{2,1,0:T(8,128)(2,1)} %bitcast.15), calls=%async_computation.1 | async-start | bytes 524288 | tf_op jit(solution)/shard_map/all_to_all | solution.py:365
  50.1 0.2 collective-permute-start.8
  50.3 0.0 collective-permute-done.9.refs_10_
  50.3 0.4 collective-permute-start.10
  50.7 11.1 %all-to-all-done.1 = bf16[64,16,128]{2,1,0:T(8,128)(2,1)S(1)} async-done(((bf16[64,16,128]{2,1,0:T(8,128)(2,1)}), bf16[64,16,128]{2,1,0:T(8,128)(2,1)S(1)}, u32[]{:S(2)}, u32[]{:S(2)}) %all-to-all-start.1) | async-done | bytes 262176 | tf_op jit(solution)/shard_map/all_to_all | solution.py:365
  61.8 0.4 pick.1
  62.2 1.5 %collective-permute-start.3 = (bf16[16,768]{1,0:T(8,128)(2,1)S(1)}, bf16[16,768]{1,0:T(8,128)(2,1)S(1)}, u32[]{:S(2)}, u32[]{:S(2)}) collective-permute-start(bf16[16,768]{1,0:T(8,128)(2,1)S(1)} %get-tuple-element.19), channel_id=1, source_target_pairs={{0,1},{1,2},{2,3},{3,0},{4,5},{5,6},{6,7},{7,4},{8,9},{9,10},{10,1... | collective-permute-start | bytes 73736 | tf_op jit(solution)/shard_map/ppermute | solution.py:294
  63.7 1.6 %collective-permute-start.4 = (bf16[16,768]{1,0:T(8,128)(2,1)S(1)}, bf16[16,768]{1,0:T(8,128)(2,1)S(1)}, u32[]{:S(2)}, u32[]{:S(2)}) collective-permute-start(bf16[16,768]{1,0:T(8,128)(2,1)S(1)} %get-tuple-element.20), channel_id=1, source_target_pairs={{0,2},{1,3},{2,0},{3,1},{4,6},{5,7},{6,4},{7,5},{8,10},{9,11},{10,... | collective-permute-start | bytes 73736 | tf_op jit(solution)/shard_map/ppermute | solution.py:294
  65.3 1.6 %collective-permute-start.5 = (bf16[16,768]{1,0:T(8,128)(2,1)S(1)}, bf16[16,768]{1,0:T(8,128)(2,1)S(1)}, u32[]{:S(2)}, u32[]{:S(2)}) collective-permute-start(bf16[16,768]{1,0:T(8,128)(2,1)S(1)} %get-tuple-element.21), channel_id=1, source_target_pairs={{0,3},{1,0},{2,1},{3,2},{4,7},{5,4},{6,5},{7,6},{8,11},{9,8},{10,9... | collective-permute-start | bytes 73736 | tf_op jit(solution)/shard_map/ppermute | solution.py:294
  66.9 0.4 collective-permute-done.3.refs_5_
  67.3 1.7 %collective-permute-done.4.refs_6_ = bf16[16,768]{1,0:T(8,128)(2,1)S(1)} collective-permute-done((bf16[16,768]{1,0:T(8,128)(2,1)S(1)}, bf16[16,768]{1,0:T(8,128)(2,1)S(1)}, u32[]{:S(2)}, u32[]{:S(2)}) %collective-permute-start.4) | collective-permute-done | bytes 24608 | tf_op jit(solution)/shard_map/ppermute | solution.py:294
  69.0 0.1 collective-permute-done.5.refs_7_
  69.2 0.0 collective-permute-done.8.refs_9_
  69.2 0.0 collective-permute-done.10.refs_11_
  69.2 7.4 %project.1 = bf16[2048,1024]{1,0:T(8,128)(2,1)} custom-call(bf16[8192,256]{1,0:T(8,128)(2,1)} %refs_0_.5, bf16[2048,256]{1,0:T(8,128)(2,1)} %collective-permute-done.refs_1_, bf16[2304,256]{1,0:T(8,128)(2,1)} %copy-done, bf16[2048,256]{1,0:T(8,128)(2,1)} %collective-permute-done.2.refs_3_, bf16[16,768]{1,0:T(8,128)(2,1)S(1)} %get-tuple-element.18.refs_4_, ...), custom_call_target="tpu_custom_call" | custom-call | tf_op jit(solution)/shard_map/project/pallas_call | solution.py:423
  (11 shorter events, 0.0 us)
Async XLA Ops:
  0.0 6.5 %copy-start.1 = (s32[64,1]{0,1:T(1,128)S(1)}, s32[64,1]{0,1:T(1,128)}, u32[]{:S(2)}) copy-start(s32[64,1]{0,1:T(1,128)} %param.8) | copy-start | bytes 772
  0.0 6.5 %copy-start.4 = (s32[64]{0:T(128)S(1)}, s32[64]{0:T(128)}, u32[]{:S(2)}) copy-start(s32[64]{0:T(128)} %param.7) | copy-start | bytes 772
  1.3 35.9 %copy-start.2 = (f32[256]{0:T(256)S(1)}, f32[256]{0:T(256)}, u32[]{:S(2)}) copy-start(f32[256]{0:T(256)} %param.9) | copy-start | bytes 3076
  1.3 35.9 %copy-start.3 = (f32[256]{0:T(256)S(1)}, f32[256]{0:T(256)}, u32[]{:S(2)}) copy-start(f32[256]{0:T(256)} %param.10) | copy-start | bytes 3076
  1.3 33.4 %collective-permute-start.1 = (bf16[2304,256]{1,0:T(8,128)(2,1)S(1)}, bf16[2304,256]{1,0:T(8,128)(2,1)S(1)}, u32[]{:S(2)}, u32[]{:S(2)}) collective-permute-start(bf16[2304,256]{1,0:T(8,128)(2,1)S(1)} %get-tuple-element.14.refs_1_), channel_id=1, source_target_pairs={{0,2},{1,3},{2,0},{3,1},{4,6},{5,7},{6,4},{7,5},{8,10},{9,11},{10,... | collective-permute-start | bytes 3538952 | tf_op jit(solution)/shard_map/ppermute | solution.py:294
  4.5 30.3 %collective-permute-start.7 = (bf16[64,1024]{1,0:T(8,128)(2,1)S(1)}, bf16[64,1024]{1,0:T(8,128)(2,1)S(1)}, u32[]{:S(2)}, u32[]{:S(2)}) collective-permute-start(bf16[64,1024]{1,0:T(8,128)(2,1)S(1)} %get-tuple-element.22.own), channel_id=1, source_target_pairs={{0,3},{1,0},{2,1},{3,2},{4,7},{5,4},{6,5},{7,6},{8,11},{9,8},{10,9... | collective-permute-start | bytes 393224 | tf_op jit(solution)/shard_map/ppermute | solution.py:294
  5.6 29.1 %collective-permute-start.6 = (bf16[64,1024]{1,0:T(8,128)(2,1)S(1)}, bf16[64,1024]{1,0:T(8,128)(2,1)S(1)}, u32[]{:S(2)}, u32[]{:S(2)}) collective-permute-start(bf16[64,1024]{1,0:T(8,128)(2,1)S(1)} %get-tuple-element.22.own), channel_id=1, source_target_pairs={{0,1},{1,2},{2,3},{3,0},{4,5},{5,6},{6,7},{7,4},{8,9},{9,10},{10,1... | collective-permute-start | bytes 393224 | tf_op jit(solution)/shard_map/ppermute | solution.py:294
  9.8 53.9 %collective-permute-start = (bf16[2048,256]{1,0:T(8,128)(2,1)}, bf16[2048,256]{1,0:T(8,128)(2,1)}, u32[]{:S(2)}, u32[]{:S(2)}) collective-permute-start(bf16[2048,256]{1,0:T(8,128)(2,1)} %get-tuple-element.15), channel_id=1, source_target_pairs={{0,1},{1,2},{2,3},{3,0},{4,5},{5,6},{6,7},{7,4},{8,9},{9,10},{10,1... | collective-permute-start | bytes 3145736 | tf_op jit(solution)/shard_map/ppermute | solution.py:294
  10.5 54.9 %collective-permute-start.2 = (bf16[2048,256]{1,0:T(8,128)(2,1)}, bf16[2048,256]{1,0:T(8,128)(2,1)}, u32[]{:S(2)}, u32[]{:S(2)}) collective-permute-start(bf16[2048,256]{1,0:T(8,128)(2,1)} %get-tuple-element.16), channel_id=1, source_target_pairs={{0,3},{1,0},{2,1},{3,2},{4,7},{5,4},{6,5},{7,6},{8,11},{9,8},{10,9... | collective-permute-start | bytes 3145736 | tf_op jit(solution)/shard_map/ppermute | solution.py:294
  13.1 24.1 %all-to-all-start = ((bf16[64,16,128]{2,1,0:T(8,128)(2,1)}), bf16[64,16,128]{2,1,0:T(8,128)(2,1)S(1)}, u32[]{:S(2)}, u32[]{:S(2)}) async-start(bf16[64,16,128]{2,1,0:T(8,128)(2,1)} %bitcast.16), calls=%async_computation | async-start | bytes 524288 | tf_op jit(solution)/shard_map/all_to_all | solution.py:365
  34.7 34.4 %copy-start = (bf16[2304,256]{1,0:T(8,128)(2,1)}, bf16[2304,256]{1,0:T(8,128)(2,1)S(1)}, u32[]{:S(2)}) copy-start(bf16[2304,256]{1,0:T(8,128)(2,1)S(1)} %collective-permute-done.1.two.refs_2_) | copy-start | bytes 3538948
  35.6 14.6 %collective-permute-start.9 = (bf16[256,1024]{1,0:T(8,128)(2,1)}, bf16[256,1024]{1,0:T(8,128)(2,1)S(1)}, u32[]{:S(2)}, u32[]{:S(2)}) collective-permute-start(bf16[256,1024]{1,0:T(8,128)(2,1)} %stack.1.refs_8_), channel_id=1, source_target_pairs={{0,64},{4,68},{8,72},{12,76},{16,80},{20,84},{24,88},{28,92},{32,9... | collective-permute-start | bytes 1572872 | tf_op jit(solution)/shard_map/ppermute | solution.py:393
  38.6 23.2 %all-to-all-start.1 = ((bf16[64,16,128]{2,1,0:T(8,128)(2,1)}), bf16[64,16,128]{2,1,0:T(8,128)(2,1)S(1)}, u32[]{:S(2)}, u32[]{:S(2)}) async-start(bf16[64,16,128]{2,1,0:T(8,128)(2,1)} %bitcast.15), calls=%async_computation.1 | async-start | bytes 524288 | tf_op jit(solution)/shard_map/all_to_all | solution.py:365
  50.1 19.1 %collective-permute-start.8 = (bf16[256,1024]{1,0:T(8,128)(2,1)}, bf16[256,1024]{1,0:T(8,128)(2,1)S(1)}, u32[]{:S(2)}, u32[]{:S(2)}) collective-permute-start(bf16[256,1024]{1,0:T(8,128)(2,1)} %stack.1.refs_8_), channel_id=1, source_target_pairs={{0,4},{4,0},{8,12},{12,8},{16,20},{20,16},{24,28},{28,24},{32,36},... | collective-permute-start | bytes 1572872 | tf_op jit(solution)/shard_map/ppermute | solution.py:393
  50.3 18.9 %collective-permute-start.10 = (bf16[256,1024]{1,0:T(8,128)(2,1)S(1)}, bf16[256,1024]{1,0:T(8,128)(2,1)S(1)}, u32[]{:S(2)}, u32[]{:S(2)}) collective-permute-start(bf16[256,1024]{1,0:T(8,128)(2,1)S(1)} %collective-permute-done.9.refs_10_), channel_id=1, source_target_pairs={{0,4},{4,0},{8,12},{12,8},{16,20},{20,16},{24,28},{28,24},{32,36},... | collective-permute-start | bytes 1572872 | tf_op jit(solution)/shard_map/ppermute | solution.py:393
  62.2 5.1 %collective-permute-start.3 = (bf16[16,768]{1,0:T(8,128)(2,1)S(1)}, bf16[16,768]{1,0:T(8,128)(2,1)S(1)}, u32[]{:S(2)}, u32[]{:S(2)}) collective-permute-start(bf16[16,768]{1,0:T(8,128)(2,1)S(1)} %get-tuple-element.19), channel_id=1, source_target_pairs={{0,1},{1,2},{2,3},{3,0},{4,5},{5,6},{6,7},{7,4},{8,9},{9,10},{10,1... | collective-permute-start | bytes 73736 | tf_op jit(solution)/shard_map/ppermute | solution.py:294
  63.7 5.3 %collective-permute-start.4 = (bf16[16,768]{1,0:T(8,128)(2,1)S(1)}, bf16[16,768]{1,0:T(8,128)(2,1)S(1)}, u32[]{:S(2)}, u32[]{:S(2)}) collective-permute-start(bf16[16,768]{1,0:T(8,128)(2,1)S(1)} %get-tuple-element.20), channel_id=1, source_target_pairs={{0,2},{1,3},{2,0},{3,1},{4,6},{5,7},{6,4},{7,5},{8,10},{9,11},{10,... | collective-permute-start | bytes 73736 | tf_op jit(solution)/shard_map/ppermute | solution.py:294
  65.3 3.8 %collective-permute-start.5 = (bf16[16,768]{1,0:T(8,128)(2,1)S(1)}, bf16[16,768]{1,0:T(8,128)(2,1)S(1)}, u32[]{:S(2)}, u32[]{:S(2)}) collective-permute-start(bf16[16,768]{1,0:T(8,128)(2,1)S(1)} %get-tuple-element.21), channel_id=1, source_target_pairs={{0,3},{1,0},{2,1},{3,2},{4,7},{5,4},{6,5},{7,6},{8,11},{9,8},{10,9... | collective-permute-start | bytes 73736 | tf_op jit(solution)/shard_map/ppermute | solution.py:294

commit v10 on v9

--- a/solution.py
+++ b/solution.py
@@ -52,15 +52,17 @@
         copy.wait()
 
 
-def slab_of(depth, slabs):
+def slabs_of(depth):
     index = lax.axis_index("shuf")
-    return lax.rem(index // (2 * depth), slabs // 2) * 2 + lax.rem(index, 2)
+    by_y, by_z = lax.rem(index // (2 * depth), 2), 2 + lax.rem(index // 2, 2)
+    first_core = lax.rem(index, 2) == 0
+    return jnp.where(first_core, by_y, by_z), jnp.where(first_core, by_z, by_y)
 
 
 def cut_kernel(values, weight, out, out_slab, sems, *, rows, blocks, depth):
     slab, cols = out_slab.shape[0], values.shape[1]
     first = pl.multiple_of(lax.rem(lax.axis_index("rep") + 2, blocks) * rows, rows)
-    mine = pl.multiple_of(slab_of(depth, weight.shape[0] // slab) * slab, slab)
+    mine = pl.multiple_of(slabs_of(depth)[0] * slab, slab)
     copies = [
         pltpu.make_async_copy(values.at[pl.ds(first, rows), :], out.at[pl.ds(blocks * slab, rows), :], sems.at[blocks]),
         pltpu.make_async_copy(weight.at[pl.ds(mine, slab), :], out_slab, sems.at[blocks + 1]),
@@ -234,11 +236,8 @@
         return pltpu.make_async_copy(source, held_rows.at[n, pl.ds(at, size), :], sems_in.at[n, p])
 
     slab = mine.shape[0] // blocks
-    slabs = cols // slab
-    own = slab_of(depth, slabs)
-    core = lax.rem(own, 2)
-    beyond = lax.rem(own + 2, slabs)
-    numbers = (own + 1 - 2 * core, beyond, beyond + 1 - 2 * core)
+    own, beside = slabs_of(depth)
+    numbers = (beside, own + 1 - 2 * lax.rem(own, 2), beside + 1 - 2 * lax.rem(beside, 2))
 
     def rows_of(n, number):
         return weight.at[pl.ds(pl.multiple_of(n * cols + number * slab, slab), slab), :]
@@ -401,7 +400,8 @@
         compiler_params=limit(8),
         name="stack",
     )(slabs[0], slabs[1], moved[2], slabs[3])
-    across = trade(mine, 2 * depth)
+    pairs = [(i, i ^ (2 if i % 2 else 2 * depth)) for i in range(peers)]
+    across = lax.ppermute(mine, "shuf", pairs)
     sibling = trade(mine, 1)
     across_sibling = trade(across, 1)
     each = tiles // blocks
@@ -420,6 +420,8 @@
 
     middle = own_rows // 4
     sizes = (middle // 2, middle, middle, middle, middle // 2)
+    if middle // 2 % tile_rows:
+        sizes = (middle,) * 4
     return pl.pallas_call(
         lambda *refs: project_kernel(
             *refs,

time: 77.6 us -> 77.7 us (level)
    ppermute x3 -> x2, starting transfers between devices: 2.17 us -> 0.6 us  [trade(): lax.ppermute(value, 'shuf', [(i, i ^ distance) for i in range(peers)])]
    ppermute x0 -> x1, starting transfers between devices: none -> 1.58 us  [on_device(): across = lax.ppermute(mine, 'shuf', pairs)]
where the time goes in v10:
time: 77.7 us; the launch traced here: 76.8 us
  starting transfers between devices  38.6 us (50%)
  waiting for transfers between devices  23.2 us (30%)
  Pallas kernels  14.7 us (19%)
    all_to_all x2, starting transfers between devices, exchange(): lax.all_to_all(message.reshape(peers, MSG, LANES), 'shuf', 0, 0, tiled=True)  23.2 us
    ppermute x8, starting transfers between devices, hop(): lax.ppermute(value, axis, [(i, (i + distance) % size) for i in range(size)])  13.2 us
    ppermute x8, waiting for transfers between devices, hop(): lax.ppermute(value, axis, [(i, (i + distance) % size) for i in range(size)])  12.1 us
    all_to_all x2, waiting for transfers between devices, exchange(): lax.all_to_all(message.reshape(peers, MSG, LANES), 'shuf', 0, 0, tiled=True)  11.1 us
    pallas_call x1, Pallas kernels, on_device(): pl.pallas_call(lambda *refs: project_kernel(*refs, blocks=blocks, tile_ro...  7.42 us
    pallas_call x1, Pallas kernels, on_device(): pl.pallas_call(lambda *refs: stats_kernel(*refs, tiles=tiles, peers=peers...  3.31 us
    ppermute x1, starting transfers between devices, on_device(): across = lax.ppermute(mine, 'shuf', pairs)  1.58 us
  transfers between devices with their start and end apart: 13, of which 5 were waited for; matrix products, arithmetic and copies ran while one was open for 0% of the time, Pallas kernels for 8%

profile of v10, /device:TPU:32, one launch (start us, length us, event | category | flops | bytes accessed | tf_op | source)
XLA Modules:
  0.0 76.8 jit_solution(13318966146981532934)
XLA Ops:
  0.0 1.3 %cut.1 = (bf16[2304,256]{1,0:T(8,128)(2,1)S(1)}, bf16[64,1024]{1,0:T(8,128)(2,1)S(1)}) custom-call(bf16[8192,256]{1,0:T(8,128)(2,1)} %refs_0_.5, bf16[256,1024]{1,0:T(8,128)(2,1)} %refs_1_.1), custom_call_target="tpu_custom_call" | custom-call | tf_op jit(solution)/shard_map/cut/pallas_call | solution.py:332
  1.3 0.0 copy-start.2
  1.3 0.0 copy-start.3
  1.3 3.1 %collective-permute-start.1 = (bf16[2304,256]{1,0:T(8,128)(2,1)S(1)}, bf16[2304,256]{1,0:T(8,128)(2,1)S(1)}, u32[]{:S(2)}, u32[]{:S(2)}) collective-permute-start(bf16[2304,256]{1,0:T(8,128)(2,1)S(1)} %get-tuple-element.14.refs_1_), channel_id=1, source_target_pairs={{0,2},{1,3},{2,0},{3,1},{4,6},{5,7},{6,4},{7,5},{8,10},{9,11},{10,... | collective-permute-start | bytes 3538952 | tf_op jit(solution)/shard_map/ppermute | solution.py:293
  4.5 1.1 %collective-permute-start.7 = (bf16[64,1024]{1,0:T(8,128)(2,1)S(1)}, bf16[64,1024]{1,0:T(8,128)(2,1)S(1)}, u32[]{:S(2)}, u32[]{:S(2)}) collective-permute-start(bf16[64,1024]{1,0:T(8,128)(2,1)S(1)} %get-tuple-element.22.own), channel_id=1, source_target_pairs={{0,3},{1,0},{2,1},{3,2},{4,7},{5,4},{6,5},{7,6},{8,11},{9,8},{10,9... | collective-permute-start | bytes 393224 | tf_op jit(solution)/shard_map/ppermute | solution.py:293
  5.6 0.9 %collective-permute-start.6 = (bf16[64,1024]{1,0:T(8,128)(2,1)S(1)}, bf16[64,1024]{1,0:T(8,128)(2,1)S(1)}, u32[]{:S(2)}, u32[]{:S(2)}) collective-permute-start(bf16[64,1024]{1,0:T(8,128)(2,1)S(1)} %get-tuple-element.22.own), channel_id=1, source_target_pairs={{0,1},{1,2},{2,3},{3,0},{4,5},{5,6},{6,7},{7,4},{8,9},{9,10},{10,1... | collective-permute-start | bytes 393224 | tf_op jit(solution)/shard_map/ppermute | solution.py:293
  6.5 3.3 %stats.1 = (bf16[1024,128]{1,0:T(8,128)(2,1)}, bf16[2048,256]{1,0:T(8,128)(2,1)}, bf16[2048,256]{1,0:T(8,128)(2,1)}) custom-call(bf16[8192,256]{1,0:T(8,128)(2,1)} %refs_0_.5, bf16[2304,256]{1,0:T(8,128)(2,1)S(1)} %get-tuple-element.14.refs_1_, s32[1,64]{1,0:T(1,128)S(1)} %bitcast.10, s32[1,64]{1,0:T(1,128)S(1)} %bitcast.14), custom_call_target="tpu_custom_call" | custom-call | tf_op jit(solution)/shard_map/stats/pallas_call | solution.py:343
  9.8 0.7 collective-permute-start
  10.5 2.6 %collective-permute-start.2 = (bf16[2048,256]{1,0:T(8,128)(2,1)}, bf16[2048,256]{1,0:T(8,128)(2,1)}, u32[]{:S(2)}, u32[]{:S(2)}) collective-permute-start(bf16[2048,256]{1,0:T(8,128)(2,1)} %get-tuple-element.16), channel_id=1, source_target_pairs={{0,3},{1,0},{2,1},{3,2},{4,7},{5,4},{6,5},{7,6},{8,11},{9,8},{10,9... | collective-permute-start | bytes 3145736 | tf_op jit(solution)/shard_map/ppermute | solution.py:293
  13.1 11.8 %all-to-all-start = ((bf16[64,16,128]{2,1,0:T(8,128)(2,1)}), bf16[64,16,128]{2,1,0:T(8,128)(2,1)S(1)}, u32[]{:S(2)}, u32[]{:S(2)}) async-start(bf16[64,16,128]{2,1,0:T(8,128)(2,1)} %bitcast.16), calls=%async_computation | async-start | bytes 524288 | tf_op jit(solution)/shard_map/all_to_all | solution.py:364
  24.9 9.8 %collective-permute-done.7.three = bf16[64,1024]{1,0:T(8,128)(2,1)S(1)} collective-permute-done((bf16[64,1024]{1,0:T(8,128)(2,1)S(1)}, bf16[64,1024]{1,0:T(8,128)(2,1)S(1)}, u32[]{:S(2)}, u32[]{:S(2)}) %collective-permute-start.7) | collective-permute-done | bytes 131104 | tf_op jit(solution)/shard_map/ppermute | solution.py:293
  34.7 0.0 collective-permute-done.6.one
  34.7 0.0 collective-permute-done.1.two.refs_2_
  34.7 0.9 %stack.1.refs_8_ = bf16[256,1024]{1,0:T(8,128)(2,1)} custom-call(bf16[64,1024]{1,0:T(8,128)(2,1)S(1)} %get-tuple-element.22.own, bf16[64,1024]{1,0:T(8,128)(2,1)S(1)} %collective-permute-done.6.one, bf16[2304,256]{1,0:T(8,128)(2,1)S(1)} %collective-permute-done.1.two.refs_2_, bf16[64,1024]{1,0:T(8,128)(2,1)S(1)} %collective-permute-done.7.three), custom_call_target="tpu_custom_call" | custom-call | tf_op jit(solution)/shard_map/stack/pallas_call | solution.py:394
  35.6 1.6 %collective-permute-start.9 = (bf16[256,1024]{1,0:T(8,128)(2,1)}, bf16[256,1024]{1,0:T(8,128)(2,1)S(1)}, u32[]{:S(2)}, u32[]{:S(2)}) collective-permute-start(bf16[256,1024]{1,0:T(8,128)(2,1)} %stack.1.refs_8_), channel_id=1, source_target_pairs={{0,64},{4,12},{8,72},{12,4},{16,80},{20,28},{24,88},{28,20},{32,96... | collective-permute-start | bytes 1572872 | tf_op jit(solution)/shard_map/ppermute | solution.py:404
  37.2 0.0 all-to-all-done
  37.2 1.4 %moments.1 = bf16[1024,128]{1,0:T(8,128)(2,1)} custom-call(bf16[1024,128]{1,0:T(8,128)(2,1)S(1)} %bitcast.8, f32[2,256]{1,0:T(2,128)S(1)} %pair.1.refs_1_), custom_call_target="tpu_custom_call" | custom-call | tf_op jit(solution)/shard_map/moments/pallas_call | solution.py:381
  38.6 11.5 %all-to-all-start.1 = ((bf16[64,16,128]{2,1,0:T(8,128)(2,1)}), bf16[64,16,128]{2,1,0:T(8,128)(2,1)S(1)}, u32[]{:S(2)}, u32[]{:S(2)}) async-start(bf16[64,16,128]{2,1,0:T(8,128)(2,1)} %bitcast.15), calls=%async_computation.1 | async-start | bytes 524288 | tf_op jit(solution)/shard_map/all_to_all | solution.py:364
  50.1 0.2 collective-permute-start.8
  50.3 0.0 collective-permute-done.9.refs_10_
  50.3 0.4 collective-permute-start.10
  50.7 11.1 %all-to-all-done.1 = bf16[64,16,128]{2,1,0:T(8,128)(2,1)S(1)} async-done(((bf16[64,16,128]{2,1,0:T(8,128)(2,1)}), bf16[64,16,128]{2,1,0:T(8,128)(2,1)S(1)}, u32[]{:S(2)}, u32[]{:S(2)}) %all-to-all-start.1) | async-done | bytes 262176 | tf_op jit(solution)/shard_map/all_to_all | solution.py:364
  61.8 0.4 pick.1
  62.2 1.5 %collective-permute-start.3 = (bf16[16,768]{1,0:T(8,128)(2,1)S(1)}, bf16[16,768]{1,0:T(8,128)(2,1)S(1)}, u32[]{:S(2)}, u32[]{:S(2)}) collective-permute-start(bf16[16,768]{1,0:T(8,128)(2,1)S(1)} %get-tuple-element.19), channel_id=1, source_target_pairs={{0,1},{1,2},{2,3},{3,0},{4,5},{5,6},{6,7},{7,4},{8,9},{9,10},{10,1... | collective-permute-start | bytes 73736 | tf_op jit(solution)/shard_map/ppermute | solution.py:293
  63.7 1.6 %collective-permute-start.4 = (bf16[16,768]{1,0:T(8,128)(2,1)S(1)}, bf16[16,768]{1,0:T(8,128)(2,1)S(1)}, u32[]{:S(2)}, u32[]{:S(2)}) collective-permute-start(bf16[16,768]{1,0:T(8,128)(2,1)S(1)} %get-tuple-element.20), channel_id=1, source_target_pairs={{0,2},{1,3},{2,0},{3,1},{4,6},{5,7},{6,4},{7,5},{8,10},{9,11},{10,... | collective-permute-start | bytes 73736 | tf_op jit(solution)/shard_map/ppermute | solution.py:293
  65.3 1.6 %collective-permute-start.5 = (bf16[16,768]{1,0:T(8,128)(2,1)S(1)}, bf16[16,768]{1,0:T(8,128)(2,1)S(1)}, u32[]{:S(2)}, u32[]{:S(2)}) collective-permute-start(bf16[16,768]{1,0:T(8,128)(2,1)S(1)} %get-tuple-element.21), channel_id=1, source_target_pairs={{0,3},{1,0},{2,1},{3,2},{4,7},{5,4},{6,5},{7,6},{8,11},{9,8},{10,9... | collective-permute-start | bytes 73736 | tf_op jit(solution)/shard_map/ppermute | solution.py:293
  66.9 0.4 collective-permute-done.3.refs_5_
  67.3 1.7 %collective-permute-done.4.refs_6_ = bf16[16,768]{1,0:T(8,128)(2,1)S(1)} collective-permute-done((bf16[16,768]{1,0:T(8,128)(2,1)S(1)}, bf16[16,768]{1,0:T(8,128)(2,1)S(1)}, u32[]{:S(2)}, u32[]{:S(2)}) %collective-permute-start.4) | collective-permute-done | bytes 24608 | tf_op jit(solution)/shard_map/ppermute | solution.py:293
  69.0 0.1 collective-permute-done.5.refs_7_
  69.2 0.0 collective-permute-done.8.refs_9_
  69.2 0.0 collective-permute-done.10.refs_11_
  69.2 7.4 %project.1 = bf16[2048,1024]{1,0:T(8,128)(2,1)} custom-call(bf16[8192,256]{1,0:T(8,128)(2,1)} %refs_0_.5, bf16[2048,256]{1,0:T(8,128)(2,1)} %collective-permute-done.refs_1_, bf16[2304,256]{1,0:T(8,128)(2,1)} %copy-done, bf16[2048,256]{1,0:T(8,128)(2,1)} %collective-permute-done.2.refs_3_, bf16[16,768]{1,0:T(8,128)(2,1)S(1)} %get-tuple-element.18.refs_4_, ...), custom_call_target="tpu_custom_call" | custom-call | tf_op jit(solution)/shard_map/project/pallas_call | solution.py:425
  (11 shorter events, 0.0 us)
Async XLA Ops:
  0.0 6.5 %copy-start.1 = (s32[64,1]{0,1:T(1,128)S(1)}, s32[64,1]{0,1:T(1,128)}, u32[]{:S(2)}) copy-start(s32[64,1]{0,1:T(1,128)} %param.8) | copy-start | bytes 772
  0.0 6.5 %copy-start.4 = (s32[64]{0:T(128)S(1)}, s32[64]{0:T(128)}, u32[]{:S(2)}) copy-start(s32[64]{0:T(128)} %param.7) | copy-start | bytes 772
  1.3 35.9 %copy-start.2 = (f32[256]{0:T(256)S(1)}, f32[256]{0:T(256)}, u32[]{:S(2)}) copy-start(f32[256]{0:T(256)} %param.9) | copy-start | bytes 3076
  1.3 35.9 %copy-start.3 = (f32[256]{0:T(256)S(1)}, f32[256]{0:T(256)}, u32[]{:S(2)}) copy-start(f32[256]{0:T(256)} %param.10) | copy-start | bytes 3076
  1.3 33.4 %collective-permute-start.1 = (bf16[2304,256]{1,0:T(8,128)(2,1)S(1)}, bf16[2304,256]{1,0:T(8,128)(2,1)S(1)}, u32[]{:S(2)}, u32[]{:S(2)}) collective-permute-start(bf16[2304,256]{1,0:T(8,128)(2,1)S(1)} %get-tuple-element.14.refs_1_), channel_id=1, source_target_pairs={{0,2},{1,3},{2,0},{3,1},{4,6},{5,7},{6,4},{7,5},{8,10},{9,11},{10,... | collective-permute-start | bytes 3538952 | tf_op jit(solution)/shard_map/ppermute | solution.py:293
  4.5 30.3 %collective-permute-start.7 = (bf16[64,1024]{1,0:T(8,128)(2,1)S(1)}, bf16[64,1024]{1,0:T(8,128)(2,1)S(1)}, u32[]{:S(2)}, u32[]{:S(2)}) collective-permute-start(bf16[64,1024]{1,0:T(8,128)(2,1)S(1)} %get-tuple-element.22.own), channel_id=1, source_target_pairs={{0,3},{1,0},{2,1},{3,2},{4,7},{5,4},{6,5},{7,6},{8,11},{9,8},{10,9... | collective-permute-start | bytes 393224 | tf_op jit(solution)/shard_map/ppermute | solution.py:293
  5.6 29.1 %collective-permute-start.6 = (bf16[64,1024]{1,0:T(8,128)(2,1)S(1)}, bf16[64,1024]{1,0:T(8,128)(2,1)S(1)}, u32[]{:S(2)}, u32[]{:S(2)}) collective-permute-start(bf16[64,1024]{1,0:T(8,128)(2,1)S(1)} %get-tuple-element.22.own), channel_id=1, source_target_pairs={{0,1},{1,2},{2,3},{3,0},{4,5},{5,6},{6,7},{7,4},{8,9},{9,10},{10,1... | collective-permute-start | bytes 393224 | tf_op jit(solution)/shard_map/ppermute | solution.py:293
  9.8 53.9 %collective-permute-start = (bf16[2048,256]{1,0:T(8,128)(2,1)}, bf16[2048,256]{1,0:T(8,128)(2,1)}, u32[]{:S(2)}, u32[]{:S(2)}) collective-permute-start(bf16[2048,256]{1,0:T(8,128)(2,1)} %get-tuple-element.15), channel_id=1, source_target_pairs={{0,1},{1,2},{2,3},{3,0},{4,5},{5,6},{6,7},{7,4},{8,9},{9,10},{10,1... | collective-permute-start | bytes 3145736 | tf_op jit(solution)/shard_map/ppermute | solution.py:293
  10.5 54.9 %collective-permute-start.2 = (bf16[2048,256]{1,0:T(8,128)(2,1)}, bf16[2048,256]{1,0:T(8,128)(2,1)}, u32[]{:S(2)}, u32[]{:S(2)}) collective-permute-start(bf16[2048,256]{1,0:T(8,128)(2,1)} %get-tuple-element.16), channel_id=1, source_target_pairs={{0,3},{1,0},{2,1},{3,2},{4,7},{5,4},{6,5},{7,6},{8,11},{9,8},{10,9... | collective-permute-start | bytes 3145736 | tf_op jit(solution)/shard_map/ppermute | solution.py:293
  13.1 24.1 %all-to-all-start = ((bf16[64,16,128]{2,1,0:T(8,128)(2,1)}), bf16[64,16,128]{2,1,0:T(8,128)(2,1)S(1)}, u32[]{:S(2)}, u32[]{:S(2)}) async-start(bf16[64,16,128]{2,1,0:T(8,128)(2,1)} %bitcast.16), calls=%async_computation | async-start | bytes 524288 | tf_op jit(solution)/shard_map/all_to_all | solution.py:364
  34.7 34.4 %copy-start = (bf16[2304,256]{1,0:T(8,128)(2,1)}, bf16[2304,256]{1,0:T(8,128)(2,1)S(1)}, u32[]{:S(2)}) copy-start(bf16[2304,256]{1,0:T(8,128)(2,1)S(1)} %collective-permute-done.1.two.refs_2_) | copy-start | bytes 3538948
  35.6 14.6 %collective-permute-start.9 = (bf16[256,1024]{1,0:T(8,128)(2,1)}, bf16[256,1024]{1,0:T(8,128)(2,1)S(1)}, u32[]{:S(2)}, u32[]{:S(2)}) collective-permute-start(bf16[256,1024]{1,0:T(8,128)(2,1)} %stack.1.refs_8_), channel_id=1, source_target_pairs={{0,64},{4,12},{8,72},{12,4},{16,80},{20,28},{24,88},{28,20},{32,96... | collective-permute-start | bytes 1572872 | tf_op jit(solution)/shard_map/ppermute | solution.py:404
  38.6 23.2 %all-to-all-start.1 = ((bf16[64,16,128]{2,1,0:T(8,128)(2,1)}), bf16[64,16,128]{2,1,0:T(8,128)(2,1)S(1)}, u32[]{:S(2)}, u32[]{:S(2)}) async-start(bf16[64,16,128]{2,1,0:T(8,128)(2,1)} %bitcast.15), calls=%async_computation.1 | async-start | bytes 524288 | tf_op jit(solution)/shard_map/all_to_all | solution.py:364
  50.1 19.1 %collective-permute-start.8 = (bf16[256,1024]{1,0:T(8,128)(2,1)}, bf16[256,1024]{1,0:T(8,128)(2,1)S(1)}, u32[]{:S(2)}, u32[]{:S(2)}) collective-permute-start(bf16[256,1024]{1,0:T(8,128)(2,1)} %stack.1.refs_8_), channel_id=1, source_target_pairs={{0,4},{4,0},{8,12},{12,8},{16,20},{20,16},{24,28},{28,24},{32,36},... | collective-permute-start | bytes 1572872 | tf_op jit(solution)/shard_map/ppermute | solution.py:392
  50.3 18.9 %collective-permute-start.10 = (bf16[256,1024]{1,0:T(8,128)(2,1)S(1)}, bf16[256,1024]{1,0:T(8,128)(2,1)S(1)}, u32[]{:S(2)}, u32[]{:S(2)}) collective-permute-start(bf16[256,1024]{1,0:T(8,128)(2,1)S(1)} %collective-permute-done.9.refs_10_), channel_id=1, source_target_pairs={{0,4},{4,0},{8,12},{12,8},{16,20},{20,16},{24,28},{28,24},{32,36},... | collective-permute-start | bytes 1572872 | tf_op jit(solution)/shard_map/ppermute | solution.py:392
  62.2 5.1 %collective-permute-start.3 = (bf16[16,768]{1,0:T(8,128)(2,1)S(1)}, bf16[16,768]{1,0:T(8,128)(2,1)S(1)}, u32[]{:S(2)}, u32[]{:S(2)}) collective-permute-start(bf16[16,768]{1,0:T(8,128)(2,1)S(1)} %get-tuple-element.19), channel_id=1, source_target_pairs={{0,1},{1,2},{2,3},{3,0},{4,5},{5,6},{6,7},{7,4},{8,9},{9,10},{10,1... | collective-permute-start | bytes 73736 | tf_op jit(solution)/shard_map/ppermute | solution.py:293
  63.7 5.3 %collective-permute-start.4 = (bf16[16,768]{1,0:T(8,128)(2,1)S(1)}, bf16[16,768]{1,0:T(8,128)(2,1)S(1)}, u32[]{:S(2)}, u32[]{:S(2)}) collective-permute-start(bf16[16,768]{1,0:T(8,128)(2,1)S(1)} %get-tuple-element.20), channel_id=1, source_target_pairs={{0,2},{1,3},{2,0},{3,1},{4,6},{5,7},{6,4},{7,5},{8,10},{9,11},{10,... | collective-permute-start | bytes 73736 | tf_op jit(solution)/shard_map/ppermute | solution.py:293
  65.3 3.8 %collective-permute-start.5 = (bf16[16,768]{1,0:T(8,128)(2,1)S(1)}, bf16[16,768]{1,0:T(8,128)(2,1)S(1)}, u32[]{:S(2)}, u32[]{:S(2)}) collective-permute-start(bf16[16,768]{1,0:T(8,128)(2,1)S(1)} %get-tuple-element.21), channel_id=1, source_target_pairs={{0,3},{1,0},{2,1},{3,2},{4,7},{5,4},{6,5},{7,6},{8,11},{9,8},{10,9... | collective-permute-start | bytes 73736 | tf_op jit(solution)/shard_map/ppermute | solution.py:293
